TPU v7x, 128 devices: a whole 4x4x4 slice. The times are simulated.
128 devices in a mesh: shard: 8 (over y, x_lo), cols: 16 (over z, x_hi, core).
Axes of the slice: x: 4 (x_hi: 2, x_lo: 2; x = x_hi * 2 + x_lo), y: 4, z: 4, core: 2. Of those that a mesh axis runs over, the one named last changes fastest.
Arguments:
- train_gate: bfloat16 [4096, 14336], P('shard', 'cols'), may hold values from -0.09375 to 0.09375
- low_gate: bfloat16 [4096, 32], P('shard'), may hold values from -0.09375 to 0.09375
- high_gate: bfloat16 [32, 14336], P(None, 'cols'), may hold values from -1 to 1
- train_up: bfloat16 [4096, 14336], P('shard', 'cols'), may hold values from -0.09375 to 0.09375
- low_up: bfloat16 [4096, 32], P('shard'), may hold values from -0.09375 to 0.09375
- high_up: bfloat16 [32, 14336], P(None, 'cols'), may hold values from -1 to 1
- norm_train: float32 [4096], P(('shard', 'cols')), may hold values from 0.25 to 1.75
- norm_step: float32 [4096], P(('shard', 'cols')), may hold values from -0.3 to 0.3
Outputs:
- ready_gate: bfloat16 [14336, 4096], P('cols')
- ready_up: bfloat16 [14336, 4096], P('cols')
- serve_norm: bfloat16 [4096], replicated
All inputs are finite; a program needn't handle non-finite values.
Results may differ from a plain program's by a relative error of at most 0.001.
Values may be sent and summed in bfloat16 or wider, within the bound.
No kernel may reach another device: no remote copies, remote signals or barrier semaphores. Data moves between devices by JAX's collectives and lax.ppermute only.
A program may use at most 128 MiB of HBM per device.

v0:
```python
import jax
import jax.numpy as jnp
from jax import lax
from jax.experimental import pallas as pl
from jax.experimental.pallas import tpu as pltpu
from jax.sharding import Mesh
from jax.sharding import PartitionSpec as P


mix_rate = 1.0
LANES = 128
UP = [(i, (i + 1) % 4) for i in range(4)]
DOWN = [(i, (i - 1) % 4) for i in range(4)]
SWAP = [(0, 1), (1, 0)]


def merged(train, low, high):
    wide = train.astype(jnp.float32) + mix_rate * jnp.dot(
        low, high, preferred_element_type=jnp.float32
    )
    return wide.astype(jnp.bfloat16)


def place(outs, parts):
    fresh = not isinstance(outs[0], jax.Array)
    count = len(parts)
    steps = [p.shape[1] // LANES for p, *_ in parts]

    def kernel(*refs):
        y, xl = lax.axis_index("y"), lax.axis_index("xl")
        piece_refs, refs = refs[:count], refs[count:]
        refs = refs[0 if fresh else 2 :]
        out_refs, refs = refs[:2], refs[2:]
        taken, turned = refs[:count], refs[count : 2 * count]
        in_sem, out_sem = refs[2 * count :]

        def load(k, c):
            columns = pl.ds(pl.multiple_of(c * LANES, LANES), LANES)
            return pltpu.make_async_copy(
                piece_refs[k].at[:, columns], taken[k].at[c], in_sem.at[k, c]
            )

        def save(k, c):
            rows = pl.ds(pl.multiple_of(parts[k][2] + c * LANES, LANES), LANES)
            size = parts[k][0].shape[0]
            source = lax.rem(y + parts[k][3], 4) * 2 + lax.rem(xl + parts[k][4], 2)
            columns = pl.ds(pl.multiple_of(source * size, LANES), size)
            return pltpu.make_async_copy(
                turned[k].at[c], out_refs[parts[k][1]].at[rows, columns], out_sem.at[k, c]
            )

        for k in range(count):
            for c in range(steps[k]):
                load(k, c).start()
        for k in range(count):

            @pl.loop(0, steps[k])
            def _(c):
                load(k, c).wait()
                turned[k][c] = taken[k][c].T
                save(k, c).start()

        for k in range(count):
            for c in range(steps[k]):
                save(k, c).wait()

    shapes = [jax.ShapeDtypeStruct(o.shape, o.dtype) for o in outs]
    any_spec = pl.BlockSpec(memory_space=pl.ANY)
    operands = [*[p for p, *_ in parts], *([] if fresh else outs)]
    moved = sum(p.size * 2 * 2 for p, *_ in parts)
    return pl.pallas_call(
        kernel,
        out_shape=shapes,
        in_specs=[any_spec] * len(operands),
        out_specs=[any_spec] * 2,
        scratch_shapes=[
            *[pltpu.VMEM((p.shape[1] // LANES, p.shape[0], LANES), p.dtype) for p, *_ in parts],
            *[pltpu.VMEM((p.shape[1] // LANES, LANES, p.shape[0]), p.dtype) for p, *_ in parts],
            pltpu.SemaphoreType.DMA((count, max(steps))),
            pltpu.SemaphoreType.DMA((count, max(steps))),
        ],
        input_output_aliases={} if fresh else {count: 0, count + 1: 1},
        compiler_params=pltpu.CompilerParams(vmem_limit_bytes=32 * 2**20),
        cost_estimate=pl.CostEstimate(flops=0, bytes_accessed=moved, transcendentals=0),
    )(*operands)


def doubled(x, axis, pairs, high):
    other = lax.ppermute(x, axis, pairs)
    return jnp.where(high, jnp.concatenate([other, x]), jnp.concatenate([x, other]))


def gathered_gain(gain):
    length = gain.shape[0]
    y, xl, cols = (lax.axis_index(axis) for axis in ("y", "xl", "cols"))
    index = jnp.arange(4)[:, None]
    x = jnp.broadcast_to(gain[None], (4, length))
    for shift in (1, 2, 3):
        part = lax.ppermute(gain, "y", [(i, (i + shift) % 4) for i in range(4)])
        x = jnp.where(index == (y - shift) % 4, part[None], x)
    x = doubled(x, "xl", SWAP, xl == 1)
    for bit in (1, 4, 8):
        pairs = [(i, i ^ bit) for i in range(16)]
        x = doubled(x, "cols", pairs, (cols & bit) != 0)
    pairs = [(i, i ^ 18) for i in range(32)]
    x = doubled(x, ("xl", "cols"), pairs, (cols & 2) != 0)
    x = x.reshape(2, 2, 2, 2, 2, 4, length)
    return x.transpose(5, 4, 1, 2, 0, 3, 6).reshape(-1)


def per_device(train_gate, low_gate, high_gate, train_up, low_up, high_up, norm_train, norm_step):
    rows, width = train_gate.shape
    cut = width * 5 // 7 // LANES * LANES

    def up(v):
        return lax.ppermute(v, "y", UP)

    def down(v):
        return lax.ppermute(v, "y", DOWN)

    def across(v):
        return lax.ppermute(v, "xl", SWAP)

    g = merged(train_gate, low_gate, high_gate)
    u = merged(train_up, low_up, high_up)
    gain = (norm_train + norm_step).astype(jnp.bfloat16)

    g_m, g_x, u_p = up(g), across(g), down(u)
    u_m, u_x, g_p = up(u), across(u), down(g)
    g_f, cg_p, cu_p = up(g_m), down(g_x), across(u_p)
    cu_m0, cu_m1 = across(u_m[:, :cut]), across(u_m[:, cut:])
    cg_m, u_f = up(g_x), down(u_p)
    cg_f0 = across(g_f[:, :cut])
    cg_f1, cu_f1 = down(cg_p[:, cut:]), down(cu_p[:, cut:])
    cu_f0 = up(cu_m0)

    out = jax.ShapeDtypeStruct((width, rows * 8), jnp.bfloat16)
    outs = place((out, out), [(g, 0, 0, 0, 0), (u, 1, 0, 0, 0)])
    outs = place(outs, [(g_m, 0, 0, 3, 0), (g_x, 0, 0, 0, 1), (u_p, 1, 0, 1, 0)])
    outs = place(outs, [(u_m, 1, 0, 3, 0), (u_x, 1, 0, 0, 1), (g_p, 0, 0, 1, 0)])
    outs = place(outs, [(g_f, 0, 0, 2, 0), (cg_p, 0, 0, 1, 1), (cu_p, 1, 0, 1, 1)])
    outs = place(
        outs, [(cu_m0, 1, 0, 3, 1), (cu_m1, 1, cut, 3, 1), (cg_m, 0, 0, 3, 1), (u_f, 1, 0, 2, 0)]
    )
    outs = place(
        outs,
        [(cg_f0, 0, 0, 2, 1), (cg_f1, 0, cut, 2, 1), (cu_f0, 1, 0, 2, 1), (cu_f1, 1, cut, 2, 1)],
    )
    return (*outs, gathered_gain(gain))


def solution(mesh):
    finer = Mesh(mesh.devices.reshape(4, 2, mesh.shape["cols"]), ("y", "xl", "cols"))
    shard, every = ("y", "xl"), ("y", "xl", "cols")
    return jax.shard_map(
        per_device,
        mesh=finer,
        in_specs=(
            P(shard, "cols"),
            P(shard, None),
            P(None, "cols"),
            P(shard, "cols"),
            P(shard, None),
            P(None, "cols"),
            P(every),
            P(every),
        ),
        out_specs=(P("cols", None), P("cols", None), P()),
        check_vma=False,
    )
```

profile of v0, /device:TPU:0, one launch (start us, length us, event | category | flops | bytes accessed | tf_op | source)
XLA Modules:
  0.0 148.9 jit_solution(9279915717344567979)
XLA Ops:
  3.1 1.7 %collective-permute-start.3 = (bf16[512,896]{1,0:T(8,128)(2,1)S(1)}, bf16[512,896]{1,0:T(8,128)(2,1)}, u32[]{:S(2)}, u32[]{:S(2)}) collective-permute-start(bf16[512,896]{1,0:T(8,128)(2,1)S(1)} %add_convert_fusion.1.refs_0_), channel_id=1, source_target_pairs={{0,16},{16,0},{1,17},{17,1},{2,18},{18,2},{3,19},{19,3},{4,20},{20... | collective-permute-start | bytes 2752520 | tf_op jit(solution)/shard_map/ppermute | solution.py:122
  7.0 1.7 %collective-permute-start.17 = (bf16[32]{0:T(256)(128)(2,1)S(1)}, bf16[32]{0:T(256)(128)(2,1)S(1)}, u32[]{:S(2)}, u32[]{:S(2)}) collective-permute-start(bf16[32]{0:T(256)(128)(2,1)S(1)} %add_convert_fusion.2), channel_id=1, source_target_pairs={{0,96},{32,0},{64,32},{96,64},{1,97},{33,1},{65,33},{97,65},{2,98}... | collective-permute-start | bytes 200 | tf_op jit(solution)/shard_map/ppermute | solution.py:99
  8.7 2.0 %collective-permute-start.18 = (bf16[32]{0:T(256)(128)(2,1)S(1)}, bf16[32]{0:T(256)(128)(2,1)S(1)}, u32[]{:S(2)}, u32[]{:S(2)}) collective-permute-start(bf16[32]{0:T(256)(128)(2,1)S(1)} %add_convert_fusion.2), channel_id=1, source_target_pairs={{0,64},{32,96},{64,0},{96,32},{1,65},{33,97},{65,1},{97,33},{2,66}... | collective-permute-start | bytes 200 | tf_op jit(solution)/shard_map/ppermute | solution.py:99
  11.4 17.7 %collective-permute-done.18 = bf16[32]{0:T(256)(128)(2,1)S(1)} collective-permute-done((bf16[32]{0:T(256)(128)(2,1)S(1)}, bf16[32]{0:T(256)(128)(2,1)S(1)}, u32[]{:S(2)}, u32[]{:S(2)}) %collective-permute-start.18) | collective-permute-done | bytes 96 | tf_op jit(solution)/shard_map/ppermute | solution.py:99
  29.7 3.0 %collective-permute-done.20 = bf16[4,32]{1,0:T(4,128)(2,1)S(1)} collective-permute-done((bf16[4,32]{1,0:T(4,128)(2,1)S(1)}, bf16[4,32]{1,0:T(4,128)(2,1)S(1)}, u32[]{:S(2)}, u32[]{:S(2)}) %collective-permute-start.20) | collective-permute-done | bytes 288 | tf_op jit(solution)/shard_map/ppermute | solution.py:89
  35.2 2.0 %collective-permute-start.22 = (bf16[16,32]{1,0:T(8,128)(2,1)S(1)}, bf16[16,32]{1,0:T(8,128)(2,1)S(1)}, u32[]{:S(2)}, u32[]{:S(2)}) collective-permute-start(bf16[16,32]{1,0:T(8,128)(2,1)S(1)} %maximum_select_fusion.3), channel_id=1, source_target_pairs={{0,4},{1,5},{2,6},{3,7},{4,0},{5,1},{6,2},{7,3},{8,12},{9,13},{10,... | collective-permute-start | bytes 3080 | tf_op jit(solution)/shard_map/ppermute | solution.py:89
  38.9 3.9 %collective-permute-start.23 = (bf16[32,32]{1,0:T(8,128)(2,1)S(1)}, bf16[32,32]{1,0:T(8,128)(2,1)S(1)}, u32[]{:S(2)}, u32[]{:S(2)}) collective-permute-start(bf16[32,32]{1,0:T(8,128)(2,1)S(1)} %maximum_select_fusion.2), channel_id=1, source_target_pairs={{0,8},{1,9},{2,10},{3,11},{4,12},{5,13},{6,14},{7,15},{8,0},{9,1},... | collective-permute-start | bytes 6152 | tf_op jit(solution)/shard_map/ppermute | solution.py:89
  44.4 2.2 %collective-permute-start.24 = (bf16[64,32]{1,0:T(8,128)(2,1)S(1)}, bf16[64,32]{1,0:T(8,128)(2,1)S(1)}, u32[]{:S(2)}, u32[]{:S(2)}) collective-permute-start(bf16[64,32]{1,0:T(8,128)(2,1)S(1)} %maximum_select_fusion.1), channel_id=1, source_target_pairs={{0,18},{1,19},{2,16},{3,17},{4,22},{5,23},{6,20},{7,21},{8,26},{9,... | collective-permute-start | bytes 12296 | tf_op jit(solution)/shard_map/ppermute | solution.py:89
  46.6 2.8 %collective-permute-done.24 = bf16[64,32]{1,0:T(8,128)(2,1)S(1)} collective-permute-done((bf16[64,32]{1,0:T(8,128)(2,1)S(1)}, bf16[64,32]{1,0:T(8,128)(2,1)S(1)}, u32[]{:S(2)}, u32[]{:S(2)}) %collective-permute-start.24) | collective-permute-done | bytes 4128 | tf_op jit(solution)/shard_map/ppermute | solution.py:89
  51.5 6.4 %collective-permute-done.9.refs_2_ = bf16[512,896]{1,0:T(8,128)(2,1)} collective-permute-done((bf16[512,896]{1,0:T(8,128)(2,1)S(1)}, bf16[512,896]{1,0:T(8,128)(2,1)}, u32[]{:S(2)}, u32[]{:S(2)}) %collective-permute-start.9) | collective-permute-done | bytes 917536 | tf_op jit(solution)/shard_map/ppermute | solution.py:119
  58.4 3.2 %collective-permute-done.6.refs_0_ = bf16[512,896]{1,0:T(8,128)(2,1)S(1)} collective-permute-done((bf16[512,896]{1,0:T(8,128)(2,1)S(1)}, bf16[512,896]{1,0:T(8,128)(2,1)S(1)}, u32[]{:S(2)}, u32[]{:S(2)}) %collective-permute-start.6) | collective-permute-done | bytes 917536 | tf_op jit(solution)/shard_map/ppermute | solution.py:116
  61.7 11.0 %collective-permute-done.15.refs_1_ = bf16[512,896]{1,0:T(8,128)(2,1)S(1)} collective-permute-done((bf16[512,896]{1,0:T(8,128)(2,1)S(1)}, bf16[512,896]{1,0:T(8,128)(2,1)S(1)}, u32[]{:S(2)}, u32[]{:S(2)}) %collective-permute-start.15) | collective-permute-done | bytes 917536 | tf_op jit(solution)/shard_map/ppermute | solution.py:122
  72.7 4.8 %collective-permute-done.16.refs_2_ = bf16[512,896]{1,0:T(8,128)(2,1)S(1)} collective-permute-done((bf16[512,896]{1,0:T(8,128)(2,1)S(1)}, bf16[512,896]{1,0:T(8,128)(2,1)S(1)}, u32[]{:S(2)}, u32[]{:S(2)}) %collective-permute-start.16) | collective-permute-done | bytes 917536 | tf_op jit(solution)/shard_map/ppermute | solution.py:119
  78.4 1.9 %collective-permute-done.1.refs_0_ = bf16[512,896]{1,0:T(8,128)(2,1)S(1)} collective-permute-done((bf16[512,896]{1,0:T(8,128)(2,1)}, bf16[512,896]{1,0:T(8,128)(2,1)S(1)}, u32[]{:S(2)}, u32[]{:S(2)}) %collective-permute-start.1) | collective-permute-done | bytes 917536 | tf_op jit(solution)/shard_map/ppermute | solution.py:116
  83.5 19.7 %collective-permute-done.7.refs_0_ = bf16[512,640]{1,0:T(8,128)(2,1)S(1)} collective-permute-done((bf16[512,640]{1,0:T(8,128)(2,1)S(1)}, bf16[512,640]{1,0:T(8,128)(2,1)S(1)}, u32[]{:S(2)}, u32[]{:S(2)}) %collective-permute-start.7) | collective-permute-done | bytes 655392 | tf_op jit(solution)/shard_map/ppermute | solution.py:122
  104.8 2.1 %collective-permute-start.12 = (bf16[512,256]{1,0:T(8,128)(2,1)S(1)}, bf16[512,256]{1,0:T(8,128)(2,1)S(1)}, u32[]{:S(2)}, u32[]{:S(2)}) collective-permute-start(bf16[512,256]{1,0:T(8,128)(2,1)S(1)} %slice.24), channel_id=1, source_target_pairs={{0,16},{16,0},{1,17},{17,1},{2,18},{18,2},{3,19},{19,3},{4,20},{20... | collective-permute-start | bytes 786440 | tf_op jit(solution)/shard_map/ppermute | solution.py:122
  110.2 12.9 %collective-permute-done.12.refs_1_ = bf16[512,256]{1,0:T(8,128)(2,1)S(1)} collective-permute-done((bf16[512,256]{1,0:T(8,128)(2,1)S(1)}, bf16[512,256]{1,0:T(8,128)(2,1)S(1)}, u32[]{:S(2)}, u32[]{:S(2)}) %collective-permute-start.12) | collective-permute-done | bytes 262176 | tf_op jit(solution)/shard_map/ppermute | solution.py:122
  123.8 2.5 %collective-permute-start.11 = (bf16[512,256]{1,0:T(8,128)(2,1)}, bf16[512,256]{1,0:T(8,128)(2,1)}, u32[]{:S(2)}, u32[]{:S(2)}) collective-permute-start(bf16[512,256]{1,0:T(8,128)(2,1)} %slice.23), channel_id=1, source_target_pairs={{0,96},{32,0},{64,32},{96,64},{1,97},{33,1},{65,33},{97,65},{2,98}... | collective-permute-start | bytes 786440 | tf_op jit(solution)/shard_map/ppermute | solution.py:119
  128.0 2.5 %shard_map.103 = (bf16[896,4096]{1,0:T(8,128)(2,1)}, bf16[896,4096]{1,0:T(8,128)(2,1)}) custom-call(bf16[512,896]{1,0:T(8,128)(2,1)S(1)} %add_convert_fusion.1.refs_0_, bf16[512,896]{1,0:T(8,128)(2,1)S(1)} %add_convert_fusion.refs_1_), custom_call_target="tpu_custom_call" | custom-call | bytes 3670016 | tf_op jit(solution)/shard_map/pallas_call | solution.py:71
  131.2 3.9 %shard_map.104 = (bf16[896,4096]{1,0:T(8,128)(2,1)}, bf16[896,4096]{1,0:T(8,128)(2,1)}) custom-call(bf16[512,896]{1,0:T(8,128)(2,1)} %collective-permute-done.refs_0_, bf16[512,896]{1,0:T(8,128)(2,1)} %collective-permute-done.3.refs_1_, bf16[512,896]{1,0:T(8,128)(2,1)} %collective-permute-done.9.refs_2_, ...), custom_call_target="tpu_custom_call", output_to_operand_aliasing={{0}: (3, {}), {1}: (4, {})} | custom-call | bytes 5505024 | tf_op jit(solution)/shard_map/pallas_call | solution.py:71
  135.2 3.4 %shard_map.105 = (bf16[896,4096]{1,0:T(8,128)(2,1)}, bf16[896,4096]{1,0:T(8,128)(2,1)}) custom-call(bf16[512,896]{1,0:T(8,128)(2,1)S(1)} %collective-permute-done.6.refs_0_, bf16[512,896]{1,0:T(8,128)(2,1)S(1)} %copy-done.8, bf16[512,896]{1,0:T(8,128)(2,1)S(1)} %copy-done.10, ...), custom_call_target="tpu_custom_call", output_to_operand_aliasing={{0}: (3, {}), {1}: (4, {})} | custom-call | bytes 5505024 | tf_op jit(solution)/shard_map/pallas_call | solution.py:71
  138.7 3.4 %shard_map.106 = (bf16[896,4096]{1,0:T(8,128)(2,1)}, bf16[896,4096]{1,0:T(8,128)(2,1)}) custom-call(bf16[512,896]{1,0:T(8,128)(2,1)S(1)} %copy-done.2, bf16[512,896]{1,0:T(8,128)(2,1)S(1)} %copy-done.6, bf16[512,896]{1,0:T(8,128)(2,1)S(1)} %copy-done.4, bf16[896,4096]{1,0:T(8,128)(2,1)} %get-tuple-element.19.refs_3_, ...), custom_call_target="tpu_custom_call", output_to_operand_aliasing={{0}: (3, {}), {1}: (4, {})} | custom-call | bytes 5505024 | tf_op jit(solution)/shard_map/pallas_call | solution.py:71
  142.1 3.4 %shard_map.107 = (bf16[896,4096]{1,0:T(8,128)(2,1)}, bf16[896,4096]{1,0:T(8,128)(2,1)}) custom-call(bf16[512,640]{1,0:T(8,128)(2,1)S(1)} %collective-permute-done.7.refs_0_, bf16[512,256]{1,0:T(8,128)(2,1)S(1)} %copy-done.14, bf16[512,896]{1,0:T(8,128)(2,1)S(1)} %copy-done.12, ...), custom_call_target="tpu_custom_call", output_to_operand_aliasing={{0}: (4, {}), {1}: (5, {})} | custom-call | bytes 5505024 | tf_op jit(solution)/shard_map/pallas_call | solution.py:71
  145.6 3.2 %shard_map.108 = (bf16[896,4096]{1,0:T(8,128)(2,1)}, bf16[896,4096]{1,0:T(8,128)(2,1)}) custom-call(bf16[512,640]{1,0:T(8,128)(2,1)} %collective-permute-done.2.refs_0_, bf16[512,256]{1,0:T(8,128)(2,1)} %collective-permute-done.5.refs_1_, bf16[512,640]{1,0:T(8,128)(2,1)} %collective-permute-done.8.refs_2_, ...), custom_call_target="tpu_custom_call", output_to_operand_aliasing={{0}: (4, {}), {1}: (5, {})} | custom-call | bytes 3670016 | tf_op jit(solution)/shard_map/pallas_call | solution.py:71
  (80 shorter events, 26.8 us)
Async XLA Ops:
  3.1 46.4 %collective-permute-start.3 = (bf16[512,896]{1,0:T(8,128)(2,1)S(1)}, bf16[512,896]{1,0:T(8,128)(2,1)}, u32[]{:S(2)}, u32[]{:S(2)}) collective-permute-start(bf16[512,896]{1,0:T(8,128)(2,1)S(1)} %add_convert_fusion.1.refs_0_), channel_id=1, source_target_pairs={{0,16},{16,0},{1,17},{17,1},{2,18},{18,2},{3,19},{19,3},{4,20},{20... | collective-permute-start | bytes 2752520 | tf_op jit(solution)/shard_map/ppermute | solution.py:122
  4.8 46.1 %collective-permute-start = (bf16[512,896]{1,0:T(8,128)(2,1)S(1)}, bf16[512,896]{1,0:T(8,128)(2,1)}, u32[]{:S(2)}, u32[]{:S(2)}) collective-permute-start(bf16[512,896]{1,0:T(8,128)(2,1)S(1)} %add_convert_fusion.1.refs_0_), channel_id=1, source_target_pairs={{0,32},{32,64},{64,96},{96,0},{1,33},{33,65},{65,97},{97,1},{2,34}... | collective-permute-start | bytes 2752520 | tf_op jit(solution)/shard_map/ppermute | solution.py:116
  7.0 4.3 %collective-permute-start.17 = (bf16[32]{0:T(256)(128)(2,1)S(1)}, bf16[32]{0:T(256)(128)(2,1)S(1)}, u32[]{:S(2)}, u32[]{:S(2)}) collective-permute-start(bf16[32]{0:T(256)(128)(2,1)S(1)} %add_convert_fusion.2), channel_id=1, source_target_pairs={{0,96},{32,0},{64,32},{96,64},{1,97},{33,1},{65,33},{97,65},{2,98}... | collective-permute-start | bytes 200 | tf_op jit(solution)/shard_map/ppermute | solution.py:99
  8.7 20.4 %collective-permute-start.18 = (bf16[32]{0:T(256)(128)(2,1)S(1)}, bf16[32]{0:T(256)(128)(2,1)S(1)}, u32[]{:S(2)}, u32[]{:S(2)}) collective-permute-start(bf16[32]{0:T(256)(128)(2,1)S(1)} %add_convert_fusion.2), channel_id=1, source_target_pairs={{0,64},{32,96},{64,0},{96,32},{1,65},{33,97},{65,1},{97,33},{2,66}... | collective-permute-start | bytes 200 | tf_op jit(solution)/shard_map/ppermute | solution.py:99
  10.7 18.4 %collective-permute-start.19 = (bf16[32]{0:T(256)(128)(2,1)S(1)}, bf16[32]{0:T(256)(128)(2,1)S(1)}, u32[]{:S(2)}, u32[]{:S(2)}) collective-permute-start(bf16[32]{0:T(256)(128)(2,1)S(1)} %add_convert_fusion.2), channel_id=1, source_target_pairs={{0,32},{32,64},{64,96},{96,0},{1,33},{33,65},{65,97},{97,1},{2,34}... | collective-permute-start | bytes 200 | tf_op jit(solution)/shard_map/ppermute | solution.py:99
  29.1 3.6 %collective-permute-start.20 = (bf16[4,32]{1,0:T(4,128)(2,1)S(1)}, bf16[4,32]{1,0:T(4,128)(2,1)S(1)}, u32[]{:S(2)}, u32[]{:S(2)}) collective-permute-start(bf16[4,32]{1,0:T(4,128)(2,1)S(1)} %select_select_fusion), channel_id=1, source_target_pairs={{0,16},{16,0},{1,17},{17,1},{2,18},{18,2},{3,19},{19,3},{4,20},{20... | collective-permute-start | bytes 776 | tf_op jit(solution)/shard_map/ppermute | solution.py:89
  34.5 23.4 %collective-permute-start.9 = (bf16[512,896]{1,0:T(8,128)(2,1)S(1)}, bf16[512,896]{1,0:T(8,128)(2,1)}, u32[]{:S(2)}, u32[]{:S(2)}) collective-permute-start(bf16[512,896]{1,0:T(8,128)(2,1)S(1)} %add_convert_fusion.refs_1_), channel_id=1, source_target_pairs={{0,96},{32,0},{64,32},{96,64},{1,97},{33,1},{65,33},{97,65},{2,98}... | collective-permute-start | bytes 2752520 | tf_op jit(solution)/shard_map/ppermute | solution.py:119
  35.2 3.7 %collective-permute-start.22 = (bf16[16,32]{1,0:T(8,128)(2,1)S(1)}, bf16[16,32]{1,0:T(8,128)(2,1)S(1)}, u32[]{:S(2)}, u32[]{:S(2)}) collective-permute-start(bf16[16,32]{1,0:T(8,128)(2,1)S(1)} %maximum_select_fusion.3), channel_id=1, source_target_pairs={{0,4},{1,5},{2,6},{3,7},{4,0},{5,1},{6,2},{7,3},{8,12},{9,13},{10,... | collective-permute-start | bytes 3080 | tf_op jit(solution)/shard_map/ppermute | solution.py:89
  37.2 24.4 %collective-permute-start.6 = (bf16[512,896]{1,0:T(8,128)(2,1)S(1)}, bf16[512,896]{1,0:T(8,128)(2,1)S(1)}, u32[]{:S(2)}, u32[]{:S(2)}) collective-permute-start(bf16[512,896]{1,0:T(8,128)(2,1)S(1)} %add_convert_fusion.refs_1_), channel_id=1, source_target_pairs={{0,32},{32,64},{64,96},{96,0},{1,33},{33,65},{65,97},{97,1},{2,34}... | collective-permute-start | bytes 2752520 | tf_op jit(solution)/shard_map/ppermute | solution.py:116
  38.9 5.5 %collective-permute-start.23 = (bf16[32,32]{1,0:T(8,128)(2,1)S(1)}, bf16[32,32]{1,0:T(8,128)(2,1)S(1)}, u32[]{:S(2)}, u32[]{:S(2)}) collective-permute-start(bf16[32,32]{1,0:T(8,128)(2,1)S(1)} %maximum_select_fusion.2), channel_id=1, source_target_pairs={{0,8},{1,9},{2,10},{3,11},{4,12},{5,13},{6,14},{7,15},{8,0},{9,1},... | collective-permute-start | bytes 6152 | tf_op jit(solution)/shard_map/ppermute | solution.py:89
  44.4 5.0 %collective-permute-start.24 = (bf16[64,32]{1,0:T(8,128)(2,1)S(1)}, bf16[64,32]{1,0:T(8,128)(2,1)S(1)}, u32[]{:S(2)}, u32[]{:S(2)}) collective-permute-start(bf16[64,32]{1,0:T(8,128)(2,1)S(1)} %maximum_select_fusion.1), channel_id=1, source_target_pairs={{0,18},{1,19},{2,16},{3,17},{4,22},{5,23},{6,20},{7,21},{8,26},{9,... | collective-permute-start | bytes 12296 | tf_op jit(solution)/shard_map/ppermute | solution.py:89
  49.5 23.2 %collective-permute-start.15 = (bf16[512,896]{1,0:T(8,128)(2,1)S(1)}, bf16[512,896]{1,0:T(8,128)(2,1)S(1)}, u32[]{:S(2)}, u32[]{:S(2)}) collective-permute-start(bf16[512,896]{1,0:T(8,128)(2,1)S(1)} %add_convert_fusion.refs_1_), channel_id=1, source_target_pairs={{0,16},{16,0},{1,17},{17,1},{2,18},{18,2},{3,19},{19,3},{4,20},{20... | collective-permute-start | bytes 2752520 | tf_op jit(solution)/shard_map/ppermute | solution.py:122
  49.5 28.0 %collective-permute-start.16 = (bf16[512,896]{1,0:T(8,128)(2,1)S(1)}, bf16[512,896]{1,0:T(8,128)(2,1)S(1)}, u32[]{:S(2)}, u32[]{:S(2)}) collective-permute-start(bf16[512,896]{1,0:T(8,128)(2,1)S(1)} %add_convert_fusion.1.refs_0_), channel_id=1, source_target_pairs={{0,96},{32,0},{64,32},{96,64},{1,97},{33,1},{65,33},{97,65},{2,98}... | collective-permute-start | bytes 2752520 | tf_op jit(solution)/shard_map/ppermute | solution.py:119
  50.8 29.5 %collective-permute-start.1 = (bf16[512,896]{1,0:T(8,128)(2,1)}, bf16[512,896]{1,0:T(8,128)(2,1)S(1)}, u32[]{:S(2)}, u32[]{:S(2)}) collective-permute-start(bf16[512,896]{1,0:T(8,128)(2,1)} %collective-permute-done.refs_0_), channel_id=1, source_target_pairs={{0,32},{32,64},{64,96},{96,0},{1,33},{33,65},{65,97},{97,1},{2,34}... | collective-permute-start | bytes 2752520 | tf_op jit(solution)/shard_map/ppermute | solution.py:116
  57.9 46.8 %collective-permute-start.10 = (bf16[512,896]{1,0:T(8,128)(2,1)}, bf16[512,896]{1,0:T(8,128)(2,1)S(1)}, u32[]{:S(2)}, u32[]{:S(2)}) collective-permute-start(bf16[512,896]{1,0:T(8,128)(2,1)} %collective-permute-done.9.refs_2_), channel_id=1, source_target_pairs={{0,16},{16,0},{1,17},{17,1},{2,18},{18,2},{3,19},{19,3},{4,20},{20... | collective-permute-start | bytes 2752520 | tf_op jit(solution)/shard_map/ppermute | solution.py:122
  61.7 43.1 %collective-permute-start.4 = (bf16[512,896]{1,0:T(8,128)(2,1)}, bf16[512,896]{1,0:T(8,128)(2,1)S(1)}, u32[]{:S(2)}, u32[]{:S(2)}) collective-permute-start(bf16[512,896]{1,0:T(8,128)(2,1)} %collective-permute-done.3.refs_1_), channel_id=1, source_target_pairs={{0,96},{32,0},{64,32},{96,64},{1,97},{33,1},{65,33},{97,65},{2,98}... | collective-permute-start | bytes 2752520 | tf_op jit(solution)/shard_map/ppermute | solution.py:119
  72.7 30.5 %collective-permute-start.7 = (bf16[512,640]{1,0:T(8,128)(2,1)S(1)}, bf16[512,640]{1,0:T(8,128)(2,1)S(1)}, u32[]{:S(2)}, u32[]{:S(2)}) collective-permute-start(bf16[512,640]{1,0:T(8,128)(2,1)S(1)} %slice.22), channel_id=1, source_target_pairs={{0,16},{16,0},{1,17},{17,1},{2,18},{18,2},{3,19},{19,3},{4,20},{20... | collective-permute-start | bytes 1966088 | tf_op jit(solution)/shard_map/ppermute | solution.py:122
  78.4 47.9 %collective-permute-start.13 = (bf16[512,896]{1,0:T(8,128)(2,1)}, bf16[512,896]{1,0:T(8,128)(2,1)S(1)}, u32[]{:S(2)}, u32[]{:S(2)}) collective-permute-start(bf16[512,896]{1,0:T(8,128)(2,1)} %collective-permute-done.3.refs_1_), channel_id=1, source_target_pairs={{0,32},{32,64},{64,96},{96,0},{1,33},{33,65},{65,97},{97,1},{2,34}... | collective-permute-start | bytes 2752520 | tf_op jit(solution)/shard_map/ppermute | solution.py:116
  80.3 61.8 %collective-permute-start.14 = (bf16[512,896]{1,0:T(8,128)(2,1)}, bf16[512,896]{1,0:T(8,128)(2,1)}, u32[]{:S(2)}, u32[]{:S(2)}) collective-permute-start(bf16[512,896]{1,0:T(8,128)(2,1)} %collective-permute-done.9.refs_2_), channel_id=1, source_target_pairs={{0,96},{32,0},{64,32},{96,64},{1,97},{33,1},{65,33},{97,65},{2,98}... | collective-permute-start | bytes 2752520 | tf_op jit(solution)/shard_map/ppermute | solution.py:119
  103.2 42.4 %collective-permute-start.8 = (bf16[512,640]{1,0:T(8,128)(2,1)S(1)}, bf16[512,640]{1,0:T(8,128)(2,1)}, u32[]{:S(2)}, u32[]{:S(2)}) collective-permute-start(bf16[512,640]{1,0:T(8,128)(2,1)S(1)} %collective-permute-done.7.refs_0_), channel_id=1, source_target_pairs={{0,32},{32,64},{64,96},{96,0},{1,33},{33,65},{65,97},{97,1},{2,34}... | collective-permute-start | bytes 1966088 | tf_op jit(solution)/shard_map/ppermute | solution.py:116
  104.7 40.8 %collective-permute-start.2 = (bf16[512,640]{1,0:T(8,128)(2,1)}, bf16[512,640]{1,0:T(8,128)(2,1)}, u32[]{:S(2)}, u32[]{:S(2)}) collective-permute-start(bf16[512,640]{1,0:T(8,128)(2,1)} %slice.20), channel_id=1, source_target_pairs={{0,16},{16,0},{1,17},{17,1},{2,18},{18,2},{3,19},{19,3},{4,20},{20... | collective-permute-start | bytes 1966088 | tf_op jit(solution)/shard_map/ppermute | solution.py:122
  104.8 18.3 %collective-permute-start.12 = (bf16[512,256]{1,0:T(8,128)(2,1)S(1)}, bf16[512,256]{1,0:T(8,128)(2,1)S(1)}, u32[]{:S(2)}, u32[]{:S(2)}) collective-permute-start(bf16[512,256]{1,0:T(8,128)(2,1)S(1)} %slice.24), channel_id=1, source_target_pairs={{0,16},{16,0},{1,17},{17,1},{2,18},{18,2},{3,19},{19,3},{4,20},{20... | collective-permute-start | bytes 786440 | tf_op jit(solution)/shard_map/ppermute | solution.py:122
  123.8 21.7 %collective-permute-start.11 = (bf16[512,256]{1,0:T(8,128)(2,1)}, bf16[512,256]{1,0:T(8,128)(2,1)}, u32[]{:S(2)}, u32[]{:S(2)}) collective-permute-start(bf16[512,256]{1,0:T(8,128)(2,1)} %slice.23), channel_id=1, source_target_pairs={{0,96},{32,0},{64,32},{96,64},{1,97},{33,1},{65,33},{97,65},{2,98}... | collective-permute-start | bytes 786440 | tf_op jit(solution)/shard_map/ppermute | solution.py:119
  127.3 18.3 %collective-permute-start.5 = (bf16[512,256]{1,0:T(8,128)(2,1)}, bf16[512,256]{1,0:T(8,128)(2,1)}, u32[]{:S(2)}, u32[]{:S(2)}) collective-permute-start(bf16[512,256]{1,0:T(8,128)(2,1)} %slice.21), channel_id=1, source_target_pairs={{0,96},{32,0},{64,32},{96,64},{1,97},{33,1},{65,33},{97,65},{2,98}... | collective-permute-start | bytes 786440 | tf_op jit(solution)/shard_map/ppermute | solution.py:119
  (16 other events, 70.5 us)
where the time goes:
time: 149 us
  waiting for transfers between devices  85.3 us (57%)
  starting transfers between devices  29.1 us (20%)
  Pallas kernels  19.8 us (13%)
  local copies, waits for them, and re-layouts  9.48 us (6%)
  matrix products  3.28 us (2%)
    ppermute x6, waiting for transfers between devices, across(): return lax.ppermute(v, 'xl', SWAP)  43.5 us
    pallas_call x6, Pallas kernels, place(): pl.pallas_call(kernel, out_shape=shapes, in_specs=[any_spec] * len(operan...  19.8 us
    ppermute x3, waiting for transfers between devices, gathered_gain(): part = lax.ppermute(gain, 'y', [(i, (i + shift) % 4) for i in range(4)])  17.7 us
    ppermute x6, waiting for transfers between devices, down(): return lax.ppermute(v, 'y', DOWN)  11.2 us
    ppermute x5, starting transfers between devices, doubled(): other = lax.ppermute(x, axis, pairs)  8.68 us
    ppermute x5, waiting for transfers between devices, doubled(): other = lax.ppermute(x, axis, pairs)  7.84 us
    ppermute x6, starting transfers between devices, down(): return lax.ppermute(v, 'y', DOWN)  6.62 us
    unnamed x30, local copies, waits for them, and re-layouts  6.37 us
  transfers between devices with their start and end apart: 25, of which 12 were waited for; matrix products, arithmetic and copies ran while one was open for 4% of the time, Pallas kernels for 11%

commit v1 on v0

--- a/solution.py
+++ b/solution.py
@@ -15,13 +15,13 @@
 
 
 def merged(train, low, high):
-    wide = train.astype(jnp.float32) + mix_rate * jnp.dot(
-        low, high, preferred_element_type=jnp.float32
+    change = lax.dot_general(
+        low, high, (((0,), (0,)), ((), ())), preferred_element_type=jnp.float32
     )
-    return wide.astype(jnp.bfloat16)
+    return (train.astype(jnp.float32) + mix_rate * change).astype(jnp.bfloat16)
 
 
-def place(outs, parts):
+def place(outs, parts, held=False):
     fresh = not isinstance(outs[0], jax.Array)
     count = len(parts)
     steps = [p.shape[1] // LANES for p, *_ in parts]
@@ -31,8 +31,8 @@
         piece_refs, refs = refs[:count], refs[count:]
         refs = refs[0 if fresh else 2 :]
         out_refs, refs = refs[:2], refs[2:]
-        taken, turned = refs[:count], refs[count : 2 * count]
-        in_sem, out_sem = refs[2 * count :]
+        taken, refs = ([], refs) if held else (refs[:count], refs[count:])
+        turned, (in_sem, out_sem) = refs[:count], refs[count:]
 
         def load(k, c):
             columns = pl.ds(pl.multiple_of(c * LANES, LANES), LANES)
@@ -50,15 +50,23 @@
             )
 
         for k in range(count):
-            for c in range(steps[k]):
+            for c in range(0 if held else steps[k]):
                 load(k, c).start()
         for k in range(count):
 
-            @pl.loop(0, steps[k])
-            def _(c):
-                load(k, c).wait()
-                turned[k][c] = taken[k][c].T
+            def step(c):
+                if held:
+                    turned[k][c] = piece_refs[k][:, c * LANES : (c + 1) * LANES].T
+                else:
+                    load(k, c).wait()
+                    turned[k][c] = taken[k][c].T
                 save(k, c).start()
+
+            if held:
+                for c in range(steps[k]):
+                    step(c)
+            else:
+                pl.loop(0, steps[k])(step)
 
         for k in range(count):
             for c in range(steps[k]):
@@ -71,10 +79,11 @@
     return pl.pallas_call(
         kernel,
         out_shape=shapes,
-        in_specs=[any_spec] * len(operands),
+        in_specs=[pl.BlockSpec(memory_space=pltpu.VMEM) if held else any_spec] * count
+            + [any_spec] * (len(operands) - count),
         out_specs=[any_spec] * 2,
         scratch_shapes=[
-            *[pltpu.VMEM((p.shape[1] // LANES, p.shape[0], LANES), p.dtype) for p, *_ in parts],
+            *([] if held else [pltpu.VMEM((p.shape[1] // LANES, p.shape[0], LANES), p.dtype) for p, *_ in parts]),
             *[pltpu.VMEM((p.shape[1] // LANES, LANES, p.shape[0]), p.dtype) for p, *_ in parts],
             pltpu.SemaphoreType.DMA((count, max(steps))),
             pltpu.SemaphoreType.DMA((count, max(steps))),
@@ -121,11 +130,16 @@
     def across(v):
         return lax.ppermute(v, "xl", SWAP)
 
-    g = merged(train_gate, low_gate, high_gate)
-    u = merged(train_up, low_up, high_up)
+    low_g, low_u = low_gate.T, low_up.T
+    raw_g_x, raw_g_m, raw_u_p = across(train_gate), up(train_gate), down(train_up)
+    low_g_x, low_g_m, low_u_p = across(low_g), up(low_g), down(low_u)
+    g = merged(train_gate, low_g, high_gate)
+    u = merged(train_up, low_u, high_up)
     gain = (norm_train + norm_step).astype(jnp.bfloat16)
 
-    g_m, g_x, u_p = up(g), across(g), down(u)
+    g_m = merged(raw_g_m, low_g_m, high_gate)
+    g_x = merged(raw_g_x, low_g_x, high_gate)
+    u_p = merged(raw_u_p, low_u_p, high_up)
     u_m, u_x, g_p = up(u), across(u), down(g)
     g_f, cg_p, cu_p = up(g_m), down(g_x), across(u_p)
     cu_m0, cu_m1 = across(u_m[:, :cut]), across(u_m[:, cut:])
@@ -145,6 +159,7 @@
     outs = place(
         outs,
         [(cg_f0, 0, 0, 2, 1), (cg_f1, 0, cut, 2, 1), (cu_f0, 1, 0, 2, 1), (cu_f1, 1, cut, 2, 1)],
+        held=True,
     )
     return (*outs, gathered_gain(gain))
 

time: 149 us -> 149 us (level)
  the two profiles are of different devices: /device:TPU:0 before, /device:TPU:10 now
where the time goes in v1:
time: 149 us; the launch traced here: 148 us
  waiting for transfers between devices  74.2 us (50%)
  starting transfers between devices  39.2 us (26%)
  Pallas kernels  19.1 us (13%)
  local copies, waits for them, and re-layouts  7.99 us (5%)
  matrix products  5.67 us (4%)
    ppermute x7, waiting for transfers between devices, across(): return lax.ppermute(v, 'xl', SWAP)  35.1 us
    ppermute x6, waiting for transfers between devices, up(): return lax.ppermute(v, 'y', UP)  28.1 us
    pallas_call x6, Pallas kernels, place(): pl.pallas_call(kernel, out_shape=shapes, in_specs=[pl.BlockSpec(memory_sp...  19.1 us
    ppermute x7, starting transfers between devices, down(): return lax.ppermute(v, 'y', DOWN)  13 us
    ppermute x5, starting transfers between devices, doubled(): other = lax.ppermute(x, axis, pairs)  8 us
    ppermute x5, waiting for transfers between devices, doubled(): other = lax.ppermute(x, axis, pairs)  6.97 us
    ppermute x7, starting transfers between devices, across(): return lax.ppermute(v, 'xl', SWAP)  6.83 us
    ppermute x6, starting transfers between devices, up(): return lax.ppermute(v, 'y', UP)  6.41 us
  transfers between devices with their start and end apart: 28, of which 14 were waited for; matrix products, arithmetic and copies ran while one was open for 6% of the time, Pallas kernels for 11%

profile of v1, /device:TPU:10, one launch (start us, length us, event | category | flops | bytes accessed | tf_op | source)
XLA Modules:
  0.0 148.3 jit_solution(16549383519000586604)
XLA Ops:
  1.9 2.6 %collective-permute-start.21 = (bf16[32]{0:T(256)(128)(2,1)S(1)}, bf16[32]{0:T(256)(128)(2,1)S(1)}, u32[]{:S(2)}, u32[]{:S(2)}) collective-permute-start(bf16[32]{0:T(256)(128)(2,1)S(1)} %add_convert_fusion.5), channel_id=1, source_target_pairs={{0,64},{32,96},{64,0},{96,32},{1,65},{33,97},{65,1},{97,33},{2,66}... | collective-permute-start | bytes 200 | tf_op jit(solution)/shard_map/ppermute | solution.py:108
  4.5 1.9 %collective-permute-start.22 = (bf16[32]{0:T(256)(128)(2,1)S(1)}, bf16[32]{0:T(256)(128)(2,1)S(1)}, u32[]{:S(2)}, u32[]{:S(2)}) collective-permute-start(bf16[32]{0:T(256)(128)(2,1)S(1)} %add_convert_fusion.5), channel_id=1, source_target_pairs={{0,32},{32,64},{64,96},{96,0},{1,33},{33,65},{65,97},{97,1},{2,34}... | collective-permute-start | bytes 200 | tf_op jit(solution)/shard_map/ppermute | solution.py:108
  8.7 3.0 %collective-permute-done.23 = bf16[4,32]{1,0:T(4,128)(2,1)S(1)} collective-permute-done((bf16[4,32]{1,0:T(4,128)(2,1)S(1)}, bf16[4,32]{1,0:T(4,128)(2,1)S(1)}, u32[]{:S(2)}, u32[]{:S(2)}) %collective-permute-start.23) | collective-permute-done | bytes 288 | tf_op jit(solution)/shard_map/ppermute | solution.py:98
  13.0 1.9 %collective-permute-start.25 = (bf16[16,32]{1,0:T(8,128)(2,1)S(1)}, bf16[16,32]{1,0:T(8,128)(2,1)S(1)}, u32[]{:S(2)}, u32[]{:S(2)}) collective-permute-start(bf16[16,32]{1,0:T(8,128)(2,1)S(1)} %maximum_select_fusion.3), channel_id=1, source_target_pairs={{0,4},{1,5},{2,6},{3,7},{4,0},{5,1},{6,2},{7,3},{8,12},{9,13},{10,... | collective-permute-start | bytes 3080 | tf_op jit(solution)/shard_map/ppermute | solution.py:98
  16.6 3.9 %collective-permute-start.26 = (bf16[32,32]{1,0:T(8,128)(2,1)S(1)}, bf16[32,32]{1,0:T(8,128)(2,1)S(1)}, u32[]{:S(2)}, u32[]{:S(2)}) collective-permute-start(bf16[32,32]{1,0:T(8,128)(2,1)S(1)} %maximum_select_fusion.2), channel_id=1, source_target_pairs={{0,8},{1,9},{2,10},{3,11},{4,12},{5,13},{6,14},{7,15},{8,0},{9,1},... | collective-permute-start | bytes 6152 | tf_op jit(solution)/shard_map/ppermute | solution.py:98
  23.7 1.8 %collective-permute-start.5 = (bf16[32,512]{1,0:T(8,128)(2,1)}, bf16[32,512]{1,0:T(8,128)(2,1)S(1)}, u32[]{:S(2)}, u32[]{:S(2)}) collective-permute-start(bf16[32,512]{1,0:T(8,128)(2,1)} %bitcast.17), channel_id=1, source_target_pairs={{0,16},{16,0},{1,17},{17,1},{2,18},{18,2},{3,19},{19,3},{4,20},{20... | collective-permute-start | bytes 98312 | tf_op jit(solution)/shard_map/ppermute | solution.py:131
  25.5 2.3 %collective-permute-start.11 = (bf16[512,896]{1,0:T(8,128)(2,1)}, bf16[512,896]{1,0:T(8,128)(2,1)S(1)}, u32[]{:S(2)}, u32[]{:S(2)}) collective-permute-start(bf16[512,896]{1,0:T(8,128)(2,1)} %param.11), channel_id=1, source_target_pairs={{0,96},{32,0},{64,32},{96,64},{1,97},{33,1},{65,33},{97,65},{2,98}... | collective-permute-start | bytes 2752520 | tf_op jit(solution)/shard_map/ppermute | solution.py:128
  29.8 12.9 %collective-permute-done.5 = bf16[32,512]{1,0:T(8,128)(2,1)S(1)} collective-permute-done((bf16[32,512]{1,0:T(8,128)(2,1)}, bf16[32,512]{1,0:T(8,128)(2,1)S(1)}, u32[]{:S(2)}, u32[]{:S(2)}) %collective-permute-start.5) | collective-permute-done | bytes 32800 | tf_op jit(solution)/shard_map/ppermute | solution.py:131
  42.8 1.9 %collective-permute-start.1 = (bf16[32,512]{1,0:T(8,128)(2,1)S(1)}, bf16[32,512]{1,0:T(8,128)(2,1)S(1)}, u32[]{:S(2)}, u32[]{:S(2)}) collective-permute-start(bf16[32,512]{1,0:T(8,128)(2,1)S(1)} %bitcast.18), channel_id=1, source_target_pairs={{0,32},{32,64},{64,96},{96,0},{1,33},{33,65},{65,97},{97,1},{2,34}... | collective-permute-start | bytes 98312 | tf_op jit(solution)/shard_map/ppermute | solution.py:125
  44.7 2.1 %collective-permute-done.12 = bf16[32,512]{1,0:T(8,128)(2,1)S(1)} collective-permute-done((bf16[32,512]{1,0:T(8,128)(2,1)}, bf16[32,512]{1,0:T(8,128)(2,1)S(1)}, u32[]{:S(2)}, u32[]{:S(2)}) %collective-permute-start.12) | collective-permute-done | bytes 32800 | tf_op jit(solution)/shard_map/ppermute | solution.py:128
  54.7 1.8 %collective-permute-start.6 = (bf16[512,896]{1,0:T(8,128)(2,1)S(1)}, bf16[512,896]{1,0:T(8,128)(2,1)S(1)}, u32[]{:S(2)}, u32[]{:S(2)}) collective-permute-start(bf16[512,896]{1,0:T(8,128)(2,1)S(1)} %add_convert_fusion.3.refs_1_), channel_id=1, source_target_pairs={{0,96},{32,0},{64,32},{96,64},{1,97},{33,1},{65,33},{97,65},{2,98}... | collective-permute-start | bytes 2752520 | tf_op jit(solution)/shard_map/ppermute | solution.py:128
  56.9 13.2 %collective-permute-done.8.refs_0_ = bf16[512,896]{1,0:T(8,128)(2,1)S(1)} collective-permute-done((bf16[512,896]{1,0:T(8,128)(2,1)S(1)}, bf16[512,896]{1,0:T(8,128)(2,1)S(1)}, u32[]{:S(2)}, u32[]{:S(2)}) %collective-permute-start.8) | collective-permute-done | bytes 917536 | tf_op jit(solution)/shard_map/ppermute | solution.py:125
  74.9 14.9 %collective-permute-done.2.refs_0_ = bf16[512,896]{1,0:T(8,128)(2,1)S(1)} collective-permute-done((bf16[512,896]{1,0:T(8,128)(2,1)S(1)}, bf16[512,896]{1,0:T(8,128)(2,1)S(1)}, u32[]{:S(2)}, u32[]{:S(2)}) %collective-permute-start.2) | collective-permute-done | bytes 917536 | tf_op jit(solution)/shard_map/ppermute | solution.py:125
  89.8 3.2 %collective-permute-start.17 = (bf16[512,896]{1,0:T(8,128)(2,1)S(1)}, bf16[512,896]{1,0:T(8,128)(2,1)}, u32[]{:S(2)}, u32[]{:S(2)}) collective-permute-start(bf16[512,896]{1,0:T(8,128)(2,1)S(1)} %add_convert_fusion.1.refs_2_), channel_id=1, source_target_pairs={{0,96},{32,0},{64,32},{96,64},{1,97},{33,1},{65,33},{97,65},{2,98}... | collective-permute-start | bytes 2752520 | tf_op jit(solution)/shard_map/ppermute | solution.py:128
  94.0 9.5 %collective-permute-done.9.refs_0_ = bf16[512,640]{1,0:T(8,128)(2,1)S(1)} collective-permute-done((bf16[512,640]{1,0:T(8,128)(2,1)S(1)}, bf16[512,640]{1,0:T(8,128)(2,1)S(1)}, u32[]{:S(2)}, u32[]{:S(2)}) %collective-permute-start.9) | collective-permute-done | bytes 655392 | tf_op jit(solution)/shard_map/ppermute | solution.py:131
  104.8 1.8 %collective-permute-start.15 = (bf16[512,256]{1,0:T(8,128)(2,1)S(1)}, bf16[512,256]{1,0:T(8,128)(2,1)S(1)}, u32[]{:S(2)}, u32[]{:S(2)}) collective-permute-start(bf16[512,256]{1,0:T(8,128)(2,1)S(1)} %slice.24), channel_id=1, source_target_pairs={{0,16},{16,0},{1,17},{17,1},{2,18},{18,2},{3,19},{19,3},{4,20},{20... | collective-permute-start | bytes 786440 | tf_op jit(solution)/shard_map/ppermute | solution.py:131
  109.0 12.5 %collective-permute-done.15.refs_1_ = bf16[512,256]{1,0:T(8,128)(2,1)S(1)} collective-permute-done((bf16[512,256]{1,0:T(8,128)(2,1)S(1)}, bf16[512,256]{1,0:T(8,128)(2,1)S(1)}, u32[]{:S(2)}, u32[]{:S(2)}) %collective-permute-start.15) | collective-permute-done | bytes 262176 | tf_op jit(solution)/shard_map/ppermute | solution.py:131
  124.7 2.1 %collective-permute-start.14 = (bf16[512,256]{1,0:T(8,128)(2,1)}, bf16[512,256]{1,0:T(8,128)(2,1)}, u32[]{:S(2)}, u32[]{:S(2)}) collective-permute-start(bf16[512,256]{1,0:T(8,128)(2,1)} %slice.23), channel_id=1, source_target_pairs={{0,96},{32,0},{64,32},{96,64},{1,97},{33,1},{65,33},{97,65},{2,98}... | collective-permute-start | bytes 786440 | tf_op jit(solution)/shard_map/ppermute | solution.py:128
  126.8 2.5 %shard_map.103 = (bf16[896,4096]{1,0:T(8,128)(2,1)}, bf16[896,4096]{1,0:T(8,128)(2,1)}) custom-call(bf16[512,896]{1,0:T(8,128)(2,1)S(1)} %add_convert_fusion.refs_0_, bf16[512,896]{1,0:T(8,128)(2,1)S(1)} %add_convert_fusion.2.refs_1_), custom_call_target="tpu_custom_call" | custom-call | bytes 3670016 | tf_op jit(solution)/shard_map/pallas_call | solution.py:79
  131.2 3.4 %shard_map.104 = (bf16[896,4096]{1,0:T(8,128)(2,1)}, bf16[896,4096]{1,0:T(8,128)(2,1)}) custom-call(bf16[512,896]{1,0:T(8,128)(2,1)S(1)} %add_convert_fusion.4.refs_0_, bf16[512,896]{1,0:T(8,128)(2,1)S(1)} %copy-done.2, bf16[512,896]{1,0:T(8,128)(2,1)S(1)} %add_convert_fusion.1.refs_2_, ...), custom_call_target="tpu_custom_call", output_to_operand_aliasing={{0}: (3, {}), {1}: (4, {})} | custom-call | bytes 5505024 | tf_op jit(solution)/shard_map/pallas_call | solution.py:79
  134.7 3.4 %shard_map.105 = (bf16[896,4096]{1,0:T(8,128)(2,1)}, bf16[896,4096]{1,0:T(8,128)(2,1)}) custom-call(bf16[512,896]{1,0:T(8,128)(2,1)S(1)} %collective-permute-done.8.refs_0_, bf16[512,896]{1,0:T(8,128)(2,1)S(1)} %copy-done.10, bf16[512,896]{1,0:T(8,128)(2,1)S(1)} %copy-done.12, ...), custom_call_target="tpu_custom_call", output_to_operand_aliasing={{0}: (3, {}), {1}: (4, {})} | custom-call | bytes 5505024 | tf_op jit(solution)/shard_map/pallas_call | solution.py:79
  138.2 3.4 %shard_map.106 = (bf16[896,4096]{1,0:T(8,128)(2,1)}, bf16[896,4096]{1,0:T(8,128)(2,1)}) custom-call(bf16[512,896]{1,0:T(8,128)(2,1)S(1)} %copy-done.4, bf16[512,896]{1,0:T(8,128)(2,1)S(1)} %copy-done.6, bf16[512,896]{1,0:T(8,128)(2,1)S(1)} %copy-done.8, bf16[896,4096]{1,0:T(8,128)(2,1)} %get-tuple-element.19.refs_3_, ...), custom_call_target="tpu_custom_call", output_to_operand_aliasing={{0}: (3, {}), {1}: (4, {})} | custom-call | bytes 5505024 | tf_op jit(solution)/shard_map/pallas_call | solution.py:79
  141.6 3.4 %shard_map.107 = (bf16[896,4096]{1,0:T(8,128)(2,1)}, bf16[896,4096]{1,0:T(8,128)(2,1)}) custom-call(bf16[512,640]{1,0:T(8,128)(2,1)S(1)} %collective-permute-done.9.refs_0_, bf16[512,256]{1,0:T(8,128)(2,1)S(1)} %copy-done.16, bf16[512,896]{1,0:T(8,128)(2,1)S(1)} %copy-done.14, ...), custom_call_target="tpu_custom_call", output_to_operand_aliasing={{0}: (4, {}), {1}: (5, {})} | custom-call | bytes 5505024 | tf_op jit(solution)/shard_map/pallas_call | solution.py:79
  145.0 3.1 %shard_map.108 = (bf16[896,4096]{1,0:T(8,128)(2,1)}, bf16[896,4096]{1,0:T(8,128)(2,1)}) custom-call(bf16[512,640]{1,0:T(8,128)(2,1)} %collective-permute-done.3.refs_0_, bf16[512,256]{1,0:T(8,128)(2,1)} %collective-permute-done.7.refs_1_, bf16[512,640]{1,0:T(8,128)(2,1)} %collective-permute-done.10.refs_2_, ...), custom_call_target="tpu_custom_call", output_to_operand_aliasing={{0}: (4, {}), {1}: (5, {})} | custom-call | bytes 3670016 | tf_op jit(solution)/shard_map/pallas_call | solution.py:79
  (99 shorter events, 34.6 us)
Async XLA Ops:
  1.4 5.0 %collective-permute-start.20 = (bf16[32]{0:T(256)(128)(2,1)S(1)}, bf16[32]{0:T(256)(128)(2,1)S(1)}, u32[]{:S(2)}, u32[]{:S(2)}) collective-permute-start(bf16[32]{0:T(256)(128)(2,1)S(1)} %add_convert_fusion.5), channel_id=1, source_target_pairs={{0,96},{32,0},{64,32},{96,64},{1,97},{33,1},{65,33},{97,65},{2,98}... | collective-permute-start | bytes 200 | tf_op jit(solution)/shard_map/ppermute | solution.py:108
  1.9 5.1 %collective-permute-start.21 = (bf16[32]{0:T(256)(128)(2,1)S(1)}, bf16[32]{0:T(256)(128)(2,1)S(1)}, u32[]{:S(2)}, u32[]{:S(2)}) collective-permute-start(bf16[32]{0:T(256)(128)(2,1)S(1)} %add_convert_fusion.5), channel_id=1, source_target_pairs={{0,64},{32,96},{64,0},{96,32},{1,65},{33,97},{65,1},{97,33},{2,66}... | collective-permute-start | bytes 200 | tf_op jit(solution)/shard_map/ppermute | solution.py:108
  6.4 43.0 %collective-permute-start = (bf16[512,896]{1,0:T(8,128)(2,1)}, bf16[512,896]{1,0:T(8,128)(2,1)}, u32[]{:S(2)}, u32[]{:S(2)}) collective-permute-start(bf16[512,896]{1,0:T(8,128)(2,1)} %param.8), channel_id=1, source_target_pairs={{0,32},{32,64},{64,96},{96,0},{1,33},{33,65},{65,97},{97,1},{2,34}... | collective-permute-start | bytes 2752520 | tf_op jit(solution)/shard_map/ppermute | solution.py:125
  16.6 5.5 %collective-permute-start.26 = (bf16[32,32]{1,0:T(8,128)(2,1)S(1)}, bf16[32,32]{1,0:T(8,128)(2,1)S(1)}, u32[]{:S(2)}, u32[]{:S(2)}) collective-permute-start(bf16[32,32]{1,0:T(8,128)(2,1)S(1)} %maximum_select_fusion.2), channel_id=1, source_target_pairs={{0,8},{1,9},{2,10},{3,11},{4,12},{5,13},{6,14},{7,15},{8,0},{9,1},... | collective-permute-start | bytes 6152 | tf_op jit(solution)/shard_map/ppermute | solution.py:98
  20.5 32.2 %collective-permute-start.4 = (bf16[512,896]{1,0:T(8,128)(2,1)}, bf16[512,896]{1,0:T(8,128)(2,1)}, u32[]{:S(2)}, u32[]{:S(2)}) collective-permute-start(bf16[512,896]{1,0:T(8,128)(2,1)} %param.8), channel_id=1, source_target_pairs={{0,16},{16,0},{1,17},{17,1},{2,18},{18,2},{3,19},{19,3},{4,20},{20... | collective-permute-start | bytes 2752520 | tf_op jit(solution)/shard_map/ppermute | solution.py:131
  22.1 5.6 %collective-permute-start.27 = (bf16[64,32]{1,0:T(8,128)(2,1)S(1)}, bf16[64,32]{1,0:T(8,128)(2,1)S(1)}, u32[]{:S(2)}, u32[]{:S(2)}) collective-permute-start(bf16[64,32]{1,0:T(8,128)(2,1)S(1)} %maximum_select_fusion.1), channel_id=1, source_target_pairs={{0,18},{1,19},{2,16},{3,17},{4,22},{5,23},{6,20},{7,21},{8,26},{9,... | collective-permute-start | bytes 12296 | tf_op jit(solution)/shard_map/ppermute | solution.py:98
  23.7 19.1 %collective-permute-start.5 = (bf16[32,512]{1,0:T(8,128)(2,1)}, bf16[32,512]{1,0:T(8,128)(2,1)S(1)}, u32[]{:S(2)}, u32[]{:S(2)}) collective-permute-start(bf16[32,512]{1,0:T(8,128)(2,1)} %bitcast.17), channel_id=1, source_target_pairs={{0,16},{16,0},{1,17},{17,1},{2,18},{18,2},{3,19},{19,3},{4,20},{20... | collective-permute-start | bytes 98312 | tf_op jit(solution)/shard_map/ppermute | solution.py:131
  25.5 29.2 %collective-permute-start.11 = (bf16[512,896]{1,0:T(8,128)(2,1)}, bf16[512,896]{1,0:T(8,128)(2,1)S(1)}, u32[]{:S(2)}, u32[]{:S(2)}) collective-permute-start(bf16[512,896]{1,0:T(8,128)(2,1)} %param.11), channel_id=1, source_target_pairs={{0,96},{32,0},{64,32},{96,64},{1,97},{33,1},{65,33},{97,65},{2,98}... | collective-permute-start | bytes 2752520 | tf_op jit(solution)/shard_map/ppermute | solution.py:128
  27.7 19.0 %collective-permute-start.12 = (bf16[32,512]{1,0:T(8,128)(2,1)}, bf16[32,512]{1,0:T(8,128)(2,1)S(1)}, u32[]{:S(2)}, u32[]{:S(2)}) collective-permute-start(bf16[32,512]{1,0:T(8,128)(2,1)} %bitcast.16), channel_id=1, source_target_pairs={{0,96},{32,0},{64,32},{96,64},{1,97},{33,1},{65,33},{97,65},{2,98}... | collective-permute-start | bytes 98312 | tf_op jit(solution)/shard_map/ppermute | solution.py:128
  42.8 6.2 %collective-permute-start.1 = (bf16[32,512]{1,0:T(8,128)(2,1)S(1)}, bf16[32,512]{1,0:T(8,128)(2,1)S(1)}, u32[]{:S(2)}, u32[]{:S(2)}) collective-permute-start(bf16[32,512]{1,0:T(8,128)(2,1)S(1)} %bitcast.18), channel_id=1, source_target_pairs={{0,32},{32,64},{64,96},{96,0},{1,33},{33,65},{65,97},{97,1},{2,34}... | collective-permute-start | bytes 98312 | tf_op jit(solution)/shard_map/ppermute | solution.py:125
  46.8 23.3 %collective-permute-start.8 = (bf16[512,896]{1,0:T(8,128)(2,1)S(1)}, bf16[512,896]{1,0:T(8,128)(2,1)S(1)}, u32[]{:S(2)}, u32[]{:S(2)}) collective-permute-start(bf16[512,896]{1,0:T(8,128)(2,1)S(1)} %add_convert_fusion.2.refs_1_), channel_id=1, source_target_pairs={{0,32},{32,64},{64,96},{96,0},{1,33},{33,65},{65,97},{97,1},{2,34}... | collective-permute-start | bytes 2752520 | tf_op jit(solution)/shard_map/ppermute | solution.py:125
  49.0 21.6 %collective-permute-start.18 = (bf16[512,896]{1,0:T(8,128)(2,1)S(1)}, bf16[512,896]{1,0:T(8,128)(2,1)S(1)}, u32[]{:S(2)}, u32[]{:S(2)}) collective-permute-start(bf16[512,896]{1,0:T(8,128)(2,1)S(1)} %add_convert_fusion.2.refs_1_), channel_id=1, source_target_pairs={{0,16},{16,0},{1,17},{17,1},{2,18},{18,2},{3,19},{19,3},{4,20},{20... | collective-permute-start | bytes 2752520 | tf_op jit(solution)/shard_map/ppermute | solution.py:131
  49.3 23.2 %collective-permute-start.19 = (bf16[512,896]{1,0:T(8,128)(2,1)S(1)}, bf16[512,896]{1,0:T(8,128)(2,1)S(1)}, u32[]{:S(2)}, u32[]{:S(2)}) collective-permute-start(bf16[512,896]{1,0:T(8,128)(2,1)S(1)} %add_convert_fusion.refs_0_), channel_id=1, source_target_pairs={{0,96},{32,0},{64,32},{96,64},{1,97},{33,1},{65,33},{97,65},{2,98}... | collective-permute-start | bytes 2752520 | tf_op jit(solution)/shard_map/ppermute | solution.py:128
  52.7 37.1 %collective-permute-start.2 = (bf16[512,896]{1,0:T(8,128)(2,1)S(1)}, bf16[512,896]{1,0:T(8,128)(2,1)S(1)}, u32[]{:S(2)}, u32[]{:S(2)}) collective-permute-start(bf16[512,896]{1,0:T(8,128)(2,1)S(1)} %add_convert_fusion.4.refs_0_), channel_id=1, source_target_pairs={{0,32},{32,64},{64,96},{96,0},{1,33},{33,65},{65,97},{97,1},{2,34}... | collective-permute-start | bytes 2752520 | tf_op jit(solution)/shard_map/ppermute | solution.py:125
  54.7 49.8 %collective-permute-start.6 = (bf16[512,896]{1,0:T(8,128)(2,1)S(1)}, bf16[512,896]{1,0:T(8,128)(2,1)S(1)}, u32[]{:S(2)}, u32[]{:S(2)}) collective-permute-start(bf16[512,896]{1,0:T(8,128)(2,1)S(1)} %add_convert_fusion.3.refs_1_), channel_id=1, source_target_pairs={{0,96},{32,0},{64,32},{96,64},{1,97},{33,1},{65,33},{97,65},{2,98}... | collective-permute-start | bytes 2752520 | tf_op jit(solution)/shard_map/ppermute | solution.py:128
  70.1 34.7 %collective-permute-start.13 = (bf16[512,896]{1,0:T(8,128)(2,1)S(1)}, bf16[512,896]{1,0:T(8,128)(2,1)S(1)}, u32[]{:S(2)}, u32[]{:S(2)}) collective-permute-start(bf16[512,896]{1,0:T(8,128)(2,1)S(1)} %add_convert_fusion.1.refs_2_), channel_id=1, source_target_pairs={{0,16},{16,0},{1,17},{17,1},{2,18},{18,2},{3,19},{19,3},{4,20},{20... | collective-permute-start | bytes 2752520 | tf_op jit(solution)/shard_map/ppermute | solution.py:131
  70.5 32.9 %collective-permute-start.9 = (bf16[512,640]{1,0:T(8,128)(2,1)S(1)}, bf16[512,640]{1,0:T(8,128)(2,1)S(1)}, u32[]{:S(2)}, u32[]{:S(2)}) collective-permute-start(bf16[512,640]{1,0:T(8,128)(2,1)S(1)} %slice.22), channel_id=1, source_target_pairs={{0,16},{16,0},{1,17},{17,1},{2,18},{18,2},{3,19},{19,3},{4,20},{20... | collective-permute-start | bytes 1966088 | tf_op jit(solution)/shard_map/ppermute | solution.py:131
  73.5 50.2 %collective-permute-start.16 = (bf16[512,896]{1,0:T(8,128)(2,1)S(1)}, bf16[512,896]{1,0:T(8,128)(2,1)S(1)}, u32[]{:S(2)}, u32[]{:S(2)}) collective-permute-start(bf16[512,896]{1,0:T(8,128)(2,1)S(1)} %add_convert_fusion.3.refs_1_), channel_id=1, source_target_pairs={{0,32},{32,64},{64,96},{96,0},{1,33},{33,65},{65,97},{97,1},{2,34}... | collective-permute-start | bytes 2752520 | tf_op jit(solution)/shard_map/ppermute | solution.py:125
  89.8 51.8 %collective-permute-start.17 = (bf16[512,896]{1,0:T(8,128)(2,1)S(1)}, bf16[512,896]{1,0:T(8,128)(2,1)}, u32[]{:S(2)}, u32[]{:S(2)}) collective-permute-start(bf16[512,896]{1,0:T(8,128)(2,1)S(1)} %add_convert_fusion.1.refs_2_), channel_id=1, source_target_pairs={{0,96},{32,0},{64,32},{96,64},{1,97},{33,1},{65,33},{97,65},{2,98}... | collective-permute-start | bytes 2752520 | tf_op jit(solution)/shard_map/ppermute | solution.py:128
  103.5 41.5 %collective-permute-start.10 = (bf16[512,640]{1,0:T(8,128)(2,1)S(1)}, bf16[512,640]{1,0:T(8,128)(2,1)}, u32[]{:S(2)}, u32[]{:S(2)}) collective-permute-start(bf16[512,640]{1,0:T(8,128)(2,1)S(1)} %collective-permute-done.9.refs_0_), channel_id=1, source_target_pairs={{0,32},{32,64},{64,96},{96,0},{1,33},{33,65},{65,97},{97,1},{2,34}... | collective-permute-start | bytes 1966088 | tf_op jit(solution)/shard_map/ppermute | solution.py:125
  104.4 40.6 %collective-permute-start.3 = (bf16[512,640]{1,0:T(8,128)(2,1)}, bf16[512,640]{1,0:T(8,128)(2,1)}, u32[]{:S(2)}, u32[]{:S(2)}) collective-permute-start(bf16[512,640]{1,0:T(8,128)(2,1)} %slice.20), channel_id=1, source_target_pairs={{0,16},{16,0},{1,17},{17,1},{2,18},{18,2},{3,19},{19,3},{4,20},{20... | collective-permute-start | bytes 1966088 | tf_op jit(solution)/shard_map/ppermute | solution.py:131
  104.8 16.8 %collective-permute-start.15 = (bf16[512,256]{1,0:T(8,128)(2,1)S(1)}, bf16[512,256]{1,0:T(8,128)(2,1)S(1)}, u32[]{:S(2)}, u32[]{:S(2)}) collective-permute-start(bf16[512,256]{1,0:T(8,128)(2,1)S(1)} %slice.24), channel_id=1, source_target_pairs={{0,16},{16,0},{1,17},{17,1},{2,18},{18,2},{3,19},{19,3},{4,20},{20... | collective-permute-start | bytes 786440 | tf_op jit(solution)/shard_map/ppermute | solution.py:131
  122.3 22.7 %collective-permute-start.7 = (bf16[512,256]{1,0:T(8,128)(2,1)}, bf16[512,256]{1,0:T(8,128)(2,1)}, u32[]{:S(2)}, u32[]{:S(2)}) collective-permute-start(bf16[512,256]{1,0:T(8,128)(2,1)} %slice.21), channel_id=1, source_target_pairs={{0,96},{32,0},{64,32},{96,64},{1,97},{33,1},{65,33},{97,65},{2,98}... | collective-permute-start | bytes 786440 | tf_op jit(solution)/shard_map/ppermute | solution.py:128
  124.7 20.3 %collective-permute-start.14 = (bf16[512,256]{1,0:T(8,128)(2,1)}, bf16[512,256]{1,0:T(8,128)(2,1)}, u32[]{:S(2)}, u32[]{:S(2)}) collective-permute-start(bf16[512,256]{1,0:T(8,128)(2,1)} %slice.23), channel_id=1, source_target_pairs={{0,96},{32,0},{64,32},{96,64},{1,97},{33,1},{65,33},{97,65},{2,98}... | collective-permute-start | bytes 786440 | tf_op jit(solution)/shard_map/ppermute | solution.py:128
  (24 other events, 332.0 us)

commit v2 on v1

--- a/solution.py
+++ b/solution.py
@@ -9,6 +9,7 @@
 
 mix_rate = 1.0
 LANES = 128
+SHARE = 512
 UP = [(i, (i + 1) % 4) for i in range(4)]
 DOWN = [(i, (i - 1) % 4) for i in range(4)]
 SWAP = [(0, 1), (1, 0)]
@@ -25,6 +26,7 @@
     fresh = not isinstance(outs[0], jax.Array)
     count = len(parts)
     steps = [p.shape[1] // LANES for p, *_ in parts]
+    parts = [part if len(part) == 6 else (*part, 0) for part in parts]
 
     def kernel(*refs):
         y, xl = lax.axis_index("y"), lax.axis_index("xl")
@@ -44,7 +46,7 @@
             rows = pl.ds(pl.multiple_of(parts[k][2] + c * LANES, LANES), LANES)
             size = parts[k][0].shape[0]
             source = lax.rem(y + parts[k][3], 4) * 2 + lax.rem(xl + parts[k][4], 2)
-            columns = pl.ds(pl.multiple_of(source * size, LANES), size)
+            columns = pl.ds(pl.multiple_of(source * SHARE + parts[k][5], LANES), size)
             return pltpu.make_async_copy(
                 turned[k].at[c], out_refs[parts[k][1]].at[rows, columns], out_sem.at[k, c]
             )
@@ -119,7 +121,6 @@
 
 def per_device(train_gate, low_gate, high_gate, train_up, low_up, high_up, norm_train, norm_step):
     rows, width = train_gate.shape
-    cut = width * 5 // 7 // LANES * LANES
 
     def up(v):
         return lax.ppermute(v, "y", UP)
@@ -142,11 +143,13 @@
     u_p = merged(raw_u_p, low_u_p, high_up)
     u_m, u_x, g_p = up(u), across(u), down(g)
     g_f, cg_p, cu_p = up(g_m), down(g_x), across(u_p)
-    cu_m0, cu_m1 = across(u_m[:, :cut]), across(u_m[:, cut:])
+    near, mid, late = width * 4 // 7, width * 5 // 7, width * 6 // 7
+    cu_m0, cu_m1, cu_m2 = (across(u_m[:, :near]), across(u_m[:, near:mid]), across(u_m[:, mid:]))
     cg_m, u_f = up(g_x), down(u_p)
-    cg_f0 = across(g_f[:, :cut])
-    cg_f1, cu_f1 = down(cg_p[:, cut:]), down(cu_p[:, cut:])
-    cu_f0 = up(cu_m0)
+    cg_f0, cg_f1 = across(g_f[:, :near]), across(g_f[LANES:, near:mid])
+    cg_f2, cg_f3 = down(cg_p[:, mid:]), down(cg_p[:LANES, near:mid])
+    cu_f2, cu_f3 = down(cu_p[:, mid:late]), down(cu_p[:, late:])
+    cu_f0, cu_f1 = up(cu_m0), up(cu_m1)
 
     out = jax.ShapeDtypeStruct((width, rows * 8), jnp.bfloat16)
     outs = place((out, out), [(g, 0, 0, 0, 0), (u, 1, 0, 0, 0)])
@@ -154,11 +157,29 @@
     outs = place(outs, [(u_m, 1, 0, 3, 0), (u_x, 1, 0, 0, 1), (g_p, 0, 0, 1, 0)])
     outs = place(outs, [(g_f, 0, 0, 2, 0), (cg_p, 0, 0, 1, 1), (cu_p, 1, 0, 1, 1)])
     outs = place(
-        outs, [(cu_m0, 1, 0, 3, 1), (cu_m1, 1, cut, 3, 1), (cg_m, 0, 0, 3, 1), (u_f, 1, 0, 2, 0)]
+        outs,
+        [
+            (cu_m0, 1, 0, 3, 1),
+            (cu_m1, 1, near, 3, 1),
+            (cu_m2, 1, mid, 3, 1),
+            (cg_m, 0, 0, 3, 1),
+            (u_f, 1, 0, 2, 0),
+        ],
     )
     outs = place(
         outs,
-        [(cg_f0, 0, 0, 2, 1), (cg_f1, 0, cut, 2, 1), (cu_f0, 1, 0, 2, 1), (cu_f1, 1, cut, 2, 1)],
+        [
+            (cg_f0, 0, 0, 2, 1),
+            (cu_f0, 1, 0, 2, 1),
+            (cg_f2, 0, mid, 2, 1),
+            (cg_f3, 0, near, 2, 1),
+            (cu_f2, 1, mid, 2, 1),
+        ],
+        held=True,
+    )
+    outs = place(
+        outs,
+        [(cg_f1, 0, near, 2, 1, LANES), (cu_f1, 1, near, 2, 1), (cu_f3, 1, late, 2, 1)],
         held=True,
     )
     return (*outs, gathered_gain(gain))

time: 149 us -> 188 us (1.26)
  the two profiles are of different devices: /device:TPU:10 before, /device:TPU:0 now
where the time goes in v2:
time: 188 us; the launch traced here: 187 us
  waiting for transfers between devices  102 us (54%)
  starting transfers between devices  42.4 us (23%)
  Pallas kernels  21.3 us (11%)
  local copies, waits for them, and re-layouts  12.9 us (7%)
  matrix products  6.87 us (4%)
    ppermute x9, waiting for transfers between devices, across(): return lax.ppermute(v, 'xl', SWAP)  33.8 us
    ppermute x7, waiting for transfers between devices, up(): return lax.ppermute(v, 'y', UP)  29.5 us
    pallas_call x7, Pallas kernels, place(): pl.pallas_call(kernel, out_shape=shapes, in_specs=[pl.BlockSpec(memory_sp...  21.3 us
    ppermute x5, waiting for transfers between devices, doubled(): other = lax.ppermute(x, axis, pairs)  18.5 us
    ppermute x9, waiting for transfers between devices, down(): return lax.ppermute(v, 'y', DOWN)  17.9 us
    ppermute x9, starting transfers between devices, down(): return lax.ppermute(v, 'y', DOWN)  13.6 us
    ppermute x5, starting transfers between devices, doubled(): other = lax.ppermute(x, axis, pairs)  9.31 us
    unnamed x50, local copies, waits for them, and re-layouts  8.91 us
  transfers between devices with their start and end apart: 33, of which 12 were waited for; matrix products, arithmetic and copies ran while one was open for 6% of the time, Pallas kernels for 10%

profile of v2, /device:TPU:0, one launch (start us, length us, event | category | flops | bytes accessed | tf_op | source)
XLA Modules:
  0.0 187.4 jit_solution(15123039951502049425)
XLA Ops:
  1.4 3.1 %collective-permute-start.25 = (bf16[32]{0:T(256)(128)(2,1)S(1)}, bf16[32]{0:T(256)(128)(2,1)S(1)}, u32[]{:S(2)}, u32[]{:S(2)}) collective-permute-start(bf16[32]{0:T(256)(128)(2,1)S(1)} %add_convert_fusion.5), channel_id=1, source_target_pairs={{0,96},{32,0},{64,32},{96,64},{1,97},{33,1},{65,33},{97,65},{2,98}... | collective-permute-start | bytes 200 | tf_op jit(solution)/shard_map/ppermute | solution.py:110
  7.6 2.0 %collective-permute-done.26 = bf16[32]{0:T(256)(128)(2,1)S(1)} collective-permute-done((bf16[32]{0:T(256)(128)(2,1)S(1)}, bf16[32]{0:T(256)(128)(2,1)S(1)}, u32[]{:S(2)}, u32[]{:S(2)}) %collective-permute-start.26) | collective-permute-done | bytes 96 | tf_op jit(solution)/shard_map/ppermute | solution.py:110
  11.5 16.2 %collective-permute-done.28 = bf16[4,32]{1,0:T(4,128)(2,1)S(1)} collective-permute-done((bf16[4,32]{1,0:T(4,128)(2,1)S(1)}, bf16[4,32]{1,0:T(4,128)(2,1)S(1)}, u32[]{:S(2)}, u32[]{:S(2)}) %collective-permute-start.28) | collective-permute-done | bytes 288 | tf_op jit(solution)/shard_map/ppermute | solution.py:100
  28.9 1.9 %collective-permute-start.30 = (bf16[16,32]{1,0:T(8,128)(2,1)S(1)}, bf16[16,32]{1,0:T(8,128)(2,1)S(1)}, u32[]{:S(2)}, u32[]{:S(2)}) collective-permute-start(bf16[16,32]{1,0:T(8,128)(2,1)S(1)} %maximum_select_fusion.3), channel_id=1, source_target_pairs={{0,4},{1,5},{2,6},{3,7},{4,0},{5,1},{6,2},{7,3},{8,12},{9,13},{10,... | collective-permute-start | bytes 3080 | tf_op jit(solution)/shard_map/ppermute | solution.py:100
  30.8 1.9 %collective-permute-start = (bf16[512,896]{1,0:T(8,128)(2,1)}, bf16[512,896]{1,0:T(8,128)(2,1)}, u32[]{:S(2)}, u32[]{:S(2)}) collective-permute-start(bf16[512,896]{1,0:T(8,128)(2,1)} %param.8), channel_id=1, source_target_pairs={{0,32},{32,64},{64,96},{96,0},{1,33},{33,65},{65,97},{97,1},{2,34}... | collective-permute-start | bytes 2752520 | tf_op jit(solution)/shard_map/ppermute | solution.py:126
  32.7 3.7 %collective-permute-start.31 = (bf16[32,32]{1,0:T(8,128)(2,1)S(1)}, bf16[32,32]{1,0:T(8,128)(2,1)S(1)}, u32[]{:S(2)}, u32[]{:S(2)}) collective-permute-start(bf16[32,32]{1,0:T(8,128)(2,1)S(1)} %maximum_select_fusion.2), channel_id=1, source_target_pairs={{0,8},{1,9},{2,10},{3,11},{4,12},{5,13},{6,14},{7,15},{8,0},{9,1},... | collective-permute-start | bytes 6152 | tf_op jit(solution)/shard_map/ppermute | solution.py:100
  38.1 1.9 %collective-permute-start.4 = (bf16[512,896]{1,0:T(8,128)(2,1)S(1)}, bf16[512,896]{1,0:T(8,128)(2,1)S(1)}, u32[]{:S(2)}, u32[]{:S(2)}) collective-permute-start(bf16[512,896]{1,0:T(8,128)(2,1)S(1)} %add_convert_fusion.3.refs_1_), channel_id=1, source_target_pairs={{0,32},{32,64},{64,96},{96,0},{1,33},{33,65},{65,97},{97,1},{2,34}... | collective-permute-start | bytes 2752520 | tf_op jit(solution)/shard_map/ppermute | solution.py:126
  45.3 29.4 %collective-permute-done.1 = bf16[32,512]{1,0:T(8,128)(2,1)S(1)} collective-permute-done((bf16[32,512]{1,0:T(8,128)(2,1)S(1)}, bf16[32,512]{1,0:T(8,128)(2,1)S(1)}, u32[]{:S(2)}, u32[]{:S(2)}) %collective-permute-start.1) | collective-permute-done | bytes 32800 | tf_op jit(solution)/shard_map/ppermute | solution.py:126
  79.6 2.1 %collective-permute-start.32 = (bf16[64,32]{1,0:T(8,128)(2,1)S(1)}, bf16[64,32]{1,0:T(8,128)(2,1)S(1)}, u32[]{:S(2)}, u32[]{:S(2)}) collective-permute-start(bf16[64,32]{1,0:T(8,128)(2,1)S(1)} %maximum_select_fusion.1), channel_id=1, source_target_pairs={{0,18},{1,19},{2,16},{3,17},{4,22},{5,23},{6,20},{7,21},{8,26},{9,... | collective-permute-start | bytes 12296 | tf_op jit(solution)/shard_map/ppermute | solution.py:100
  86.3 13.9 %collective-permute-done.8 = bf16[32,512]{1,0:T(8,128)(2,1)S(1)} collective-permute-done((bf16[32,512]{1,0:T(8,128)(2,1)S(1)}, bf16[32,512]{1,0:T(8,128)(2,1)S(1)}, u32[]{:S(2)}, u32[]{:S(2)}) %collective-permute-start.8) | collective-permute-done | bytes 32800 | tf_op jit(solution)/shard_map/ppermute | solution.py:129
  105.1 13.4 %collective-permute-done.5.refs_1_ = bf16[512,128]{1,0:T(8,128)(2,1)S(1)} collective-permute-done((bf16[512,128]{1,0:T(8,128)(2,1)S(1)}, bf16[512,128]{1,0:T(8,128)(2,1)S(1)}, u32[]{:S(2)}, u32[]{:S(2)}) %collective-permute-start.5) | collective-permute-done | bytes 131104 | tf_op jit(solution)/shard_map/ppermute | solution.py:132
  119.0 5.1 %collective-permute-done.20.refs_2_ = bf16[512,256]{1,0:T(8,128)(2,1)S(1)} collective-permute-done((bf16[512,256]{1,0:T(8,128)(2,1)S(1)}, bf16[512,256]{1,0:T(8,128)(2,1)S(1)}, u32[]{:S(2)}, u32[]{:S(2)}) %collective-permute-start.20) | collective-permute-done | bytes 262176 | tf_op jit(solution)/shard_map/ppermute | solution.py:132
  125.1 3.0 %collective-permute-start.22 = (bf16[512,896]{1,0:T(8,128)(2,1)S(1)}, bf16[512,896]{1,0:T(8,128)(2,1)S(1)}, u32[]{:S(2)}, u32[]{:S(2)}) collective-permute-start(bf16[512,896]{1,0:T(8,128)(2,1)S(1)} %add_convert_fusion.2.refs_2_), channel_id=1, source_target_pairs={{0,96},{32,0},{64,32},{96,64},{1,97},{33,1},{65,33},{97,65},{2,98}... | collective-permute-start | bytes 2752520 | tf_op jit(solution)/shard_map/ppermute | solution.py:129
  130.2 13.5 %collective-permute-done.9.refs_2_ = bf16[512,896]{1,0:T(8,128)(2,1)S(1)} collective-permute-done((bf16[512,896]{1,0:T(8,128)(2,1)S(1)}, bf16[512,896]{1,0:T(8,128)(2,1)S(1)}, u32[]{:S(2)}, u32[]{:S(2)}) %collective-permute-start.9) | collective-permute-done | bytes 917536 | tf_op jit(solution)/shard_map/ppermute | solution.py:132
  143.8 2.6 %collective-permute-start.17 = (bf16[512,256]{1,0:T(8,128)(2,1)}, bf16[512,256]{1,0:T(8,128)(2,1)}, u32[]{:S(2)}, u32[]{:S(2)}) collective-permute-start(bf16[512,256]{1,0:T(8,128)(2,1)} %slice.41), channel_id=1, source_target_pairs={{0,96},{32,0},{64,32},{96,64},{1,97},{33,1},{65,33},{97,65},{2,98}... | collective-permute-start | bytes 786440 | tf_op jit(solution)/shard_map/ppermute | solution.py:129
  151.9 3.9 %collective-permute-done.18.refs_3_ = bf16[128,128]{1,0:T(8,128)(2,1)S(1)} collective-permute-done((bf16[128,128]{1,0:T(8,128)(2,1)S(1)}, bf16[128,128]{1,0:T(8,128)(2,1)S(1)}, u32[]{:S(2)}, u32[]{:S(2)}) %collective-permute-start.18) | collective-permute-done | bytes 32800 | tf_op jit(solution)/shard_map/ppermute | solution.py:129
  157.6 2.3 %collective-permute-start.10 = (bf16[512,128]{1,0:T(8,128)(2,1)}, bf16[512,128]{1,0:T(8,128)(2,1)}, u32[]{:S(2)}, u32[]{:S(2)}) collective-permute-start(bf16[512,128]{1,0:T(8,128)(2,1)} %get-tuple-element.32), channel_id=1, source_target_pairs={{0,96},{32,0},{64,32},{96,64},{1,97},{33,1},{65,33},{97,65},{2,98}... | collective-permute-start | bytes 393224 | tf_op jit(solution)/shard_map/ppermute | solution.py:129
  159.9 2.5 %shard_map.103 = (bf16[896,4096]{1,0:T(8,128)(2,1)}, bf16[896,4096]{1,0:T(8,128)(2,1)}) custom-call(bf16[512,896]{1,0:T(8,128)(2,1)S(1)} %add_convert_fusion.refs_0_, bf16[512,896]{1,0:T(8,128)(2,1)S(1)} %add_convert_fusion.3.refs_1_), custom_call_target="tpu_custom_call" | custom-call | bytes 3670016 | tf_op jit(solution)/shard_map/pallas_call | solution.py:81
  168.2 3.4 %shard_map.104 = (bf16[896,4096]{1,0:T(8,128)(2,1)}, bf16[896,4096]{1,0:T(8,128)(2,1)}) custom-call(bf16[512,896]{1,0:T(8,128)(2,1)S(1)} %copy-done.4, bf16[512,896]{1,0:T(8,128)(2,1)S(1)} %copy-done.2, bf16[512,896]{1,0:T(8,128)(2,1)S(1)} %copy-done.6, bf16[896,4096]{1,0:T(8,128)(2,1)} %get-tuple-element.17.refs_3_, ...), custom_call_target="tpu_custom_call", output_to_operand_aliasing={{0}: (3, {}), {1}: (4, {})} | custom-call | bytes 5505024 | tf_op jit(solution)/shard_map/pallas_call | solution.py:81
  171.6 3.7 %shard_map.105 = (bf16[896,4096]{1,0:T(8,128)(2,1)}, bf16[896,4096]{1,0:T(8,128)(2,1)}) custom-call(bf16[512,896]{1,0:T(8,128)(2,1)S(1)} %collective-permute-done.4.refs_0_, bf16[512,896]{1,0:T(8,128)(2,1)} %collective-permute-done.23.refs_1_, bf16[512,896]{1,0:T(8,128)(2,1)} %collective-permute-done.24.refs_2_, ...), custom_call_target="tpu_custom_call", output_to_operand_aliasing={{0}: (3, {}), {1}: (4, {})} | custom-call | bytes 5505024 | tf_op jit(solution)/shard_map/pallas_call | solution.py:81
  175.4 3.4 %shard_map.106 = (bf16[896,4096]{1,0:T(8,128)(2,1)}, bf16[896,4096]{1,0:T(8,128)(2,1)}) custom-call(bf16[512,896]{1,0:T(8,128)(2,1)S(1)} %copy-done.8, bf16[512,896]{1,0:T(8,128)(2,1)S(1)} %copy-done.10, bf16[512,896]{1,0:T(8,128)(2,1)S(1)} %copy-done.12, bf16[896,4096]{1,0:T(8,128)(2,1)} %get-tuple-element.21.refs_3_, ...), custom_call_target="tpu_custom_call", output_to_operand_aliasing={{0}: (3, {}), {1}: (4, {})} | custom-call | bytes 5505024 | tf_op jit(solution)/shard_map/pallas_call | solution.py:81
  178.9 3.8 %shard_map.107 = (bf16[896,4096]{1,0:T(8,128)(2,1)}, bf16[896,4096]{1,0:T(8,128)(2,1)}) custom-call(bf16[512,512]{1,0:T(8,128)(2,1)S(1)} %collective-permute-done.12.refs_0_, bf16[512,128]{1,0:T(8,128)(2,1)S(1)} %collective-permute-done.5.refs_1_, bf16[512,256]{1,0:T(8,128)(2,1)S(1)} %copy-done.20, ...), custom_call_target="tpu_custom_call", output_to_operand_aliasing={{0}: (5, {}), {1}: (6, {})} | custom-call | bytes 5505024 | tf_op jit(solution)/shard_map/pallas_call | solution.py:81
  182.7 2.7 %shard_map.108 = (bf16[896,4096]{1,0:T(8,128)(2,1)}, bf16[896,4096]{1,0:T(8,128)(2,1)}) custom-call(bf16[512,512]{1,0:T(8,128)(2,1)} %collective-permute-done.11.refs_0_, bf16[512,512]{1,0:T(8,128)(2,1)S(1)} %copy-done.18, bf16[512,256]{1,0:T(8,128)(2,1)} %collective-permute-done.17.refs_2_, ...), custom_call_target="tpu_custom_call", output_to_operand_aliasing={{0}: (5, {}), {1}: (6, {})} | custom-call | bytes 2949120 | tf_op jit(solution)/shard_map/pallas_call | solution.py:81
  185.4 1.8 shard_map.109
  (123 shorter events, 45.0 us)
Async XLA Ops:
  6.1 70.2 %collective-permute-start.14 = (bf16[512,896]{1,0:T(8,128)(2,1)}, bf16[512,896]{1,0:T(8,128)(2,1)}, u32[]{:S(2)}, u32[]{:S(2)}) collective-permute-start(bf16[512,896]{1,0:T(8,128)(2,1)} %param.8), channel_id=1, source_target_pairs={{0,16},{16,0},{1,17},{17,1},{2,18},{18,2},{3,19},{19,3},{4,20},{20... | collective-permute-start | bytes 2752520 | tf_op jit(solution)/shard_map/ppermute | solution.py:132
  10.0 17.7 %collective-permute-start.28 = (bf16[4,32]{1,0:T(4,128)(2,1)S(1)}, bf16[4,32]{1,0:T(4,128)(2,1)S(1)}, u32[]{:S(2)}, u32[]{:S(2)}) collective-permute-start(bf16[4,32]{1,0:T(4,128)(2,1)S(1)} %select_select_fusion), channel_id=1, source_target_pairs={{0,16},{16,0},{1,17},{17,1},{2,18},{18,2},{3,19},{19,3},{4,20},{20... | collective-permute-start | bytes 776 | tf_op jit(solution)/shard_map/ppermute | solution.py:100
  30.8 48.1 %collective-permute-start = (bf16[512,896]{1,0:T(8,128)(2,1)}, bf16[512,896]{1,0:T(8,128)(2,1)}, u32[]{:S(2)}, u32[]{:S(2)}) collective-permute-start(bf16[512,896]{1,0:T(8,128)(2,1)} %param.8), channel_id=1, source_target_pairs={{0,32},{32,64},{64,96},{96,0},{1,33},{33,65},{65,97},{97,1},{2,34}... | collective-permute-start | bytes 2752520 | tf_op jit(solution)/shard_map/ppermute | solution.py:126
  38.1 41.5 %collective-permute-start.4 = (bf16[512,896]{1,0:T(8,128)(2,1)S(1)}, bf16[512,896]{1,0:T(8,128)(2,1)S(1)}, u32[]{:S(2)}, u32[]{:S(2)}) collective-permute-start(bf16[512,896]{1,0:T(8,128)(2,1)S(1)} %add_convert_fusion.3.refs_1_), channel_id=1, source_target_pairs={{0,32},{32,64},{64,96},{96,0},{1,33},{33,65},{65,97},{97,1},{2,34}... | collective-permute-start | bytes 2752520 | tf_op jit(solution)/shard_map/ppermute | solution.py:126
  41.5 33.2 %collective-permute-start.1 = (bf16[32,512]{1,0:T(8,128)(2,1)S(1)}, bf16[32,512]{1,0:T(8,128)(2,1)S(1)}, u32[]{:S(2)}, u32[]{:S(2)}) collective-permute-start(bf16[32,512]{1,0:T(8,128)(2,1)S(1)} %bitcast.17), channel_id=1, source_target_pairs={{0,32},{32,64},{64,96},{96,0},{1,33},{33,65},{65,97},{97,1},{2,34}... | collective-permute-start | bytes 98312 | tf_op jit(solution)/shard_map/ppermute | solution.py:126
  44.0 56.9 %collective-permute-start.7 = (bf16[512,896]{1,0:T(8,128)(2,1)}, bf16[512,896]{1,0:T(8,128)(2,1)}, u32[]{:S(2)}, u32[]{:S(2)}) collective-permute-start(bf16[512,896]{1,0:T(8,128)(2,1)} %param.11), channel_id=1, source_target_pairs={{0,96},{32,0},{64,32},{96,64},{1,97},{33,1},{65,33},{97,65},{2,98}... | collective-permute-start | bytes 2752520 | tf_op jit(solution)/shard_map/ppermute | solution.py:129
  74.8 26.6 %collective-permute-start.23 = (bf16[512,896]{1,0:T(8,128)(2,1)S(1)}, bf16[512,896]{1,0:T(8,128)(2,1)}, u32[]{:S(2)}, u32[]{:S(2)}) collective-permute-start(bf16[512,896]{1,0:T(8,128)(2,1)S(1)} %add_convert_fusion.3.refs_1_), channel_id=1, source_target_pairs={{0,16},{16,0},{1,17},{17,1},{2,18},{18,2},{3,19},{19,3},{4,20},{20... | collective-permute-start | bytes 2752520 | tf_op jit(solution)/shard_map/ppermute | solution.py:132
  76.3 26.6 %collective-permute-start.24 = (bf16[512,896]{1,0:T(8,128)(2,1)S(1)}, bf16[512,896]{1,0:T(8,128)(2,1)}, u32[]{:S(2)}, u32[]{:S(2)}) collective-permute-start(bf16[512,896]{1,0:T(8,128)(2,1)S(1)} %add_convert_fusion.refs_0_), channel_id=1, source_target_pairs={{0,96},{32,0},{64,32},{96,64},{1,97},{33,1},{65,33},{97,65},{2,98}... | collective-permute-start | bytes 2752520 | tf_op jit(solution)/shard_map/ppermute | solution.py:129
  79.0 21.2 %collective-permute-start.8 = (bf16[32,512]{1,0:T(8,128)(2,1)S(1)}, bf16[32,512]{1,0:T(8,128)(2,1)S(1)}, u32[]{:S(2)}, u32[]{:S(2)}) collective-permute-start(bf16[32,512]{1,0:T(8,128)(2,1)S(1)} %bitcast.18), channel_id=1, source_target_pairs={{0,96},{32,0},{64,32},{96,64},{1,97},{33,1},{65,33},{97,65},{2,98}... | collective-permute-start | bytes 98312 | tf_op jit(solution)/shard_map/ppermute | solution.py:129
  84.5 44.4 %collective-permute-start.16 = (bf16[512,896]{1,0:T(8,128)(2,1)S(1)}, bf16[512,896]{1,0:T(8,128)(2,1)S(1)}, u32[]{:S(2)}, u32[]{:S(2)}) collective-permute-start(bf16[512,896]{1,0:T(8,128)(2,1)S(1)} %add_convert_fusion.1.refs_1_), channel_id=1, source_target_pairs={{0,96},{32,0},{64,32},{96,64},{1,97},{33,1},{65,33},{97,65},{2,98}... | collective-permute-start | bytes 2752520 | tf_op jit(solution)/shard_map/ppermute | solution.py:129
  100.2 27.9 %collective-permute-start.2 = (bf16[512,896]{1,0:T(8,128)(2,1)S(1)}, bf16[512,896]{1,0:T(8,128)(2,1)S(1)}, u32[]{:S(2)}, u32[]{:S(2)}) collective-permute-start(bf16[512,896]{1,0:T(8,128)(2,1)S(1)} %add_convert_fusion.4.refs_0_), channel_id=1, source_target_pairs={{0,32},{32,64},{64,96},{96,0},{1,33},{33,65},{65,97},{97,1},{2,34}... | collective-permute-start | bytes 2752520 | tf_op jit(solution)/shard_map/ppermute | solution.py:126
  100.9 24.2 %collective-permute-start.12 = (bf16[512,512]{1,0:T(8,128)(2,1)S(1)}, bf16[512,512]{1,0:T(8,128)(2,1)S(1)}, u32[]{:S(2)}, u32[]{:S(2)}) collective-permute-start(bf16[512,512]{1,0:T(8,128)(2,1)S(1)} %slice.40), channel_id=1, source_target_pairs={{0,16},{16,0},{1,17},{17,1},{2,18},{18,2},{3,19},{19,3},{4,20},{20... | collective-permute-start | bytes 1572872 | tf_op jit(solution)/shard_map/ppermute | solution.py:132
  101.4 17.1 %collective-permute-start.5 = (bf16[512,128]{1,0:T(8,128)(2,1)S(1)}, bf16[512,128]{1,0:T(8,128)(2,1)S(1)}, u32[]{:S(2)}, u32[]{:S(2)}) collective-permute-start(bf16[512,128]{1,0:T(8,128)(2,1)S(1)} %slice.37), channel_id=1, source_target_pairs={{0,16},{16,0},{1,17},{17,1},{2,18},{18,2},{3,19},{19,3},{4,20},{20... | collective-permute-start | bytes 393224 | tf_op jit(solution)/shard_map/ppermute | solution.py:132
  102.9 21.2 %collective-permute-start.20 = (bf16[512,256]{1,0:T(8,128)(2,1)S(1)}, bf16[512,256]{1,0:T(8,128)(2,1)S(1)}, u32[]{:S(2)}, u32[]{:S(2)}) collective-permute-start(bf16[512,256]{1,0:T(8,128)(2,1)S(1)} %slice.44), channel_id=1, source_target_pairs={{0,16},{16,0},{1,17},{17,1},{2,18},{18,2},{3,19},{19,3},{4,20},{20... | collective-permute-start | bytes 786440 | tf_op jit(solution)/shard_map/ppermute | solution.py:132
  118.5 25.3 %collective-permute-start.9 = (bf16[512,896]{1,0:T(8,128)(2,1)S(1)}, bf16[512,896]{1,0:T(8,128)(2,1)S(1)}, u32[]{:S(2)}, u32[]{:S(2)}) collective-permute-start(bf16[512,896]{1,0:T(8,128)(2,1)S(1)} %add_convert_fusion.2.refs_2_), channel_id=1, source_target_pairs={{0,16},{16,0},{1,17},{17,1},{2,18},{18,2},{3,19},{19,3},{4,20},{20... | collective-permute-start | bytes 2752520 | tf_op jit(solution)/shard_map/ppermute | solution.py:132
  124.8 23.2 %collective-permute-start.21 = (bf16[512,896]{1,0:T(8,128)(2,1)S(1)}, bf16[512,896]{1,0:T(8,128)(2,1)S(1)}, u32[]{:S(2)}, u32[]{:S(2)}) collective-permute-start(bf16[512,896]{1,0:T(8,128)(2,1)S(1)} %add_convert_fusion.1.refs_1_), channel_id=1, source_target_pairs={{0,32},{32,64},{64,96},{96,0},{1,33},{33,65},{65,97},{97,1},{2,34}... | collective-permute-start | bytes 2752520 | tf_op jit(solution)/shard_map/ppermute | solution.py:126
  125.1 25.9 %collective-permute-start.22 = (bf16[512,896]{1,0:T(8,128)(2,1)S(1)}, bf16[512,896]{1,0:T(8,128)(2,1)S(1)}, u32[]{:S(2)}, u32[]{:S(2)}) collective-permute-start(bf16[512,896]{1,0:T(8,128)(2,1)S(1)} %add_convert_fusion.2.refs_2_), channel_id=1, source_target_pairs={{0,96},{32,0},{64,32},{96,64},{1,97},{33,1},{65,33},{97,65},{2,98}... | collective-permute-start | bytes 2752520 | tf_op jit(solution)/shard_map/ppermute | solution.py:129
  128.0 28.8 %collective-permute-start.13 = (bf16[512,512]{1,0:T(8,128)(2,1)S(1)}, bf16[512,512]{1,0:T(8,128)(2,1)S(1)}, u32[]{:S(2)}, u32[]{:S(2)}) collective-permute-start(bf16[512,512]{1,0:T(8,128)(2,1)S(1)} %collective-permute-done.12.refs_0_), channel_id=1, source_target_pairs={{0,32},{32,64},{64,96},{96,0},{1,33},{33,65},{65,97},{97,1},{2,34}... | collective-permute-start | bytes 1572872 | tf_op jit(solution)/shard_map/ppermute | solution.py:126
  129.0 53.7 %collective-permute-start.11 = (bf16[512,512]{1,0:T(8,128)(2,1)}, bf16[512,512]{1,0:T(8,128)(2,1)}, u32[]{:S(2)}, u32[]{:S(2)}) collective-permute-start(bf16[512,512]{1,0:T(8,128)(2,1)} %slice.39), channel_id=1, source_target_pairs={{0,16},{16,0},{1,17},{17,1},{2,18},{18,2},{3,19},{19,3},{4,20},{20... | collective-permute-start | bytes 1572872 | tf_op jit(solution)/shard_map/ppermute | solution.py:132
  143.8 38.9 %collective-permute-start.17 = (bf16[512,256]{1,0:T(8,128)(2,1)}, bf16[512,256]{1,0:T(8,128)(2,1)}, u32[]{:S(2)}, u32[]{:S(2)}) collective-permute-start(bf16[512,256]{1,0:T(8,128)(2,1)} %slice.41), channel_id=1, source_target_pairs={{0,96},{32,0},{64,32},{96,64},{1,97},{33,1},{65,33},{97,65},{2,98}... | collective-permute-start | bytes 786440 | tf_op jit(solution)/shard_map/ppermute | solution.py:129
  149.0 14.3 %collective-permute-start.19 = (bf16[512,128]{1,0:T(8,128)(2,1)}, bf16[512,128]{1,0:T(8,128)(2,1)}, u32[]{:S(2)}, u32[]{:S(2)}) collective-permute-start(bf16[512,128]{1,0:T(8,128)(2,1)} %get-tuple-element.31), channel_id=1, source_target_pairs={{0,96},{32,0},{64,32},{96,64},{1,97},{33,1},{65,33},{97,65},{2,98}... | collective-permute-start | bytes 393224 | tf_op jit(solution)/shard_map/ppermute | solution.py:129
  155.8 29.6 %collective-permute-start.6 = (bf16[512,128]{1,0:T(8,128)(2,1)S(1)}, bf16[512,128]{1,0:T(8,128)(2,1)}, u32[]{:S(2)}, u32[]{:S(2)}) collective-permute-start(bf16[512,128]{1,0:T(8,128)(2,1)S(1)} %collective-permute-done.5.refs_1_), channel_id=1, source_target_pairs={{0,32},{32,64},{64,96},{96,0},{1,33},{33,65},{65,97},{97,1},{2,34}... | collective-permute-start | bytes 393224 | tf_op jit(solution)/shard_map/ppermute | solution.py:126
  157.6 27.8 %collective-permute-start.10 = (bf16[512,128]{1,0:T(8,128)(2,1)}, bf16[512,128]{1,0:T(8,128)(2,1)}, u32[]{:S(2)}, u32[]{:S(2)}) collective-permute-start(bf16[512,128]{1,0:T(8,128)(2,1)} %get-tuple-element.32), channel_id=1, source_target_pairs={{0,96},{32,0},{64,32},{96,64},{1,97},{33,1},{65,33},{97,65},{2,98}... | collective-permute-start | bytes 393224 | tf_op jit(solution)/shard_map/ppermute | solution.py:129
  163.3 22.1 %collective-permute-start.3 = (bf16[384,128]{1,0:T(8,128)(2,1)S(1)}, bf16[384,128]{1,0:T(8,128)(2,1)S(1)}, u32[]{:S(2)}, u32[]{:S(2)}) collective-permute-start(bf16[384,128]{1,0:T(8,128)(2,1)S(1)} %slice.36), channel_id=1, source_target_pairs={{0,16},{16,0},{1,17},{17,1},{2,18},{18,2},{3,19},{19,3},{4,20},{20... | collective-permute-start | bytes 294920 | tf_op jit(solution)/shard_map/ppermute | solution.py:132
  (34 other events, 362.9 us)

commit v3 on v2

--- a/solution.py
+++ b/solution.py
@@ -143,13 +143,14 @@
     u_p = merged(raw_u_p, low_u_p, high_up)
     u_m, u_x, g_p = up(u), across(u), down(g)
     g_f, cg_p, cu_p = up(g_m), down(g_x), across(u_p)
-    near, mid, late = width * 4 // 7, width * 5 // 7, width * 6 // 7
+    first, near, mid, late = width * 2 // 7, width * 4 // 7, width * 5 // 7, width * 6 // 7
     cu_m0, cu_m1, cu_m2 = (across(u_m[:, :near]), across(u_m[:, near:mid]), across(u_m[:, mid:]))
     cg_m, u_f = up(g_x), down(u_p)
-    cg_f0, cg_f1 = across(g_f[:, :near]), across(g_f[LANES:, near:mid])
+    cg_f0, cg_f4, cg_f1 = (across(g_f[:, :first]), across(g_f[:, first:near]), across(g_f[LANES:, near:mid]))
     cg_f2, cg_f3 = down(cg_p[:, mid:]), down(cg_p[:LANES, near:mid])
     cu_f2, cu_f3 = down(cu_p[:, mid:late]), down(cu_p[:, late:])
-    cu_f0, cu_f1 = up(cu_m0), up(cu_m1)
+    cu_f4 = down(cu_p[:LANES, near:mid])
+    cu_f0, cu_f1 = up(cu_m0), up(cu_m1[LANES:])
 
     out = jax.ShapeDtypeStruct((width, rows * 8), jnp.bfloat16)
     outs = place((out, out), [(g, 0, 0, 0, 0), (u, 1, 0, 0, 0)])
@@ -166,21 +167,10 @@
             (u_f, 1, 0, 2, 0),
         ],
     )
+    outs = place(outs, [(cg_f2, 0, mid, 2, 1), (cg_f3, 0, near, 2, 1), (cu_f4, 1, near, 2, 1), (cg_f0, 0, 0, 2, 1)], held=True)
+    outs = place(outs, [(cg_f4, 0, first, 2, 1), (cu_f0, 1, 0, 2, 1), (cu_f2, 1, mid, 2, 1)], held=True)
     outs = place(
-        outs,
-        [
-            (cg_f0, 0, 0, 2, 1),
-            (cu_f0, 1, 0, 2, 1),
-            (cg_f2, 0, mid, 2, 1),
-            (cg_f3, 0, near, 2, 1),
-            (cu_f2, 1, mid, 2, 1),
-        ],
-        held=True,
-    )
-    outs = place(
-        outs,
-        [(cg_f1, 0, near, 2, 1, LANES), (cu_f1, 1, near, 2, 1), (cu_f3, 1, late, 2, 1)],
-        held=True,
+        outs, [(cg_f1, 0, near, 2, 1, LANES), (cu_f1, 1, near, 2, 1, LANES), (cu_f3, 1, late, 2, 1)], held=True
     )
     return (*outs, gathered_gain(gain))
 

time: 188 us -> 174 us (0.926)
  the two profiles are of different devices: /device:TPU:0 before, /device:TPU:2 now
where the time goes in v3:
time: 174 us; the launch traced here: 173 us
  waiting for transfers between devices  80.4 us (46%)
  starting transfers between devices  47.6 us (27%)
  Pallas kernels  22.7 us (13%)
  local copies, waits for them, and re-layouts  14 us (8%)
  matrix products  5.7 us (3%)
    ppermute x10, waiting for transfers between devices, down(): return lax.ppermute(v, 'y', DOWN)  25.6 us
    ppermute x7, waiting for transfers between devices, up(): return lax.ppermute(v, 'y', UP)  23.8 us
    pallas_call x8, Pallas kernels, place(): pl.pallas_call(kernel, out_shape=shapes, in_specs=[pl.BlockSpec(memory_sp...  22.7 us
    ppermute x5, waiting for transfers between devices, doubled(): other = lax.ppermute(x, axis, pairs)  20.6 us
    ppermute x10, starting transfers between devices, down(): return lax.ppermute(v, 'y', DOWN)  16.8 us
    ppermute x10, starting transfers between devices, across(): return lax.ppermute(v, 'xl', SWAP)  12.1 us
    unnamed x52, local copies, waits for them, and re-layouts  8.78 us
    ppermute x5, starting transfers between devices, doubled(): other = lax.ppermute(x, axis, pairs)  8.08 us
  transfers between devices with their start and end apart: 35, of which 14 were waited for; matrix products, arithmetic and copies ran while one was open for 7% of the time, Pallas kernels for 12%

profile of v3, /device:TPU:2, one launch (start us, length us, event | category | flops | bytes accessed | tf_op | source)
XLA Modules:
  0.0 173.2 jit_solution(599978995651576857)
XLA Ops:
  1.4 3.0 %collective-permute-start.27 = (bf16[32]{0:T(256)(128)(2,1)S(1)}, bf16[32]{0:T(256)(128)(2,1)S(1)}, u32[]{:S(2)}, u32[]{:S(2)}) collective-permute-start(bf16[32]{0:T(256)(128)(2,1)S(1)} %add_convert_fusion.5), channel_id=1, source_target_pairs={{0,96},{32,0},{64,32},{96,64},{1,97},{33,1},{65,33},{97,65},{2,98}... | collective-permute-start | bytes 200 | tf_op jit(solution)/shard_map/ppermute | solution.py:110
  6.5 2.9 %collective-permute-done.28 = bf16[32]{0:T(256)(128)(2,1)S(1)} collective-permute-done((bf16[32]{0:T(256)(128)(2,1)S(1)}, bf16[32]{0:T(256)(128)(2,1)S(1)}, u32[]{:S(2)}, u32[]{:S(2)}) %collective-permute-start.28) | collective-permute-done | bytes 96 | tf_op jit(solution)/shard_map/ppermute | solution.py:110
  10.4 17.1 %collective-permute-done.30 = bf16[4,32]{1,0:T(4,128)(2,1)S(1)} collective-permute-done((bf16[4,32]{1,0:T(4,128)(2,1)S(1)}, bf16[4,32]{1,0:T(4,128)(2,1)S(1)}, u32[]{:S(2)}, u32[]{:S(2)}) %collective-permute-start.30) | collective-permute-done | bytes 288 | tf_op jit(solution)/shard_map/ppermute | solution.py:100
  29.3 2.0 %collective-permute-start.4 = (bf16[512,896]{1,0:T(8,128)(2,1)S(1)}, bf16[512,896]{1,0:T(8,128)(2,1)S(1)}, u32[]{:S(2)}, u32[]{:S(2)}) collective-permute-start(bf16[512,896]{1,0:T(8,128)(2,1)S(1)} %add_convert_fusion.3.refs_1_), channel_id=1, source_target_pairs={{0,32},{32,64},{64,96},{96,0},{1,33},{33,65},{65,97},{97,1},{2,34}... | collective-permute-start | bytes 2752520 | tf_op jit(solution)/shard_map/ppermute | solution.py:126
  31.2 2.0 %collective-permute-start.32 = (bf16[16,32]{1,0:T(8,128)(2,1)S(1)}, bf16[16,32]{1,0:T(8,128)(2,1)S(1)}, u32[]{:S(2)}, u32[]{:S(2)}) collective-permute-start(bf16[16,32]{1,0:T(8,128)(2,1)S(1)} %maximum_select_fusion.3), channel_id=1, source_target_pairs={{0,4},{1,5},{2,6},{3,7},{4,0},{5,1},{6,2},{7,3},{8,12},{9,13},{10,... | collective-permute-start | bytes 3080 | tf_op jit(solution)/shard_map/ppermute | solution.py:100
  34.9 3.9 %collective-permute-start.33 = (bf16[32,32]{1,0:T(8,128)(2,1)S(1)}, bf16[32,32]{1,0:T(8,128)(2,1)S(1)}, u32[]{:S(2)}, u32[]{:S(2)}) collective-permute-start(bf16[32,32]{1,0:T(8,128)(2,1)S(1)} %maximum_select_fusion.2), channel_id=1, source_target_pairs={{0,8},{1,9},{2,10},{3,11},{4,12},{5,13},{6,14},{7,15},{8,0},{9,1},... | collective-permute-start | bytes 6152 | tf_op jit(solution)/shard_map/ppermute | solution.py:100
  44.3 2.8 %collective-permute-start.8 = (bf16[32,512]{1,0:T(8,128)(2,1)}, bf16[32,512]{1,0:T(8,128)(2,1)S(1)}, u32[]{:S(2)}, u32[]{:S(2)}) collective-permute-start(bf16[32,512]{1,0:T(8,128)(2,1)} %bitcast.16), channel_id=1, source_target_pairs={{0,96},{32,0},{64,32},{96,64},{1,97},{33,1},{65,33},{97,65},{2,98}... | collective-permute-start | bytes 98312 | tf_op jit(solution)/shard_map/ppermute | solution.py:129
  56.1 17.6 %collective-permute-done.1 = bf16[32,512]{1,0:T(8,128)(2,1)S(1)} collective-permute-done((bf16[32,512]{1,0:T(8,128)(2,1)}, bf16[32,512]{1,0:T(8,128)(2,1)S(1)}, u32[]{:S(2)}, u32[]{:S(2)}) %collective-permute-start.1) | collective-permute-done | bytes 32800 | tf_op jit(solution)/shard_map/ppermute | solution.py:126
  79.3 12.6 %collective-permute-done.26.refs_2_ = bf16[512,896]{1,0:T(8,128)(2,1)S(1)} collective-permute-done((bf16[512,896]{1,0:T(8,128)(2,1)S(1)}, bf16[512,896]{1,0:T(8,128)(2,1)S(1)}, u32[]{:S(2)}, u32[]{:S(2)}) %collective-permute-start.26) | collective-permute-done | bytes 917536 | tf_op jit(solution)/shard_map/ppermute | solution.py:129
  94.4 6.6 %collective-permute-done.22.refs_2_ = bf16[512,256]{1,0:T(8,128)(2,1)S(1)} collective-permute-done((bf16[512,256]{1,0:T(8,128)(2,1)S(1)}, bf16[512,256]{1,0:T(8,128)(2,1)S(1)}, u32[]{:S(2)}, u32[]{:S(2)}) %collective-permute-start.22) | collective-permute-done | bytes 262176 | tf_op jit(solution)/shard_map/ppermute | solution.py:132
  101.8 3.2 %collective-permute-start.24 = (bf16[512,896]{1,0:T(8,128)(2,1)S(1)}, bf16[512,896]{1,0:T(8,128)(2,1)S(1)}, u32[]{:S(2)}, u32[]{:S(2)}) collective-permute-start(bf16[512,896]{1,0:T(8,128)(2,1)S(1)} %add_convert_fusion.2.refs_2_), channel_id=1, source_target_pairs={{0,96},{32,0},{64,32},{96,64},{1,97},{33,1},{65,33},{97,65},{2,98}... | collective-permute-start | bytes 2752520 | tf_op jit(solution)/shard_map/ppermute | solution.py:129
  105.0 6.5 %collective-permute-done.17.refs_1_ = bf16[512,896]{1,0:T(8,128)(2,1)S(1)} collective-permute-done((bf16[512,896]{1,0:T(8,128)(2,1)S(1)}, bf16[512,896]{1,0:T(8,128)(2,1)S(1)}, u32[]{:S(2)}, u32[]{:S(2)}) %collective-permute-start.17) | collective-permute-done | bytes 917536 | tf_op jit(solution)/shard_map/ppermute | solution.py:129
  111.6 3.3 %collective-permute-start.19 = (bf16[128,128]{1,0:T(8,128)(2,1)S(1)}, bf16[128,128]{1,0:T(8,128)(2,1)S(1)}, u32[]{:S(2)}, u32[]{:S(2)}) collective-permute-start(bf16[128,128]{1,0:T(8,128)(2,1)S(1)} %slice.56), channel_id=1, source_target_pairs={{0,96},{32,0},{64,32},{96,64},{1,97},{33,1},{65,33},{97,65},{2,98}... | collective-permute-start | bytes 98312 | tf_op jit(solution)/shard_map/ppermute | solution.py:129
  118.1 5.5 %collective-permute-done.23.refs_3_ = bf16[512,896]{1,0:T(8,128)(2,1)S(1)} collective-permute-done((bf16[512,896]{1,0:T(8,128)(2,1)S(1)}, bf16[512,896]{1,0:T(8,128)(2,1)S(1)}, u32[]{:S(2)}, u32[]{:S(2)}) %collective-permute-start.23) | collective-permute-done | bytes 917536 | tf_op jit(solution)/shard_map/ppermute | solution.py:126
  124.6 6.5 %collective-permute-done.24.refs_4_ = bf16[512,896]{1,0:T(8,128)(2,1)S(1)} collective-permute-done((bf16[512,896]{1,0:T(8,128)(2,1)S(1)}, bf16[512,896]{1,0:T(8,128)(2,1)S(1)}, u32[]{:S(2)}, u32[]{:S(2)}) %collective-permute-start.24) | collective-permute-done | bytes 917536 | tf_op jit(solution)/shard_map/ppermute | solution.py:129
  137.5 2.0 %collective-permute-start.14 = (bf16[512,128]{1,0:T(8,128)(2,1)}, bf16[512,128]{1,0:T(8,128)(2,1)}, u32[]{:S(2)}, u32[]{:S(2)}) collective-permute-start(bf16[512,128]{1,0:T(8,128)(2,1)} %get-tuple-element.37), channel_id=1, source_target_pairs={{0,96},{32,0},{64,32},{96,64},{1,97},{33,1},{65,33},{97,65},{2,98}... | collective-permute-start | bytes 393224 | tf_op jit(solution)/shard_map/ppermute | solution.py:129
  140.3 2.5 %shard_map.103 = (bf16[896,4096]{1,0:T(8,128)(2,1)}, bf16[896,4096]{1,0:T(8,128)(2,1)}) custom-call(bf16[512,896]{1,0:T(8,128)(2,1)S(1)} %add_convert_fusion.refs_0_, bf16[512,896]{1,0:T(8,128)(2,1)S(1)} %add_convert_fusion.3.refs_1_), custom_call_target="tpu_custom_call" | custom-call | bytes 3670016 | tf_op jit(solution)/shard_map/pallas_call | solution.py:81
  144.9 2.0 %collective-permute-start.6 = (bf16[384,128]{1,0:T(8,128)(2,1)}, bf16[384,128]{1,0:T(8,128)(2,1)}, u32[]{:S(2)}, u32[]{:S(2)}) collective-permute-start(bf16[384,128]{1,0:T(8,128)(2,1)} %slice.50), channel_id=1, source_target_pairs={{0,32},{32,64},{64,96},{96,0},{1,33},{33,65},{65,97},{97,1},{2,34}... | collective-permute-start | bytes 294920 | tf_op jit(solution)/shard_map/ppermute | solution.py:126
  152.6 3.4 %shard_map.104 = (bf16[896,4096]{1,0:T(8,128)(2,1)}, bf16[896,4096]{1,0:T(8,128)(2,1)}) custom-call(bf16[512,896]{1,0:T(8,128)(2,1)S(1)} %copy-done.2, bf16[512,896]{1,0:T(8,128)(2,1)S(1)} %add_convert_fusion.1.refs_1_, bf16[512,896]{1,0:T(8,128)(2,1)S(1)} %copy-done.4, ...), custom_call_target="tpu_custom_call", output_to_operand_aliasing={{0}: (3, {}), {1}: (4, {})} | custom-call | bytes 5505024 | tf_op jit(solution)/shard_map/pallas_call | solution.py:81
  156.1 3.4 %shard_map.105 = (bf16[896,4096]{1,0:T(8,128)(2,1)}, bf16[896,4096]{1,0:T(8,128)(2,1)}) custom-call(bf16[512,896]{1,0:T(8,128)(2,1)S(1)} %collective-permute-done.4.refs_0_, bf16[512,896]{1,0:T(8,128)(2,1)S(1)} %copy-done.12, bf16[512,896]{1,0:T(8,128)(2,1)S(1)} %copy-done.14, ...), custom_call_target="tpu_custom_call", output_to_operand_aliasing={{0}: (3, {}), {1}: (4, {})} | custom-call | bytes 5505024 | tf_op jit(solution)/shard_map/pallas_call | solution.py:81
  159.6 3.4 %shard_map.106 = (bf16[896,4096]{1,0:T(8,128)(2,1)}, bf16[896,4096]{1,0:T(8,128)(2,1)}) custom-call(bf16[512,896]{1,0:T(8,128)(2,1)S(1)} %copy-done.6, bf16[512,896]{1,0:T(8,128)(2,1)S(1)} %copy-done.8, bf16[512,896]{1,0:T(8,128)(2,1)S(1)} %copy-done.10, bf16[896,4096]{1,0:T(8,128)(2,1)} %get-tuple-element.23.refs_3_, ...), custom_call_target="tpu_custom_call", output_to_operand_aliasing={{0}: (3, {}), {1}: (4, {})} | custom-call | bytes 5505024 | tf_op jit(solution)/shard_map/pallas_call | solution.py:81
  163.0 3.8 %shard_map.107 = (bf16[896,4096]{1,0:T(8,128)(2,1)}, bf16[896,4096]{1,0:T(8,128)(2,1)}) custom-call(bf16[512,512]{1,0:T(8,128)(2,1)S(1)} %collective-permute-done.12.refs_0_, bf16[512,128]{1,0:T(8,128)(2,1)S(1)} %collective-permute-done.5.refs_1_, bf16[512,256]{1,0:T(8,128)(2,1)S(1)} %copy-done.22, ...), custom_call_target="tpu_custom_call", output_to_operand_aliasing={{0}: (5, {}), {1}: (6, {})} | custom-call | bytes 5505024 | tf_op jit(solution)/shard_map/pallas_call | solution.py:81
  166.8 2.1 %shard_map.108 = (bf16[896,4096]{1,0:T(8,128)(2,1)}, bf16[896,4096]{1,0:T(8,128)(2,1)}) custom-call(bf16[512,256]{1,0:T(8,128)(2,1)} %collective-permute-done.18.refs_0_, bf16[128,128]{1,0:T(8,128)(2,1)S(1)} %collective-permute-done.19.refs_1_, bf16[128,128]{1,0:T(8,128)(2,1)S(1)} %collective-permute-done.20.refs_2_, ...), custom_call_target="tpu_custom_call", output_to_operand_aliasing={{0}: (4, {}), {1}: (5, {})} | custom-call | bytes 1179648 | tf_op jit(solution)/shard_map/pallas_call | solution.py:81
  169.0 2.2 %shard_map.109 = (bf16[896,4096]{1,0:T(8,128)(2,1)}, bf16[896,4096]{1,0:T(8,128)(2,1)}) custom-call(bf16[512,256]{1,0:T(8,128)(2,1)} %collective-permute-done.11.refs_0_, bf16[512,512]{1,0:T(8,128)(2,1)S(1)} %copy-done.20, bf16[512,128]{1,0:T(8,128)(2,1)} %collective-permute-done.14.refs_2_, ...), custom_call_target="tpu_custom_call", output_to_operand_aliasing={{0}: (3, {}), {1}: (4, {})} | custom-call | bytes 1835008 | tf_op jit(solution)/shard_map/pallas_call | solution.py:81
  (132 shorter events, 51.7 us)
Async XLA Ops:
  6.0 45.2 %collective-permute-start.15 = (bf16[512,896]{1,0:T(8,128)(2,1)}, bf16[512,896]{1,0:T(8,128)(2,1)S(1)}, u32[]{:S(2)}, u32[]{:S(2)}) collective-permute-start(bf16[512,896]{1,0:T(8,128)(2,1)} %param.8), channel_id=1, source_target_pairs={{0,16},{16,0},{1,17},{17,1},{2,18},{18,2},{3,19},{19,3},{4,20},{20... | collective-permute-start | bytes 2752520 | tf_op jit(solution)/shard_map/ppermute | solution.py:132
  9.9 17.6 %collective-permute-start.30 = (bf16[4,32]{1,0:T(4,128)(2,1)S(1)}, bf16[4,32]{1,0:T(4,128)(2,1)S(1)}, u32[]{:S(2)}, u32[]{:S(2)}) collective-permute-start(bf16[4,32]{1,0:T(4,128)(2,1)S(1)} %select_select_fusion), channel_id=1, source_target_pairs={{0,16},{16,0},{1,17},{17,1},{2,18},{18,2},{3,19},{19,3},{4,20},{20... | collective-permute-start | bytes 776 | tf_op jit(solution)/shard_map/ppermute | solution.py:100
  29.3 24.5 %collective-permute-start.4 = (bf16[512,896]{1,0:T(8,128)(2,1)S(1)}, bf16[512,896]{1,0:T(8,128)(2,1)S(1)}, u32[]{:S(2)}, u32[]{:S(2)}) collective-permute-start(bf16[512,896]{1,0:T(8,128)(2,1)S(1)} %add_convert_fusion.3.refs_1_), channel_id=1, source_target_pairs={{0,32},{32,64},{64,96},{96,0},{1,33},{33,65},{65,97},{97,1},{2,34}... | collective-permute-start | bytes 2752520 | tf_op jit(solution)/shard_map/ppermute | solution.py:126
  42.0 32.7 %collective-permute-start = (bf16[512,896]{1,0:T(8,128)(2,1)}, bf16[512,896]{1,0:T(8,128)(2,1)S(1)}, u32[]{:S(2)}, u32[]{:S(2)}) collective-permute-start(bf16[512,896]{1,0:T(8,128)(2,1)} %param.8), channel_id=1, source_target_pairs={{0,32},{32,64},{64,96},{96,0},{1,33},{33,65},{65,97},{97,1},{2,34}... | collective-permute-start | bytes 2752520 | tf_op jit(solution)/shard_map/ppermute | solution.py:126
  48.7 27.0 %collective-permute-start.7 = (bf16[512,896]{1,0:T(8,128)(2,1)}, bf16[512,896]{1,0:T(8,128)(2,1)S(1)}, u32[]{:S(2)}, u32[]{:S(2)}) collective-permute-start(bf16[512,896]{1,0:T(8,128)(2,1)} %param.11), channel_id=1, source_target_pairs={{0,96},{32,0},{64,32},{96,64},{1,97},{33,1},{65,33},{97,65},{2,98}... | collective-permute-start | bytes 2752520 | tf_op jit(solution)/shard_map/ppermute | solution.py:129
  49.4 27.4 %collective-permute-start.25 = (bf16[512,896]{1,0:T(8,128)(2,1)S(1)}, bf16[512,896]{1,0:T(8,128)(2,1)S(1)}, u32[]{:S(2)}, u32[]{:S(2)}) collective-permute-start(bf16[512,896]{1,0:T(8,128)(2,1)S(1)} %add_convert_fusion.3.refs_1_), channel_id=1, source_target_pairs={{0,16},{16,0},{1,17},{17,1},{2,18},{18,2},{3,19},{19,3},{4,20},{20... | collective-permute-start | bytes 2752520 | tf_op jit(solution)/shard_map/ppermute | solution.py:132
  51.2 40.7 %collective-permute-start.26 = (bf16[512,896]{1,0:T(8,128)(2,1)S(1)}, bf16[512,896]{1,0:T(8,128)(2,1)S(1)}, u32[]{:S(2)}, u32[]{:S(2)}) collective-permute-start(bf16[512,896]{1,0:T(8,128)(2,1)S(1)} %add_convert_fusion.refs_0_), channel_id=1, source_target_pairs={{0,96},{32,0},{64,32},{96,64},{1,97},{33,1},{65,33},{97,65},{2,98}... | collective-permute-start | bytes 2752520 | tf_op jit(solution)/shard_map/ppermute | solution.py:129
  53.8 19.9 %collective-permute-start.1 = (bf16[32,512]{1,0:T(8,128)(2,1)}, bf16[32,512]{1,0:T(8,128)(2,1)S(1)}, u32[]{:S(2)}, u32[]{:S(2)}) collective-permute-start(bf16[32,512]{1,0:T(8,128)(2,1)} %bitcast.18), channel_id=1, source_target_pairs={{0,32},{32,64},{64,96},{96,0},{1,33},{33,65},{65,97},{97,1},{2,34}... | collective-permute-start | bytes 98312 | tf_op jit(solution)/shard_map/ppermute | solution.py:126
  73.7 37.9 %collective-permute-start.17 = (bf16[512,896]{1,0:T(8,128)(2,1)S(1)}, bf16[512,896]{1,0:T(8,128)(2,1)S(1)}, u32[]{:S(2)}, u32[]{:S(2)}) collective-permute-start(bf16[512,896]{1,0:T(8,128)(2,1)S(1)} %add_convert_fusion.1.refs_1_), channel_id=1, source_target_pairs={{0,96},{32,0},{64,32},{96,64},{1,97},{33,1},{65,33},{97,65},{2,98}... | collective-permute-start | bytes 2752520 | tf_op jit(solution)/shard_map/ppermute | solution.py:129
  74.7 27.0 %collective-permute-start.12 = (bf16[512,512]{1,0:T(8,128)(2,1)S(1)}, bf16[512,512]{1,0:T(8,128)(2,1)S(1)}, u32[]{:S(2)}, u32[]{:S(2)}) collective-permute-start(bf16[512,512]{1,0:T(8,128)(2,1)S(1)} %slice.53), channel_id=1, source_target_pairs={{0,16},{16,0},{1,17},{17,1},{2,18},{18,2},{3,19},{19,3},{4,20},{20... | collective-permute-start | bytes 1572872 | tf_op jit(solution)/shard_map/ppermute | solution.py:132
  75.7 35.8 %collective-permute-start.2 = (bf16[512,896]{1,0:T(8,128)(2,1)S(1)}, bf16[512,896]{1,0:T(8,128)(2,1)S(1)}, u32[]{:S(2)}, u32[]{:S(2)}) collective-permute-start(bf16[512,896]{1,0:T(8,128)(2,1)S(1)} %add_convert_fusion.4.refs_0_), channel_id=1, source_target_pairs={{0,32},{32,64},{64,96},{96,0},{1,33},{33,65},{65,97},{97,1},{2,34}... | collective-permute-start | bytes 2752520 | tf_op jit(solution)/shard_map/ppermute | solution.py:126
  77.8 14.8 %collective-permute-start.5 = (bf16[512,128]{1,0:T(8,128)(2,1)S(1)}, bf16[512,128]{1,0:T(8,128)(2,1)S(1)}, u32[]{:S(2)}, u32[]{:S(2)}) collective-permute-start(bf16[512,128]{1,0:T(8,128)(2,1)S(1)} %slice.49), channel_id=1, source_target_pairs={{0,16},{16,0},{1,17},{17,1},{2,18},{18,2},{3,19},{19,3},{4,20},{20... | collective-permute-start | bytes 393224 | tf_op jit(solution)/shard_map/ppermute | solution.py:132
  92.6 25.2 %collective-permute-start.9 = (bf16[512,896]{1,0:T(8,128)(2,1)S(1)}, bf16[512,896]{1,0:T(8,128)(2,1)S(1)}, u32[]{:S(2)}, u32[]{:S(2)}) collective-permute-start(bf16[512,896]{1,0:T(8,128)(2,1)S(1)} %add_convert_fusion.2.refs_2_), channel_id=1, source_target_pairs={{0,16},{16,0},{1,17},{17,1},{2,18},{18,2},{3,19},{19,3},{4,20},{20... | collective-permute-start | bytes 2752520 | tf_op jit(solution)/shard_map/ppermute | solution.py:132
  101.8 21.9 %collective-permute-start.23 = (bf16[512,896]{1,0:T(8,128)(2,1)S(1)}, bf16[512,896]{1,0:T(8,128)(2,1)S(1)}, u32[]{:S(2)}, u32[]{:S(2)}) collective-permute-start(bf16[512,896]{1,0:T(8,128)(2,1)S(1)} %add_convert_fusion.1.refs_1_), channel_id=1, source_target_pairs={{0,32},{32,64},{64,96},{96,0},{1,33},{33,65},{65,97},{97,1},{2,34}... | collective-permute-start | bytes 2752520 | tf_op jit(solution)/shard_map/ppermute | solution.py:126
  101.8 29.3 %collective-permute-start.24 = (bf16[512,896]{1,0:T(8,128)(2,1)S(1)}, bf16[512,896]{1,0:T(8,128)(2,1)S(1)}, u32[]{:S(2)}, u32[]{:S(2)}) collective-permute-start(bf16[512,896]{1,0:T(8,128)(2,1)S(1)} %add_convert_fusion.2.refs_2_), channel_id=1, source_target_pairs={{0,96},{32,0},{64,32},{96,64},{1,97},{33,1},{65,33},{97,65},{2,98}... | collective-permute-start | bytes 2752520 | tf_op jit(solution)/shard_map/ppermute | solution.py:129
  111.5 27.9 %collective-permute-start.13 = (bf16[512,512]{1,0:T(8,128)(2,1)S(1)}, bf16[512,512]{1,0:T(8,128)(2,1)S(1)}, u32[]{:S(2)}, u32[]{:S(2)}) collective-permute-start(bf16[512,512]{1,0:T(8,128)(2,1)S(1)} %collective-permute-done.12.refs_0_), channel_id=1, source_target_pairs={{0,32},{32,64},{64,96},{96,0},{1,33},{33,65},{65,97},{97,1},{2,34}... | collective-permute-start | bytes 1572872 | tf_op jit(solution)/shard_map/ppermute | solution.py:126
  111.6 22.4 %collective-permute-start.19 = (bf16[128,128]{1,0:T(8,128)(2,1)S(1)}, bf16[128,128]{1,0:T(8,128)(2,1)S(1)}, u32[]{:S(2)}, u32[]{:S(2)}) collective-permute-start(bf16[128,128]{1,0:T(8,128)(2,1)S(1)} %slice.56), channel_id=1, source_target_pairs={{0,96},{32,0},{64,32},{96,64},{1,97},{33,1},{65,33},{97,65},{2,98}... | collective-permute-start | bytes 98312 | tf_op jit(solution)/shard_map/ppermute | solution.py:129
  117.8 27.2 %collective-permute-start.21 = (bf16[512,256]{1,0:T(8,128)(2,1)}, bf16[512,256]{1,0:T(8,128)(2,1)}, u32[]{:S(2)}, u32[]{:S(2)}) collective-permute-start(bf16[512,256]{1,0:T(8,128)(2,1)} %get-tuple-element.35), channel_id=1, source_target_pairs={{0,16},{16,0},{1,17},{17,1},{2,18},{18,2},{3,19},{19,3},{4,20},{20... | collective-permute-start | bytes 786440 | tf_op jit(solution)/shard_map/ppermute | solution.py:132
  124.6 22.4 %collective-permute-start.18 = (bf16[512,256]{1,0:T(8,128)(2,1)}, bf16[512,256]{1,0:T(8,128)(2,1)}, u32[]{:S(2)}, u32[]{:S(2)}) collective-permute-start(bf16[512,256]{1,0:T(8,128)(2,1)} %slice.55), channel_id=1, source_target_pairs={{0,96},{32,0},{64,32},{96,64},{1,97},{33,1},{65,33},{97,65},{2,98}... | collective-permute-start | bytes 786440 | tf_op jit(solution)/shard_map/ppermute | solution.py:129
  134.0 35.0 %collective-permute-start.11 = (bf16[512,256]{1,0:T(8,128)(2,1)}, bf16[512,256]{1,0:T(8,128)(2,1)}, u32[]{:S(2)}, u32[]{:S(2)}) collective-permute-start(bf16[512,256]{1,0:T(8,128)(2,1)} %get-tuple-element.36), channel_id=1, source_target_pairs={{0,16},{16,0},{1,17},{17,1},{2,18},{18,2},{3,19},{19,3},{4,20},{20... | collective-permute-start | bytes 786440 | tf_op jit(solution)/shard_map/ppermute | solution.py:132
  137.5 31.5 %collective-permute-start.14 = (bf16[512,128]{1,0:T(8,128)(2,1)}, bf16[512,128]{1,0:T(8,128)(2,1)}, u32[]{:S(2)}, u32[]{:S(2)}) collective-permute-start(bf16[512,128]{1,0:T(8,128)(2,1)} %get-tuple-element.37), channel_id=1, source_target_pairs={{0,96},{32,0},{64,32},{96,64},{1,97},{33,1},{65,33},{97,65},{2,98}... | collective-permute-start | bytes 393224 | tf_op jit(solution)/shard_map/ppermute | solution.py:129
  140.3 31.0 %collective-permute-start.10 = (bf16[512,128]{1,0:T(8,128)(2,1)}, bf16[512,128]{1,0:T(8,128)(2,1)}, u32[]{:S(2)}, u32[]{:S(2)}) collective-permute-start(bf16[512,128]{1,0:T(8,128)(2,1)} %get-tuple-element.38), channel_id=1, source_target_pairs={{0,96},{32,0},{64,32},{96,64},{1,97},{33,1},{65,33},{97,65},{2,98}... | collective-permute-start | bytes 393224 | tf_op jit(solution)/shard_map/ppermute | solution.py:129
  144.9 26.2 %collective-permute-start.6 = (bf16[384,128]{1,0:T(8,128)(2,1)}, bf16[384,128]{1,0:T(8,128)(2,1)}, u32[]{:S(2)}, u32[]{:S(2)}) collective-permute-start(bf16[384,128]{1,0:T(8,128)(2,1)} %slice.50), channel_id=1, source_target_pairs={{0,32},{32,64},{64,96},{96,0},{1,33},{33,65},{65,97},{97,1},{2,34}... | collective-permute-start | bytes 294920 | tf_op jit(solution)/shard_map/ppermute | solution.py:126
  147.0 24.2 %collective-permute-start.3 = (bf16[384,128]{1,0:T(8,128)(2,1)}, bf16[384,128]{1,0:T(8,128)(2,1)}, u32[]{:S(2)}, u32[]{:S(2)}) collective-permute-start(bf16[384,128]{1,0:T(8,128)(2,1)} %slice.48), channel_id=1, source_target_pairs={{0,16},{16,0},{1,17},{17,1},{2,18},{18,2},{3,19},{19,3},{4,20},{20... | collective-permute-start | bytes 294920 | tf_op jit(solution)/shard_map/ppermute | solution.py:132
  (37 other events, 389.7 us)

commit v4 on v3

--- a/solution.py
+++ b/solution.py
@@ -104,19 +104,24 @@
 def gathered_gain(gain):
     length = gain.shape[0]
     y, xl, cols = (lax.axis_index(axis) for axis in ("y", "xl", "cols"))
-    index = jnp.arange(4)[:, None]
-    x = jnp.broadcast_to(gain[None], (4, length))
-    for shift in (1, 2, 3):
-        part = lax.ppermute(gain, "y", [(i, (i + shift) % 4) for i in range(4)])
-        x = jnp.where(index == (y - shift) % 4, part[None], x)
-    x = doubled(x, "xl", SWAP, xl == 1)
+    x_hi = (cols >> 1) & 1
+    x = gain[None]
     for bit in (1, 4, 8):
         pairs = [(i, i ^ bit) for i in range(16)]
         x = doubled(x, "cols", pairs, (cols & bit) != 0)
     pairs = [(i, i ^ 18) for i in range(32)]
-    x = doubled(x, ("xl", "cols"), pairs, (cols & 2) != 0)
-    x = x.reshape(2, 2, 2, 2, 2, 4, length)
-    return x.transpose(5, 4, 1, 2, 0, 3, 6).reshape(-1)
+    x = doubled(x, ("xl", "cols"), pairs, x_hi == 1)
+    index = jnp.arange(4)[:, None, None]
+    mine = jnp.broadcast_to(x[None], (4, *x.shape))
+    for shift in (1, 2, 3):
+        part = lax.ppermute(x, "y", [(i, (i + shift) % 4) for i in range(4)])
+        mine = jnp.where(index == (y - shift) % 4, part[None], mine)
+    other = lax.ppermute(mine, "xl", SWAP)
+    mine, other = (v.reshape(4, 1, 2, 2, 2, 2, length) for v in (mine, other))
+    both = jnp.arange(2)
+    own = (both[:, None] ^ both[None, :] ^ xl ^ x_hi) == 0
+    x = jnp.where(own.reshape(1, 2, 2, 1, 1, 1, 1), mine, other)
+    return x.transpose(0, 1, 3, 4, 2, 5, 6).reshape(-1)
 
 
 def per_device(train_gate, low_gate, high_gate, train_up, low_up, high_up, norm_train, norm_step):
@@ -149,8 +154,7 @@
     cg_f0, cg_f4, cg_f1 = (across(g_f[:, :first]), across(g_f[:, first:near]), across(g_f[LANES:, near:mid]))
     cg_f2, cg_f3 = down(cg_p[:, mid:]), down(cg_p[:LANES, near:mid])
     cu_f2, cu_f3 = down(cu_p[:, mid:late]), down(cu_p[:, late:])
-    cu_f4 = down(cu_p[:LANES, near:mid])
-    cu_f0, cu_f1 = up(cu_m0), up(cu_m1[LANES:])
+    cu_f0, cu_f1 = up(cu_m0), up(cu_m1)
 
     out = jax.ShapeDtypeStruct((width, rows * 8), jnp.bfloat16)
     outs = place((out, out), [(g, 0, 0, 0, 0), (u, 1, 0, 0, 0)])
@@ -167,11 +171,9 @@
             (u_f, 1, 0, 2, 0),
         ],
     )
-    outs = place(outs, [(cg_f2, 0, mid, 2, 1), (cg_f3, 0, near, 2, 1), (cu_f4, 1, near, 2, 1), (cg_f0, 0, 0, 2, 1)], held=True)
+    outs = place(outs, [(cg_f2, 0, mid, 2, 1), (cg_f3, 0, near, 2, 1), (cg_f0, 0, 0, 2, 1)], held=True)
     outs = place(outs, [(cg_f4, 0, first, 2, 1), (cu_f0, 1, 0, 2, 1), (cu_f2, 1, mid, 2, 1)], held=True)
-    outs = place(
-        outs, [(cg_f1, 0, near, 2, 1, LANES), (cu_f1, 1, near, 2, 1, LANES), (cu_f3, 1, late, 2, 1)], held=True
-    )
+    outs = place(outs, [(cg_f1, 0, near, 2, 1, LANES), (cu_f1, 1, near, 2, 1), (cu_f3, 1, late, 2, 1)], held=True)
     return (*outs, gathered_gain(gain))
 
 

time: 174 us -> 180 us (1.034)
  the two profiles are of different devices: /device:TPU:2 before, /device:TPU:74 now
where the time goes in v4:
time: 180 us
  waiting for transfers between devices  70.7 us (39%)
  starting transfers between devices  61.5 us (34%)
  Pallas kernels  22.7 us (13%)
  local copies, waits for them, and re-layouts  11.1 us (6%)
  matrix products  8.79 us (5%)
  other arithmetic  3.9 us (2%)
    ppermute x9, starting transfers between devices, down(): return lax.ppermute(v, 'y', DOWN)  36.1 us
    ppermute x10, waiting for transfers between devices, across(): return lax.ppermute(v, 'xl', SWAP)  35.9 us
    pallas_call x8, Pallas kernels, place(): pl.pallas_call(kernel, out_shape=shapes, in_specs=[pl.BlockSpec(memory_sp...  22.7 us
    ppermute x10, starting transfers between devices, across(): return lax.ppermute(v, 'xl', SWAP)  12.6 us
    ppermute x9, waiting for transfers between devices, down(): return lax.ppermute(v, 'y', DOWN)  11.9 us
    ppermute x4, waiting for transfers between devices, doubled(): other = lax.ppermute(x, axis, pairs)  9.82 us
    dot_general x5, matrix products, merged(): lax.dot_general(low, high, (((0,), (0,)), ((), ())), preferred_element_ty...  8.79 us
    ppermute x7, waiting for transfers between devices, up(): return lax.ppermute(v, 'y', UP)  7.04 us
  transfers between devices with their start and end apart: 34, of which 16 were waited for; matrix products, arithmetic and copies ran while one was open for 11% of the time, Pallas kernels for 12%

profile of v4, /device:TPU:74, one launch (start us, length us, event | category | flops | bytes accessed | tf_op | source)
XLA Modules:
  0.0 179.8 jit_solution(14330275922818078165)
XLA Ops:
  9.4 1.9 %collective-permute-done.27 = bf16[2,32]{1,0:T(2,128)(2,1)S(1)} collective-permute-done((bf16[2,32]{1,0:T(2,128)(2,1)S(1)}, bf16[2,32]{1,0:T(2,128)(2,1)S(1)}, u32[]{:S(2)}, u32[]{:S(2)}) %collective-permute-start.27) | collective-permute-done | bytes 160 | tf_op jit(solution)/shard_map/ppermute | solution.py:100
  11.5 5.0 %collective-permute-done.28 = bf16[4,32]{1,0:T(4,128)(2,1)S(1)} collective-permute-done((bf16[4,32]{1,0:T(4,128)(2,1)S(1)}, bf16[4,32]{1,0:T(4,128)(2,1)S(1)}, u32[]{:S(2)}, u32[]{:S(2)}) %collective-permute-start.28) | collective-permute-done | bytes 288 | tf_op jit(solution)/shard_map/ppermute | solution.py:100
  16.5 2.2 %collective-permute-start.29 = (bf16[8,32]{1,0:T(8,128)(2,1)S(1)}, bf16[8,32]{1,0:T(8,128)(2,1)}, u32[]{:S(2)}, u32[]{:S(2)}) collective-permute-start(bf16[8,32]{1,0:T(8,128)(2,1)S(1)} %maximum_select_fusion.2), channel_id=1, source_target_pairs={{0,18},{1,19},{2,16},{3,17},{4,22},{5,23},{6,20},{7,21},{8,26},{9,... | collective-permute-start | bytes 1544 | tf_op jit(solution)/shard_map/ppermute | solution.py:100
  25.2 2.0 %collective-permute-done.31 = bf16[16,32]{1,0:T(8,128)(2,1)S(1)} collective-permute-done((bf16[16,32]{1,0:T(8,128)(2,1)S(1)}, bf16[16,32]{1,0:T(8,128)(2,1)S(1)}, u32[]{:S(2)}, u32[]{:S(2)}) %collective-permute-start.31) | collective-permute-done | bytes 1056 | tf_op jit(solution)/shard_map/ppermute | solution.py:117
  27.2 18.8 %collective-permute-start.7 = (bf16[512,896]{1,0:T(8,128)(2,1)}, bf16[512,896]{1,0:T(8,128)(2,1)S(1)}, u32[]{:S(2)}, u32[]{:S(2)}) collective-permute-start(bf16[512,896]{1,0:T(8,128)(2,1)} %param.11), channel_id=1, source_target_pairs={{0,96},{32,0},{64,32},{96,64},{1,97},{33,1},{65,33},{97,65},{2,98}... | collective-permute-start | bytes 2752520 | tf_op jit(solution)/shard_map/ppermute | solution.py:134
  47.7 2.2 %collective-permute-done.33 = bf16[4,16,32]{2,1,0:T(8,128)(2,1)S(1)} collective-permute-done((bf16[4,16,32]{2,1,0:T(8,128)(2,1)S(1)}, bf16[4,16,32]{2,1,0:T(8,128)(2,1)S(1)}, u32[]{:S(2)}, u32[]{:S(2)}) %collective-permute-start.33) | collective-permute-done | bytes 4128 | tf_op jit(solution)/shard_map/ppermute | solution.py:119
  51.4 2.6 %collective-permute-done.16 = bf16[32,512]{1,0:T(8,128)(2,1)S(1)} collective-permute-done((bf16[32,512]{1,0:T(8,128)(2,1)}, bf16[32,512]{1,0:T(8,128)(2,1)S(1)}, u32[]{:S(2)}, u32[]{:S(2)}) %collective-permute-start.16) | collective-permute-done | bytes 32800 | tf_op jit(solution)/shard_map/ppermute | solution.py:137
  54.1 11.1 %collective-permute-done.8 = bf16[32,512]{1,0:T(8,128)(2,1)S(1)} collective-permute-done((bf16[32,512]{1,0:T(8,128)(2,1)}, bf16[32,512]{1,0:T(8,128)(2,1)S(1)}, u32[]{:S(2)}, u32[]{:S(2)}) %collective-permute-start.8) | collective-permute-done | bytes 32800 | tf_op jit(solution)/shard_map/ppermute | solution.py:134
  68.3 2.4 %collective-permute-start.25 = (bf16[512,896]{1,0:T(8,128)(2,1)S(1)}, bf16[512,896]{1,0:T(8,128)(2,1)S(1)}, u32[]{:S(2)}, u32[]{:S(2)}) collective-permute-start(bf16[512,896]{1,0:T(8,128)(2,1)S(1)} %add_convert_fusion.refs_0_), channel_id=1, source_target_pairs={{0,96},{32,0},{64,32},{96,64},{1,97},{33,1},{65,33},{97,65},{2,98}... | collective-permute-start | bytes 2752520 | tf_op jit(solution)/shard_map/ppermute | solution.py:134
  72.4 2.5 %collective-permute-done.1 = bf16[32,512]{1,0:T(8,128)(2,1)S(1)} collective-permute-done((bf16[32,512]{1,0:T(8,128)(2,1)}, bf16[32,512]{1,0:T(8,128)(2,1)S(1)}, u32[]{:S(2)}, u32[]{:S(2)}) %collective-permute-start.1) | collective-permute-done | bytes 32800 | tf_op jit(solution)/shard_map/ppermute | solution.py:131
  74.9 2.7 %collective-permute-start.17 = (bf16[512,896]{1,0:T(8,128)(2,1)S(1)}, bf16[512,896]{1,0:T(8,128)(2,1)}, u32[]{:S(2)}, u32[]{:S(2)}) collective-permute-start(bf16[512,896]{1,0:T(8,128)(2,1)S(1)} %add_convert_fusion.1.refs_1_), channel_id=1, source_target_pairs={{0,96},{32,0},{64,32},{96,64},{1,97},{33,1},{65,33},{97,65},{2,98}... | collective-permute-start | bytes 2752520 | tf_op jit(solution)/shard_map/ppermute | solution.py:134
  78.1 2.5 %add_convert_fusion.4.refs_0_ = bf16[512,896]{1,0:T(8,128)(2,1)} fusion(bf16[512,896]{1,0:T(8,128)(2,1)} %collective-permute-done, bf16[32,512]{1,0:T(8,128)(2,1)S(1)} %collective-permute-done.1, bf16[32,896]{1,0:T(8,128)(2,1)S(1)} %copy-done), kind=kOutput, calls=%fused_computation.4 | convolution fusion | flops 30736384 | bytes 1925120 | tf_op jit(solution)/shard_map/dot_general | solution.py:19
  82.0 6.3 %collective-permute-done.24.refs_1_ = bf16[512,896]{1,0:T(8,128)(2,1)S(1)} collective-permute-done((bf16[512,896]{1,0:T(8,128)(2,1)S(1)}, bf16[512,896]{1,0:T(8,128)(2,1)S(1)}, u32[]{:S(2)}, u32[]{:S(2)}) %collective-permute-start.24) | collective-permute-done | bytes 917536 | tf_op jit(solution)/shard_map/ppermute | solution.py:137
  93.1 25.5 %collective-permute-done.5.refs_1_ = bf16[512,128]{1,0:T(8,128)(2,1)S(1)} collective-permute-done((bf16[512,128]{1,0:T(8,128)(2,1)S(1)}, bf16[512,128]{1,0:T(8,128)(2,1)S(1)}, u32[]{:S(2)}, u32[]{:S(2)}) %collective-permute-start.5) | collective-permute-done | bytes 131104 | tf_op jit(solution)/shard_map/ppermute | solution.py:137
  121.0 2.5 %shard_map.103 = (bf16[896,4096]{1,0:T(8,128)(2,1)}, bf16[896,4096]{1,0:T(8,128)(2,1)}) custom-call(bf16[512,896]{1,0:T(8,128)(2,1)S(1)} %add_convert_fusion.refs_0_, bf16[512,896]{1,0:T(8,128)(2,1)S(1)} %add_convert_fusion.3.refs_1_), custom_call_target="tpu_custom_call" | custom-call | bytes 3670016 | tf_op jit(solution)/shard_map/pallas_call | solution.py:81
  133.9 3.5 %collective-permute-start.18 = (bf16[512,256]{1,0:T(8,128)(2,1)S(1)}, bf16[512,256]{1,0:T(8,128)(2,1)S(1)}, u32[]{:S(2)}, u32[]{:S(2)}) collective-permute-start(bf16[512,256]{1,0:T(8,128)(2,1)S(1)} %slice.46), channel_id=1, source_target_pairs={{0,96},{32,0},{64,32},{96,64},{1,97},{33,1},{65,33},{97,65},{2,98}... | collective-permute-start | bytes 786440 | tf_op jit(solution)/shard_map/ppermute | solution.py:134
  138.9 3.4 %collective-permute-done.22.refs_3_ = bf16[512,896]{1,0:T(8,128)(2,1)} collective-permute-done((bf16[512,896]{1,0:T(8,128)(2,1)S(1)}, bf16[512,896]{1,0:T(8,128)(2,1)}, u32[]{:S(2)}, u32[]{:S(2)}) %collective-permute-start.22) | collective-permute-done | bytes 917536 | tf_op jit(solution)/shard_map/ppermute | solution.py:131
  142.3 3.2 %collective-permute-start.19 = (bf16[128,128]{1,0:T(8,128)(2,1)S(1)}, bf16[128,128]{1,0:T(8,128)(2,1)S(1)}, u32[]{:S(2)}, u32[]{:S(2)}) collective-permute-start(bf16[128,128]{1,0:T(8,128)(2,1)S(1)} %slice.47), channel_id=1, source_target_pairs={{0,96},{32,0},{64,32},{96,64},{1,97},{33,1},{65,33},{97,65},{2,98}... | collective-permute-start | bytes 98312 | tf_op jit(solution)/shard_map/ppermute | solution.py:134
  151.7 3.0 %collective-permute-start.14 = (bf16[512,128]{1,0:T(8,128)(2,1)}, bf16[512,128]{1,0:T(8,128)(2,1)}, u32[]{:S(2)}, u32[]{:S(2)}) collective-permute-start(bf16[512,128]{1,0:T(8,128)(2,1)} %get-tuple-element.37), channel_id=1, source_target_pairs={{0,96},{32,0},{64,32},{96,64},{1,97},{33,1},{65,33},{97,65},{2,98}... | collective-permute-start | bytes 393224 | tf_op jit(solution)/shard_map/ppermute | solution.py:134
  159.2 3.9 %shard_map.104 = (bf16[896,4096]{1,0:T(8,128)(2,1)}, bf16[896,4096]{1,0:T(8,128)(2,1)}) custom-call(bf16[512,896]{1,0:T(8,128)(2,1)} %add_convert_fusion.4.refs_0_, bf16[512,896]{1,0:T(8,128)(2,1)S(1)} %add_convert_fusion.1.refs_1_, bf16[512,896]{1,0:T(8,128)(2,1)} %add_convert_fusion.2.refs_2_, ...), custom_call_target="tpu_custom_call", output_to_operand_aliasing={{0}: (3, {}), {1}: (4, {})} | custom-call | bytes 5505024 | tf_op jit(solution)/shard_map/pallas_call | solution.py:81
  163.2 3.4 %shard_map.105 = (bf16[896,4096]{1,0:T(8,128)(2,1)}, bf16[896,4096]{1,0:T(8,128)(2,1)}) custom-call(bf16[512,896]{1,0:T(8,128)(2,1)S(1)} %collective-permute-done.4.refs_0_, bf16[512,896]{1,0:T(8,128)(2,1)S(1)} %copy-done.2, bf16[512,896]{1,0:T(8,128)(2,1)S(1)} %copy-done.4, ...), custom_call_target="tpu_custom_call", output_to_operand_aliasing={{0}: (3, {}), {1}: (4, {})} | custom-call | bytes 5505024 | tf_op jit(solution)/shard_map/pallas_call | solution.py:81
  166.6 3.9 %shard_map.106 = (bf16[896,4096]{1,0:T(8,128)(2,1)}, bf16[896,4096]{1,0:T(8,128)(2,1)}) custom-call(bf16[512,896]{1,0:T(8,128)(2,1)} %collective-permute-done.2.refs_0_, bf16[512,896]{1,0:T(8,128)(2,1)} %collective-permute-done.17.refs_1_, bf16[512,896]{1,0:T(8,128)(2,1)} %collective-permute-done.9.refs_2_, ...), custom_call_target="tpu_custom_call", output_to_operand_aliasing={{0}: (3, {}), {1}: (4, {})} | custom-call | bytes 5505024 | tf_op jit(solution)/shard_map/pallas_call | solution.py:81
  170.5 3.9 %shard_map.107 = (bf16[896,4096]{1,0:T(8,128)(2,1)}, bf16[896,4096]{1,0:T(8,128)(2,1)}) custom-call(bf16[512,512]{1,0:T(8,128)(2,1)S(1)} %collective-permute-done.12.refs_0_, bf16[512,128]{1,0:T(8,128)(2,1)S(1)} %collective-permute-done.5.refs_1_, bf16[512,256]{1,0:T(8,128)(2,1)S(1)} %copy-done.8, ...), custom_call_target="tpu_custom_call", output_to_operand_aliasing={{0}: (5, {}), {1}: (6, {})} | custom-call | bytes 5505024 | tf_op jit(solution)/shard_map/pallas_call | solution.py:81
  175.6 2.2 %shard_map.109 = (bf16[896,4096]{1,0:T(8,128)(2,1)}, bf16[896,4096]{1,0:T(8,128)(2,1)}) custom-call(bf16[512,256]{1,0:T(8,128)(2,1)} %collective-permute-done.11.refs_0_, bf16[512,512]{1,0:T(8,128)(2,1)S(1)} %copy-done.6, bf16[512,128]{1,0:T(8,128)(2,1)} %collective-permute-done.14.refs_2_, ...), custom_call_target="tpu_custom_call", output_to_operand_aliasing={{0}: (3, {}), {1}: (4, {})} | custom-call | bytes 1835008 | tf_op jit(solution)/shard_map/pallas_call | solution.py:81
  (117 shorter events, 57.8 us)
Async XLA Ops:
  0.7 67.6 %collective-permute-start.15 = (bf16[512,896]{1,0:T(8,128)(2,1)}, bf16[512,896]{1,0:T(8,128)(2,1)S(1)}, u32[]{:S(2)}, u32[]{:S(2)}) collective-permute-start(bf16[512,896]{1,0:T(8,128)(2,1)} %param.8), channel_id=1, source_target_pairs={{0,16},{16,0},{1,17},{17,1},{2,18},{18,2},{3,19},{19,3},{4,20},{20... | collective-permute-start | bytes 2752520 | tf_op jit(solution)/shard_map/ppermute | solution.py:137
  1.3 76.3 %collective-permute-start = (bf16[512,896]{1,0:T(8,128)(2,1)}, bf16[512,896]{1,0:T(8,128)(2,1)}, u32[]{:S(2)}, u32[]{:S(2)}) collective-permute-start(bf16[512,896]{1,0:T(8,128)(2,1)} %param.8), channel_id=1, source_target_pairs={{0,32},{32,64},{64,96},{96,0},{1,33},{33,65},{65,97},{97,1},{2,34}... | collective-permute-start | bytes 2752520 | tf_op jit(solution)/shard_map/ppermute | solution.py:131
  4.5 66.2 %collective-permute-start.4 = (bf16[512,896]{1,0:T(8,128)(2,1)S(1)}, bf16[512,896]{1,0:T(8,128)(2,1)S(1)}, u32[]{:S(2)}, u32[]{:S(2)}) collective-permute-start(bf16[512,896]{1,0:T(8,128)(2,1)S(1)} %add_convert_fusion.3.refs_1_), channel_id=1, source_target_pairs={{0,32},{32,64},{64,96},{96,0},{1,33},{33,65},{65,97},{97,1},{2,34}... | collective-permute-start | bytes 2752520 | tf_op jit(solution)/shard_map/ppermute | solution.py:131
  24.8 21.2 %collective-permute-start.32 = (bf16[16,32]{1,0:T(8,128)(2,1)S(1)}, bf16[16,32]{1,0:T(8,128)(2,1)S(1)}, u32[]{:S(2)}, u32[]{:S(2)}) collective-permute-start(bf16[16,32]{1,0:T(8,128)(2,1)S(1)} %maximum_select_fusion), channel_id=1, source_target_pairs={{0,32},{32,64},{64,96},{96,0},{1,33},{33,65},{65,97},{97,1},{2,34}... | collective-permute-start | bytes 3080 | tf_op jit(solution)/shard_map/ppermute | solution.py:117
  27.2 53.5 %collective-permute-start.7 = (bf16[512,896]{1,0:T(8,128)(2,1)}, bf16[512,896]{1,0:T(8,128)(2,1)S(1)}, u32[]{:S(2)}, u32[]{:S(2)}) collective-permute-start(bf16[512,896]{1,0:T(8,128)(2,1)} %param.11), channel_id=1, source_target_pairs={{0,96},{32,0},{64,32},{96,64},{1,97},{33,1},{65,33},{97,65},{2,98}... | collective-permute-start | bytes 2752520 | tf_op jit(solution)/shard_map/ppermute | solution.py:134
  54.0 11.1 %collective-permute-start.8 = (bf16[32,512]{1,0:T(8,128)(2,1)}, bf16[32,512]{1,0:T(8,128)(2,1)S(1)}, u32[]{:S(2)}, u32[]{:S(2)}) collective-permute-start(bf16[32,512]{1,0:T(8,128)(2,1)} %bitcast.32), channel_id=1, source_target_pairs={{0,96},{32,0},{64,32},{96,64},{1,97},{33,1},{65,33},{97,65},{2,98}... | collective-permute-start | bytes 98312 | tf_op jit(solution)/shard_map/ppermute | solution.py:134
  65.1 23.2 %collective-permute-start.24 = (bf16[512,896]{1,0:T(8,128)(2,1)S(1)}, bf16[512,896]{1,0:T(8,128)(2,1)S(1)}, u32[]{:S(2)}, u32[]{:S(2)}) collective-permute-start(bf16[512,896]{1,0:T(8,128)(2,1)S(1)} %add_convert_fusion.3.refs_1_), channel_id=1, source_target_pairs={{0,16},{16,0},{1,17},{17,1},{2,18},{18,2},{3,19},{19,3},{4,20},{20... | collective-permute-start | bytes 2752520 | tf_op jit(solution)/shard_map/ppermute | solution.py:137
  68.3 23.3 %collective-permute-start.25 = (bf16[512,896]{1,0:T(8,128)(2,1)S(1)}, bf16[512,896]{1,0:T(8,128)(2,1)S(1)}, u32[]{:S(2)}, u32[]{:S(2)}) collective-permute-start(bf16[512,896]{1,0:T(8,128)(2,1)S(1)} %add_convert_fusion.refs_0_), channel_id=1, source_target_pairs={{0,96},{32,0},{64,32},{96,64},{1,97},{33,1},{65,33},{97,65},{2,98}... | collective-permute-start | bytes 2752520 | tf_op jit(solution)/shard_map/ppermute | solution.py:134
  74.9 49.4 %collective-permute-start.17 = (bf16[512,896]{1,0:T(8,128)(2,1)S(1)}, bf16[512,896]{1,0:T(8,128)(2,1)}, u32[]{:S(2)}, u32[]{:S(2)}) collective-permute-start(bf16[512,896]{1,0:T(8,128)(2,1)S(1)} %add_convert_fusion.1.refs_1_), channel_id=1, source_target_pairs={{0,96},{32,0},{64,32},{96,64},{1,97},{33,1},{65,33},{97,65},{2,98}... | collective-permute-start | bytes 2752520 | tf_op jit(solution)/shard_map/ppermute | solution.py:134
  77.6 41.9 %collective-permute-start.12 = (bf16[512,512]{1,0:T(8,128)(2,1)S(1)}, bf16[512,512]{1,0:T(8,128)(2,1)S(1)}, u32[]{:S(2)}, u32[]{:S(2)}) collective-permute-start(bf16[512,512]{1,0:T(8,128)(2,1)S(1)} %slice.44), channel_id=1, source_target_pairs={{0,16},{16,0},{1,17},{17,1},{2,18},{18,2},{3,19},{19,3},{4,20},{20... | collective-permute-start | bytes 1572872 | tf_op jit(solution)/shard_map/ppermute | solution.py:137
  80.7 46.0 %collective-permute-start.2 = (bf16[512,896]{1,0:T(8,128)(2,1)}, bf16[512,896]{1,0:T(8,128)(2,1)}, u32[]{:S(2)}, u32[]{:S(2)}) collective-permute-start(bf16[512,896]{1,0:T(8,128)(2,1)} %add_convert_fusion.4.refs_0_), channel_id=1, source_target_pairs={{0,32},{32,64},{64,96},{96,0},{1,33},{33,65},{65,97},{97,1},{2,34}... | collective-permute-start | bytes 2752520 | tf_op jit(solution)/shard_map/ppermute | solution.py:131
  89.3 44.6 %collective-permute-start.9 = (bf16[512,896]{1,0:T(8,128)(2,1)}, bf16[512,896]{1,0:T(8,128)(2,1)}, u32[]{:S(2)}, u32[]{:S(2)}) collective-permute-start(bf16[512,896]{1,0:T(8,128)(2,1)} %add_convert_fusion.2.refs_2_), channel_id=1, source_target_pairs={{0,16},{16,0},{1,17},{17,1},{2,18},{18,2},{3,19},{19,3},{4,20},{20... | collective-permute-start | bytes 2752520 | tf_op jit(solution)/shard_map/ppermute | solution.py:137
  92.6 26.0 %collective-permute-start.5 = (bf16[512,128]{1,0:T(8,128)(2,1)S(1)}, bf16[512,128]{1,0:T(8,128)(2,1)S(1)}, u32[]{:S(2)}, u32[]{:S(2)}) collective-permute-start(bf16[512,128]{1,0:T(8,128)(2,1)S(1)} %slice.41), channel_id=1, source_target_pairs={{0,16},{16,0},{1,17},{17,1},{2,18},{18,2},{3,19},{19,3},{4,20},{20... | collective-permute-start | bytes 393224 | tf_op jit(solution)/shard_map/ppermute | solution.py:137
  118.6 23.7 %collective-permute-start.22 = (bf16[512,896]{1,0:T(8,128)(2,1)S(1)}, bf16[512,896]{1,0:T(8,128)(2,1)}, u32[]{:S(2)}, u32[]{:S(2)}) collective-permute-start(bf16[512,896]{1,0:T(8,128)(2,1)S(1)} %add_convert_fusion.1.refs_1_), channel_id=1, source_target_pairs={{0,32},{32,64},{64,96},{96,0},{1,33},{33,65},{65,97},{97,1},{2,34}... | collective-permute-start | bytes 2752520 | tf_op jit(solution)/shard_map/ppermute | solution.py:131
  119.5 26.1 %collective-permute-start.23 = (bf16[512,896]{1,0:T(8,128)(2,1)}, bf16[512,896]{1,0:T(8,128)(2,1)}, u32[]{:S(2)}, u32[]{:S(2)}) collective-permute-start(bf16[512,896]{1,0:T(8,128)(2,1)} %add_convert_fusion.2.refs_2_), channel_id=1, source_target_pairs={{0,96},{32,0},{64,32},{96,64},{1,97},{33,1},{65,33},{97,65},{2,98}... | collective-permute-start | bytes 2752520 | tf_op jit(solution)/shard_map/ppermute | solution.py:134
  124.3 7.7 %collective-permute-start.21 = (bf16[512,256]{1,0:T(8,128)(2,1)S(1)}, bf16[512,256]{1,0:T(8,128)(2,1)S(1)}, u32[]{:S(2)}, u32[]{:S(2)}) collective-permute-start(bf16[512,256]{1,0:T(8,128)(2,1)S(1)} %slice.49), channel_id=1, source_target_pairs={{0,16},{16,0},{1,17},{17,1},{2,18},{18,2},{3,19},{19,3},{4,20},{20... | collective-permute-start | bytes 786440 | tf_op jit(solution)/shard_map/ppermute | solution.py:137
  126.6 24.3 %collective-permute-start.13 = (bf16[512,512]{1,0:T(8,128)(2,1)S(1)}, bf16[512,512]{1,0:T(8,128)(2,1)S(1)}, u32[]{:S(2)}, u32[]{:S(2)}) collective-permute-start(bf16[512,512]{1,0:T(8,128)(2,1)S(1)} %collective-permute-done.12.refs_0_), channel_id=1, source_target_pairs={{0,32},{32,64},{64,96},{96,0},{1,33},{33,65},{65,97},{97,1},{2,34}... | collective-permute-start | bytes 1572872 | tf_op jit(solution)/shard_map/ppermute | solution.py:131
  132.0 22.6 %collective-permute-start.20 = (bf16[512,256]{1,0:T(8,128)(2,1)S(1)}, bf16[512,256]{1,0:T(8,128)(2,1)S(1)}, u32[]{:S(2)}, u32[]{:S(2)}) collective-permute-start(bf16[512,256]{1,0:T(8,128)(2,1)S(1)} %get-tuple-element.35), channel_id=1, source_target_pairs={{0,16},{16,0},{1,17},{17,1},{2,18},{18,2},{3,19},{19,3},{4,20},{20... | collective-permute-start | bytes 786440 | tf_op jit(solution)/shard_map/ppermute | solution.py:137
  133.9 22.3 %collective-permute-start.18 = (bf16[512,256]{1,0:T(8,128)(2,1)S(1)}, bf16[512,256]{1,0:T(8,128)(2,1)S(1)}, u32[]{:S(2)}, u32[]{:S(2)}) collective-permute-start(bf16[512,256]{1,0:T(8,128)(2,1)S(1)} %slice.46), channel_id=1, source_target_pairs={{0,96},{32,0},{64,32},{96,64},{1,97},{33,1},{65,33},{97,65},{2,98}... | collective-permute-start | bytes 786440 | tf_op jit(solution)/shard_map/ppermute | solution.py:134
  145.5 29.9 %collective-permute-start.11 = (bf16[512,256]{1,0:T(8,128)(2,1)}, bf16[512,256]{1,0:T(8,128)(2,1)}, u32[]{:S(2)}, u32[]{:S(2)}) collective-permute-start(bf16[512,256]{1,0:T(8,128)(2,1)} %get-tuple-element.36), channel_id=1, source_target_pairs={{0,16},{16,0},{1,17},{17,1},{2,18},{18,2},{3,19},{19,3},{4,20},{20... | collective-permute-start | bytes 786440 | tf_op jit(solution)/shard_map/ppermute | solution.py:137
  149.6 28.1 %collective-permute-start.6 = (bf16[512,128]{1,0:T(8,128)(2,1)S(1)}, bf16[512,128]{1,0:T(8,128)(2,1)}, u32[]{:S(2)}, u32[]{:S(2)}) collective-permute-start(bf16[512,128]{1,0:T(8,128)(2,1)S(1)} %collective-permute-done.5.refs_1_), channel_id=1, source_target_pairs={{0,32},{32,64},{64,96},{96,0},{1,33},{33,65},{65,97},{97,1},{2,34}... | collective-permute-start | bytes 393224 | tf_op jit(solution)/shard_map/ppermute | solution.py:131
  151.7 23.7 %collective-permute-start.14 = (bf16[512,128]{1,0:T(8,128)(2,1)}, bf16[512,128]{1,0:T(8,128)(2,1)}, u32[]{:S(2)}, u32[]{:S(2)}) collective-permute-start(bf16[512,128]{1,0:T(8,128)(2,1)} %get-tuple-element.37), channel_id=1, source_target_pairs={{0,96},{32,0},{64,32},{96,64},{1,97},{33,1},{65,33},{97,65},{2,98}... | collective-permute-start | bytes 393224 | tf_op jit(solution)/shard_map/ppermute | solution.py:134
  155.4 22.4 %collective-permute-start.10 = (bf16[512,128]{1,0:T(8,128)(2,1)}, bf16[512,128]{1,0:T(8,128)(2,1)}, u32[]{:S(2)}, u32[]{:S(2)}) collective-permute-start(bf16[512,128]{1,0:T(8,128)(2,1)} %get-tuple-element.38), channel_id=1, source_target_pairs={{0,96},{32,0},{64,32},{96,64},{1,97},{33,1},{65,33},{97,65},{2,98}... | collective-permute-start | bytes 393224 | tf_op jit(solution)/shard_map/ppermute | solution.py:134
  156.9 20.9 %collective-permute-start.3 = (bf16[384,128]{1,0:T(8,128)(2,1)S(1)}, bf16[384,128]{1,0:T(8,128)(2,1)}, u32[]{:S(2)}, u32[]{:S(2)}) collective-permute-start(bf16[384,128]{1,0:T(8,128)(2,1)S(1)} %slice.40), channel_id=1, source_target_pairs={{0,16},{16,0},{1,17},{17,1},{2,18},{18,2},{3,19},{19,3},{4,20},{20... | collective-permute-start | bytes 294920 | tf_op jit(solution)/shard_map/ppermute | solution.py:137
  (29 other events, 317.0 us)

commit v5 on v4

--- a/solution.py
+++ b/solution.py
@@ -154,7 +154,8 @@
     cg_f0, cg_f4, cg_f1 = (across(g_f[:, :first]), across(g_f[:, first:near]), across(g_f[LANES:, near:mid]))
     cg_f2, cg_f3 = down(cg_p[:, mid:]), down(cg_p[:LANES, near:mid])
     cu_f2, cu_f3 = down(cu_p[:, mid:late]), down(cu_p[:, late:])
-    cu_f0, cu_f1 = up(cu_m0), up(cu_m1)
+    cu_f4 = down(cu_p[:LANES, near:mid])
+    cu_f0, cu_f1 = up(cu_m0), up(cu_m1[LANES:])
 
     out = jax.ShapeDtypeStruct((width, rows * 8), jnp.bfloat16)
     outs = place((out, out), [(g, 0, 0, 0, 0), (u, 1, 0, 0, 0)])
@@ -171,9 +172,11 @@
             (u_f, 1, 0, 2, 0),
         ],
     )
-    outs = place(outs, [(cg_f2, 0, mid, 2, 1), (cg_f3, 0, near, 2, 1), (cg_f0, 0, 0, 2, 1)], held=True)
+    outs = place(outs, [(cg_f2, 0, mid, 2, 1), (cg_f3, 0, near, 2, 1), (cu_f4, 1, near, 2, 1), (cg_f0, 0, 0, 2, 1)], held=True)
     outs = place(outs, [(cg_f4, 0, first, 2, 1), (cu_f0, 1, 0, 2, 1), (cu_f2, 1, mid, 2, 1)], held=True)
-    outs = place(outs, [(cg_f1, 0, near, 2, 1, LANES), (cu_f1, 1, near, 2, 1), (cu_f3, 1, late, 2, 1)], held=True)
+    outs = place(
+        outs, [(cg_f1, 0, near, 2, 1, LANES), (cu_f1, 1, near, 2, 1, LANES), (cu_f3, 1, late, 2, 1)], held=True
+    )
     return (*outs, gathered_gain(gain))
 
 

time: 180 us -> 171 us (0.950)
  the two profiles are of different devices: /device:TPU:74 before, /device:TPU:0 now
where the time goes in v5:
time: 171 us; the launch traced here: 170 us
  waiting for transfers between devices  75.8 us (44%)
  starting transfers between devices  45.5 us (27%)
  Pallas kernels  22.7 us (13%)
  local copies, waits for them, and re-layouts  12.2 us (7%)
  matrix products  8.87 us (5%)
  other arithmetic  3.82 us (2%)
    ppermute x10, waiting for transfers between devices, down(): return lax.ppermute(v, 'y', DOWN)  41.1 us
    pallas_call x8, Pallas kernels, place(): pl.pallas_call(kernel, out_shape=shapes, in_specs=[pl.BlockSpec(memory_sp...  22.7 us
    ppermute x3, waiting for transfers between devices, gathered_gain(): part = lax.ppermute(x, 'y', [(i, (i + shift) % 4) for i in range(4)])  17.9 us
    ppermute x10, starting transfers between devices, down(): return lax.ppermute(v, 'y', DOWN)  14.8 us
    ppermute x10, starting transfers between devices, across(): return lax.ppermute(v, 'xl', SWAP)  12.2 us
    dot_general x5, matrix products, merged(): lax.dot_general(low, high, (((0,), (0,)), ((), ())), preferred_element_ty...  8.87 us
    ppermute x4, starting transfers between devices, doubled(): other = lax.ppermute(x, axis, pairs)  8.13 us
    ppermute x4, waiting for transfers between devices, doubled(): other = lax.ppermute(x, axis, pairs)  7.17 us
  transfers between devices with their start and end apart: 35, of which 17 were waited for; matrix products, arithmetic and copies ran while one was open for 13% of the time, Pallas kernels for 12%

profile of v5, /device:TPU:0, one launch (start us, length us, event | category | flops | bytes accessed | tf_op | source)
XLA Modules:
  0.0 169.9 jit_solution(13323525560024617702)
XLA Ops:
  9.1 2.0 %collective-permute-start.28 = (bf16[2,32]{1,0:T(2,128)(2,1)S(1)}, bf16[2,32]{1,0:T(2,128)(2,1)S(1)}, u32[]{:S(2)}, u32[]{:S(2)}) collective-permute-start(bf16[2,32]{1,0:T(2,128)(2,1)S(1)} %broadcast_select_fusion.4), channel_id=1, source_target_pairs={{0,4},{1,5},{2,6},{3,7},{4,0},{5,1},{6,2},{7,3},{8,12},{9,13},{10,... | collective-permute-start | bytes 392 | tf_op jit(solution)/shard_map/ppermute | solution.py:100
  12.7 3.9 %collective-permute-start.29 = (bf16[4,32]{1,0:T(4,128)(2,1)S(1)}, bf16[4,32]{1,0:T(4,128)(2,1)S(1)}, u32[]{:S(2)}, u32[]{:S(2)}) collective-permute-start(bf16[4,32]{1,0:T(4,128)(2,1)S(1)} %maximum_select_fusion.4), channel_id=1, source_target_pairs={{0,8},{1,9},{2,10},{3,11},{4,12},{5,13},{6,14},{7,15},{8,0},{9,1},... | collective-permute-start | bytes 776 | tf_op jit(solution)/shard_map/ppermute | solution.py:100
  18.3 2.2 %collective-permute-start.30 = (bf16[8,32]{1,0:T(8,128)(2,1)S(1)}, bf16[8,32]{1,0:T(8,128)(2,1)}, u32[]{:S(2)}, u32[]{:S(2)}) collective-permute-start(bf16[8,32]{1,0:T(8,128)(2,1)S(1)} %maximum_select_fusion.2), channel_id=1, source_target_pairs={{0,18},{1,19},{2,16},{3,17},{4,22},{5,23},{6,20},{7,21},{8,26},{9,... | collective-permute-start | bytes 1544 | tf_op jit(solution)/shard_map/ppermute | solution.py:100
  20.4 2.8 %collective-permute-done.30 = bf16[8,32]{1,0:T(8,128)(2,1)} collective-permute-done((bf16[8,32]{1,0:T(8,128)(2,1)S(1)}, bf16[8,32]{1,0:T(8,128)(2,1)}, u32[]{:S(2)}, u32[]{:S(2)}) %collective-permute-start.30) | collective-permute-done | bytes 544 | tf_op jit(solution)/shard_map/ppermute | solution.py:100
  28.8 17.8 %collective-permute-done.32 = bf16[16,32]{1,0:T(8,128)(2,1)S(1)} collective-permute-done((bf16[16,32]{1,0:T(8,128)(2,1)S(1)}, bf16[16,32]{1,0:T(8,128)(2,1)S(1)}, u32[]{:S(2)}, u32[]{:S(2)}) %collective-permute-start.32) | collective-permute-done | bytes 1056 | tf_op jit(solution)/shard_map/ppermute | solution.py:117
  52.1 3.0 %collective-permute-done.8 = bf16[32,512]{1,0:T(8,128)(2,1)S(1)} collective-permute-done((bf16[32,512]{1,0:T(8,128)(2,1)}, bf16[32,512]{1,0:T(8,128)(2,1)S(1)}, u32[]{:S(2)}, u32[]{:S(2)}) %collective-permute-start.8) | collective-permute-done | bytes 32800 | tf_op jit(solution)/shard_map/ppermute | solution.py:134
  57.2 1.9 %collective-permute-start.26 = (bf16[512,896]{1,0:T(8,128)(2,1)S(1)}, bf16[512,896]{1,0:T(8,128)(2,1)S(1)}, u32[]{:S(2)}, u32[]{:S(2)}) collective-permute-start(bf16[512,896]{1,0:T(8,128)(2,1)S(1)} %add_convert_fusion.refs_0_), channel_id=1, source_target_pairs={{0,96},{32,0},{64,32},{96,64},{1,97},{33,1},{65,33},{97,65},{2,98}... | collective-permute-start | bytes 2752520 | tf_op jit(solution)/shard_map/ppermute | solution.py:134
  60.9 3.5 %collective-permute-done.1 = bf16[32,512]{1,0:T(8,128)(2,1)S(1)} collective-permute-done((bf16[32,512]{1,0:T(8,128)(2,1)}, bf16[32,512]{1,0:T(8,128)(2,1)S(1)}, u32[]{:S(2)}, u32[]{:S(2)}) %collective-permute-start.1) | collective-permute-done | bytes 32800 | tf_op jit(solution)/shard_map/ppermute | solution.py:131
  65.9 2.6 %add_convert_fusion.4.refs_0_ = bf16[512,896]{1,0:T(8,128)(2,1)} fusion(bf16[512,896]{1,0:T(8,128)(2,1)} %collective-permute-done, bf16[32,512]{1,0:T(8,128)(2,1)S(1)} %collective-permute-done.1, bf16[32,896]{1,0:T(8,128)(2,1)S(1)} %copy-done), kind=kOutput, calls=%fused_computation.4 | convolution fusion | flops 30736384 | bytes 1925120 | tf_op jit(solution)/shard_map/dot_general | solution.py:19
  68.5 6.4 %collective-permute-done.7 = bf16[512,896]{1,0:T(8,128)(2,1)S(1)} collective-permute-done((bf16[512,896]{1,0:T(8,128)(2,1)}, bf16[512,896]{1,0:T(8,128)(2,1)S(1)}, u32[]{:S(2)}, u32[]{:S(2)}) %collective-permute-start.7) | collective-permute-done | bytes 917536 | tf_op jit(solution)/shard_map/ppermute | solution.py:134
  76.0 2.2 %collective-permute-done.25.refs_1_ = bf16[512,896]{1,0:T(8,128)(2,1)S(1)} collective-permute-done((bf16[512,896]{1,0:T(8,128)(2,1)S(1)}, bf16[512,896]{1,0:T(8,128)(2,1)S(1)}, u32[]{:S(2)}, u32[]{:S(2)}) %collective-permute-start.25) | collective-permute-done | bytes 917536 | tf_op jit(solution)/shard_map/ppermute | solution.py:137
  80.2 14.3 %collective-permute-done.26.refs_2_ = bf16[512,896]{1,0:T(8,128)(2,1)S(1)} collective-permute-done((bf16[512,896]{1,0:T(8,128)(2,1)S(1)}, bf16[512,896]{1,0:T(8,128)(2,1)S(1)}, u32[]{:S(2)}, u32[]{:S(2)}) %collective-permute-start.26) | collective-permute-done | bytes 917536 | tf_op jit(solution)/shard_map/ppermute | solution.py:134
  97.1 3.1 %collective-permute-start.24 = (bf16[512,896]{1,0:T(8,128)(2,1)}, bf16[512,896]{1,0:T(8,128)(2,1)}, u32[]{:S(2)}, u32[]{:S(2)}) collective-permute-start(bf16[512,896]{1,0:T(8,128)(2,1)} %add_convert_fusion.2.refs_2_), channel_id=1, source_target_pairs={{0,96},{32,0},{64,32},{96,64},{1,97},{33,1},{65,33},{97,65},{2,98}... | collective-permute-start | bytes 2752520 | tf_op jit(solution)/shard_map/ppermute | solution.py:134
  100.2 2.5 %shard_map.103 = (bf16[896,4096]{1,0:T(8,128)(2,1)}, bf16[896,4096]{1,0:T(8,128)(2,1)}) custom-call(bf16[512,896]{1,0:T(8,128)(2,1)S(1)} %add_convert_fusion.refs_0_, bf16[512,896]{1,0:T(8,128)(2,1)S(1)} %add_convert_fusion.3.refs_1_), custom_call_target="tpu_custom_call" | custom-call | bytes 3670016 | tf_op jit(solution)/shard_map/pallas_call | solution.py:81
  103.5 10.8 %collective-permute-done.17.refs_1_ = bf16[512,896]{1,0:T(8,128)(2,1)} collective-permute-done((bf16[512,896]{1,0:T(8,128)(2,1)S(1)}, bf16[512,896]{1,0:T(8,128)(2,1)}, u32[]{:S(2)}, u32[]{:S(2)}) %collective-permute-start.17) | collective-permute-done | bytes 917536 | tf_op jit(solution)/shard_map/ppermute | solution.py:134
  123.6 2.4 %collective-permute-start.18 = (bf16[512,256]{1,0:T(8,128)(2,1)S(1)}, bf16[512,256]{1,0:T(8,128)(2,1)S(1)}, u32[]{:S(2)}, u32[]{:S(2)}) collective-permute-start(bf16[512,256]{1,0:T(8,128)(2,1)S(1)} %slice.55), channel_id=1, source_target_pairs={{0,96},{32,0},{64,32},{96,64},{1,97},{33,1},{65,33},{97,65},{2,98}... | collective-permute-start | bytes 786440 | tf_op jit(solution)/shard_map/ppermute | solution.py:134
  128.3 5.5 %collective-permute-done.24.refs_4_ = bf16[512,896]{1,0:T(8,128)(2,1)} collective-permute-done((bf16[512,896]{1,0:T(8,128)(2,1)}, bf16[512,896]{1,0:T(8,128)(2,1)}, u32[]{:S(2)}, u32[]{:S(2)}) %collective-permute-start.24) | collective-permute-done | bytes 917536 | tf_op jit(solution)/shard_map/ppermute | solution.py:134
  133.8 2.0 %collective-permute-start.20 = (bf16[128,128]{1,0:T(8,128)(2,1)S(1)}, bf16[128,128]{1,0:T(8,128)(2,1)S(1)}, u32[]{:S(2)}, u32[]{:S(2)}) collective-permute-start(bf16[128,128]{1,0:T(8,128)(2,1)S(1)} %slice.57), channel_id=1, source_target_pairs={{0,96},{32,0},{64,32},{96,64},{1,97},{33,1},{65,33},{97,65},{2,98}... | collective-permute-start | bytes 98312 | tf_op jit(solution)/shard_map/ppermute | solution.py:134
  142.6 3.1 %collective-permute-start.14 = (bf16[512,128]{1,0:T(8,128)(2,1)}, bf16[512,128]{1,0:T(8,128)(2,1)}, u32[]{:S(2)}, u32[]{:S(2)}) collective-permute-start(bf16[512,128]{1,0:T(8,128)(2,1)} %get-tuple-element.37), channel_id=1, source_target_pairs={{0,96},{32,0},{64,32},{96,64},{1,97},{33,1},{65,33},{97,65},{2,98}... | collective-permute-start | bytes 393224 | tf_op jit(solution)/shard_map/ppermute | solution.py:134
  149.3 3.9 %shard_map.104 = (bf16[896,4096]{1,0:T(8,128)(2,1)}, bf16[896,4096]{1,0:T(8,128)(2,1)}) custom-call(bf16[512,896]{1,0:T(8,128)(2,1)} %add_convert_fusion.4.refs_0_, bf16[512,896]{1,0:T(8,128)(2,1)S(1)} %add_convert_fusion.1.refs_1_, bf16[512,896]{1,0:T(8,128)(2,1)} %add_convert_fusion.2.refs_2_, ...), custom_call_target="tpu_custom_call", output_to_operand_aliasing={{0}: (3, {}), {1}: (4, {})} | custom-call | bytes 5505024 | tf_op jit(solution)/shard_map/pallas_call | solution.py:81
  153.3 3.4 %shard_map.105 = (bf16[896,4096]{1,0:T(8,128)(2,1)}, bf16[896,4096]{1,0:T(8,128)(2,1)}) custom-call(bf16[512,896]{1,0:T(8,128)(2,1)S(1)} %collective-permute-done.4.refs_0_, bf16[512,896]{1,0:T(8,128)(2,1)S(1)} %copy-done.2, bf16[512,896]{1,0:T(8,128)(2,1)S(1)} %copy-done.4, ...), custom_call_target="tpu_custom_call", output_to_operand_aliasing={{0}: (3, {}), {1}: (4, {})} | custom-call | bytes 5505024 | tf_op jit(solution)/shard_map/pallas_call | solution.py:81
  156.7 3.9 %shard_map.106 = (bf16[896,4096]{1,0:T(8,128)(2,1)}, bf16[896,4096]{1,0:T(8,128)(2,1)}) custom-call(bf16[512,896]{1,0:T(8,128)(2,1)} %collective-permute-done.2.refs_0_, bf16[512,896]{1,0:T(8,128)(2,1)} %collective-permute-done.17.refs_1_, bf16[512,896]{1,0:T(8,128)(2,1)} %collective-permute-done.9.refs_2_, ...), custom_call_target="tpu_custom_call", output_to_operand_aliasing={{0}: (3, {}), {1}: (4, {})} | custom-call | bytes 5505024 | tf_op jit(solution)/shard_map/pallas_call | solution.py:81
  160.6 3.9 %shard_map.107 = (bf16[896,4096]{1,0:T(8,128)(2,1)}, bf16[896,4096]{1,0:T(8,128)(2,1)}) custom-call(bf16[512,512]{1,0:T(8,128)(2,1)S(1)} %collective-permute-done.12.refs_0_, bf16[512,128]{1,0:T(8,128)(2,1)S(1)} %collective-permute-done.5.refs_1_, bf16[512,256]{1,0:T(8,128)(2,1)S(1)} %copy-done.8, ...), custom_call_target="tpu_custom_call", output_to_operand_aliasing={{0}: (5, {}), {1}: (6, {})} | custom-call | bytes 5505024 | tf_op jit(solution)/shard_map/pallas_call | solution.py:81
  165.7 2.2 %shard_map.109 = (bf16[896,4096]{1,0:T(8,128)(2,1)}, bf16[896,4096]{1,0:T(8,128)(2,1)}) custom-call(bf16[512,256]{1,0:T(8,128)(2,1)} %collective-permute-done.11.refs_0_, bf16[512,512]{1,0:T(8,128)(2,1)S(1)} %copy-done.6, bf16[512,128]{1,0:T(8,128)(2,1)} %collective-permute-done.14.refs_2_, ...), custom_call_target="tpu_custom_call", output_to_operand_aliasing={{0}: (3, {}), {1}: (4, {})} | custom-call | bytes 1835008 | tf_op jit(solution)/shard_map/pallas_call | solution.py:81
  (121 shorter events, 59.7 us)
Async XLA Ops:
  0.7 56.5 %collective-permute-start.15 = (bf16[512,896]{1,0:T(8,128)(2,1)}, bf16[512,896]{1,0:T(8,128)(2,1)S(1)}, u32[]{:S(2)}, u32[]{:S(2)}) collective-permute-start(bf16[512,896]{1,0:T(8,128)(2,1)} %param.8), channel_id=1, source_target_pairs={{0,16},{16,0},{1,17},{17,1},{2,18},{18,2},{3,19},{19,3},{4,20},{20... | collective-permute-start | bytes 2752520 | tf_op jit(solution)/shard_map/ppermute | solution.py:137
  2.3 62.1 %collective-permute-start = (bf16[512,896]{1,0:T(8,128)(2,1)}, bf16[512,896]{1,0:T(8,128)(2,1)}, u32[]{:S(2)}, u32[]{:S(2)}) collective-permute-start(bf16[512,896]{1,0:T(8,128)(2,1)} %param.8), channel_id=1, source_target_pairs={{0,32},{32,64},{64,96},{96,0},{1,33},{33,65},{65,97},{97,1},{2,34}... | collective-permute-start | bytes 2752520 | tf_op jit(solution)/shard_map/ppermute | solution.py:131
  5.6 53.5 %collective-permute-start.4 = (bf16[512,896]{1,0:T(8,128)(2,1)S(1)}, bf16[512,896]{1,0:T(8,128)(2,1)S(1)}, u32[]{:S(2)}, u32[]{:S(2)}) collective-permute-start(bf16[512,896]{1,0:T(8,128)(2,1)S(1)} %add_convert_fusion.3.refs_1_), channel_id=1, source_target_pairs={{0,32},{32,64},{64,96},{96,0},{1,33},{33,65},{65,97},{97,1},{2,34}... | collective-permute-start | bytes 2752520 | tf_op jit(solution)/shard_map/ppermute | solution.py:131
  25.6 21.0 %collective-permute-start.32 = (bf16[16,32]{1,0:T(8,128)(2,1)S(1)}, bf16[16,32]{1,0:T(8,128)(2,1)S(1)}, u32[]{:S(2)}, u32[]{:S(2)}) collective-permute-start(bf16[16,32]{1,0:T(8,128)(2,1)S(1)} %maximum_select_fusion), channel_id=1, source_target_pairs={{0,64},{32,96},{64,0},{96,32},{1,65},{33,97},{65,1},{97,33},{2,66}... | collective-permute-start | bytes 3080 | tf_op jit(solution)/shard_map/ppermute | solution.py:117
  27.5 19.1 %collective-permute-start.33 = (bf16[16,32]{1,0:T(8,128)(2,1)S(1)}, bf16[16,32]{1,0:T(8,128)(2,1)S(1)}, u32[]{:S(2)}, u32[]{:S(2)}) collective-permute-start(bf16[16,32]{1,0:T(8,128)(2,1)S(1)} %maximum_select_fusion), channel_id=1, source_target_pairs={{0,32},{32,64},{64,96},{96,0},{1,33},{33,65},{65,97},{97,1},{2,34}... | collective-permute-start | bytes 3080 | tf_op jit(solution)/shard_map/ppermute | solution.py:117
  51.5 23.4 %collective-permute-start.7 = (bf16[512,896]{1,0:T(8,128)(2,1)}, bf16[512,896]{1,0:T(8,128)(2,1)S(1)}, u32[]{:S(2)}, u32[]{:S(2)}) collective-permute-start(bf16[512,896]{1,0:T(8,128)(2,1)} %param.11), channel_id=1, source_target_pairs={{0,96},{32,0},{64,32},{96,64},{1,97},{33,1},{65,33},{97,65},{2,98}... | collective-permute-start | bytes 2752520 | tf_op jit(solution)/shard_map/ppermute | solution.py:134
  55.0 23.2 %collective-permute-start.25 = (bf16[512,896]{1,0:T(8,128)(2,1)S(1)}, bf16[512,896]{1,0:T(8,128)(2,1)S(1)}, u32[]{:S(2)}, u32[]{:S(2)}) collective-permute-start(bf16[512,896]{1,0:T(8,128)(2,1)S(1)} %add_convert_fusion.3.refs_1_), channel_id=1, source_target_pairs={{0,16},{16,0},{1,17},{17,1},{2,18},{18,2},{3,19},{19,3},{4,20},{20... | collective-permute-start | bytes 2752520 | tf_op jit(solution)/shard_map/ppermute | solution.py:137
  57.2 37.4 %collective-permute-start.26 = (bf16[512,896]{1,0:T(8,128)(2,1)S(1)}, bf16[512,896]{1,0:T(8,128)(2,1)S(1)}, u32[]{:S(2)}, u32[]{:S(2)}) collective-permute-start(bf16[512,896]{1,0:T(8,128)(2,1)S(1)} %add_convert_fusion.refs_0_), channel_id=1, source_target_pairs={{0,96},{32,0},{64,32},{96,64},{1,97},{33,1},{65,33},{97,65},{2,98}... | collective-permute-start | bytes 2752520 | tf_op jit(solution)/shard_map/ppermute | solution.py:134
  64.4 49.9 %collective-permute-start.17 = (bf16[512,896]{1,0:T(8,128)(2,1)S(1)}, bf16[512,896]{1,0:T(8,128)(2,1)}, u32[]{:S(2)}, u32[]{:S(2)}) collective-permute-start(bf16[512,896]{1,0:T(8,128)(2,1)S(1)} %add_convert_fusion.1.refs_1_), channel_id=1, source_target_pairs={{0,96},{32,0},{64,32},{96,64},{1,97},{33,1},{65,33},{97,65},{2,98}... | collective-permute-start | bytes 2752520 | tf_op jit(solution)/shard_map/ppermute | solution.py:134
  64.4 32.7 %collective-permute-start.12 = (bf16[512,512]{1,0:T(8,128)(2,1)S(1)}, bf16[512,512]{1,0:T(8,128)(2,1)S(1)}, u32[]{:S(2)}, u32[]{:S(2)}) collective-permute-start(bf16[512,512]{1,0:T(8,128)(2,1)S(1)} %slice.53), channel_id=1, source_target_pairs={{0,16},{16,0},{1,17},{17,1},{2,18},{18,2},{3,19},{19,3},{4,20},{20... | collective-permute-start | bytes 1572872 | tf_op jit(solution)/shard_map/ppermute | solution.py:137
  74.9 41.6 %collective-permute-start.2 = (bf16[512,896]{1,0:T(8,128)(2,1)}, bf16[512,896]{1,0:T(8,128)(2,1)}, u32[]{:S(2)}, u32[]{:S(2)}) collective-permute-start(bf16[512,896]{1,0:T(8,128)(2,1)} %add_convert_fusion.4.refs_0_), channel_id=1, source_target_pairs={{0,32},{32,64},{64,96},{96,0},{1,33},{33,65},{65,97},{97,1},{2,34}... | collective-permute-start | bytes 2752520 | tf_op jit(solution)/shard_map/ppermute | solution.py:131
  78.2 18.8 %collective-permute-start.5 = (bf16[512,128]{1,0:T(8,128)(2,1)S(1)}, bf16[512,128]{1,0:T(8,128)(2,1)S(1)}, u32[]{:S(2)}, u32[]{:S(2)}) collective-permute-start(bf16[512,128]{1,0:T(8,128)(2,1)S(1)} %slice.49), channel_id=1, source_target_pairs={{0,16},{16,0},{1,17},{17,1},{2,18},{18,2},{3,19},{19,3},{4,20},{20... | collective-permute-start | bytes 393224 | tf_op jit(solution)/shard_map/ppermute | solution.py:137
  95.5 28.1 %collective-permute-start.9 = (bf16[512,896]{1,0:T(8,128)(2,1)}, bf16[512,896]{1,0:T(8,128)(2,1)}, u32[]{:S(2)}, u32[]{:S(2)}) collective-permute-start(bf16[512,896]{1,0:T(8,128)(2,1)} %add_convert_fusion.2.refs_2_), channel_id=1, source_target_pairs={{0,16},{16,0},{1,17},{17,1},{2,18},{18,2},{3,19},{19,3},{4,20},{20... | collective-permute-start | bytes 2752520 | tf_op jit(solution)/shard_map/ppermute | solution.py:137
  97.0 28.9 %collective-permute-start.23 = (bf16[512,896]{1,0:T(8,128)(2,1)S(1)}, bf16[512,896]{1,0:T(8,128)(2,1)}, u32[]{:S(2)}, u32[]{:S(2)}) collective-permute-start(bf16[512,896]{1,0:T(8,128)(2,1)S(1)} %add_convert_fusion.1.refs_1_), channel_id=1, source_target_pairs={{0,32},{32,64},{64,96},{96,0},{1,33},{33,65},{65,97},{97,1},{2,34}... | collective-permute-start | bytes 2752520 | tf_op jit(solution)/shard_map/ppermute | solution.py:131
  97.1 36.7 %collective-permute-start.24 = (bf16[512,896]{1,0:T(8,128)(2,1)}, bf16[512,896]{1,0:T(8,128)(2,1)}, u32[]{:S(2)}, u32[]{:S(2)}) collective-permute-start(bf16[512,896]{1,0:T(8,128)(2,1)} %add_convert_fusion.2.refs_2_), channel_id=1, source_target_pairs={{0,96},{32,0},{64,32},{96,64},{1,97},{33,1},{65,33},{97,65},{2,98}... | collective-permute-start | bytes 2752520 | tf_op jit(solution)/shard_map/ppermute | solution.py:134
  116.5 25.2 %collective-permute-start.13 = (bf16[512,512]{1,0:T(8,128)(2,1)S(1)}, bf16[512,512]{1,0:T(8,128)(2,1)S(1)}, u32[]{:S(2)}, u32[]{:S(2)}) collective-permute-start(bf16[512,512]{1,0:T(8,128)(2,1)S(1)} %collective-permute-done.12.refs_0_), channel_id=1, source_target_pairs={{0,32},{32,64},{64,96},{96,0},{1,33},{33,65},{65,97},{97,1},{2,34}... | collective-permute-start | bytes 1572872 | tf_op jit(solution)/shard_map/ppermute | solution.py:131
  122.1 23.6 %collective-permute-start.21 = (bf16[512,256]{1,0:T(8,128)(2,1)S(1)}, bf16[512,256]{1,0:T(8,128)(2,1)S(1)}, u32[]{:S(2)}, u32[]{:S(2)}) collective-permute-start(bf16[512,256]{1,0:T(8,128)(2,1)S(1)} %get-tuple-element.35), channel_id=1, source_target_pairs={{0,16},{16,0},{1,17},{17,1},{2,18},{18,2},{3,19},{19,3},{4,20},{20... | collective-permute-start | bytes 786440 | tf_op jit(solution)/shard_map/ppermute | solution.py:137
  123.6 23.7 %collective-permute-start.18 = (bf16[512,256]{1,0:T(8,128)(2,1)S(1)}, bf16[512,256]{1,0:T(8,128)(2,1)S(1)}, u32[]{:S(2)}, u32[]{:S(2)}) collective-permute-start(bf16[512,256]{1,0:T(8,128)(2,1)S(1)} %slice.55), channel_id=1, source_target_pairs={{0,96},{32,0},{64,32},{96,64},{1,97},{33,1},{65,33},{97,65},{2,98}... | collective-permute-start | bytes 786440 | tf_op jit(solution)/shard_map/ppermute | solution.py:134
  125.9 11.0 %collective-permute-start.19 = (bf16[128,128]{1,0:T(8,128)(2,1)S(1)}, bf16[128,128]{1,0:T(8,128)(2,1)S(1)}, u32[]{:S(2)}, u32[]{:S(2)}) collective-permute-start(bf16[128,128]{1,0:T(8,128)(2,1)S(1)} %slice.56), channel_id=1, source_target_pairs={{0,96},{32,0},{64,32},{96,64},{1,97},{33,1},{65,33},{97,65},{2,98}... | collective-permute-start | bytes 98312 | tf_op jit(solution)/shard_map/ppermute | solution.py:134
  136.9 28.7 %collective-permute-start.11 = (bf16[512,256]{1,0:T(8,128)(2,1)}, bf16[512,256]{1,0:T(8,128)(2,1)}, u32[]{:S(2)}, u32[]{:S(2)}) collective-permute-start(bf16[512,256]{1,0:T(8,128)(2,1)} %get-tuple-element.36), channel_id=1, source_target_pairs={{0,16},{16,0},{1,17},{17,1},{2,18},{18,2},{3,19},{19,3},{4,20},{20... | collective-permute-start | bytes 786440 | tf_op jit(solution)/shard_map/ppermute | solution.py:137
  141.6 26.3 %collective-permute-start.6 = (bf16[384,128]{1,0:T(8,128)(2,1)}, bf16[384,128]{1,0:T(8,128)(2,1)}, u32[]{:S(2)}, u32[]{:S(2)}) collective-permute-start(bf16[384,128]{1,0:T(8,128)(2,1)} %slice.50), channel_id=1, source_target_pairs={{0,32},{32,64},{64,96},{96,0},{1,33},{33,65},{65,97},{97,1},{2,34}... | collective-permute-start | bytes 294920 | tf_op jit(solution)/shard_map/ppermute | solution.py:131
  142.6 23.0 %collective-permute-start.14 = (bf16[512,128]{1,0:T(8,128)(2,1)}, bf16[512,128]{1,0:T(8,128)(2,1)}, u32[]{:S(2)}, u32[]{:S(2)}) collective-permute-start(bf16[512,128]{1,0:T(8,128)(2,1)} %get-tuple-element.37), channel_id=1, source_target_pairs={{0,96},{32,0},{64,32},{96,64},{1,97},{33,1},{65,33},{97,65},{2,98}... | collective-permute-start | bytes 393224 | tf_op jit(solution)/shard_map/ppermute | solution.py:134
  146.4 21.5 %collective-permute-start.10 = (bf16[512,128]{1,0:T(8,128)(2,1)}, bf16[512,128]{1,0:T(8,128)(2,1)}, u32[]{:S(2)}, u32[]{:S(2)}) collective-permute-start(bf16[512,128]{1,0:T(8,128)(2,1)} %get-tuple-element.38), channel_id=1, source_target_pairs={{0,96},{32,0},{64,32},{96,64},{1,97},{33,1},{65,33},{97,65},{2,98}... | collective-permute-start | bytes 393224 | tf_op jit(solution)/shard_map/ppermute | solution.py:134
  148.0 19.9 %collective-permute-start.3 = (bf16[384,128]{1,0:T(8,128)(2,1)}, bf16[384,128]{1,0:T(8,128)(2,1)}, u32[]{:S(2)}, u32[]{:S(2)}) collective-permute-start(bf16[384,128]{1,0:T(8,128)(2,1)} %slice.48), channel_id=1, source_target_pairs={{0,16},{16,0},{1,17},{17,1},{2,18},{18,2},{3,19},{19,3},{4,20},{20... | collective-permute-start | bytes 294920 | tf_op jit(solution)/shard_map/ppermute | solution.py:137
  (30 other events, 324.3 us)

commit v6 on v5

--- a/solution.py
+++ b/solution.py
@@ -51,9 +51,12 @@
                 turned[k].at[c], out_refs[parts[k][1]].at[rows, columns], out_sem.at[k, c]
             )
 
-        for k in range(count):
-            for c in range(0 if held else steps[k]):
+        for k in range(0 if held else count):
+
+            @pl.loop(0, steps[k])
+            def _(c):
                 load(k, c).start()
+
         for k in range(count):
 
             def step(c):
@@ -71,8 +74,15 @@
                 pl.loop(0, steps[k])(step)
 
         for k in range(count):
-            for c in range(steps[k]):
-                save(k, c).wait()
+            if held:
+                for c in range(steps[k]):
+                    save(k, c).wait()
+            else:
+
+                @pl.loop(0, steps[k])
+                def _(c):
+                    save(k, c).wait()
+
 
     shapes = [jax.ShapeDtypeStruct(o.shape, o.dtype) for o in outs]
     any_spec = pl.BlockSpec(memory_space=pl.ANY)
@@ -151,7 +161,9 @@
     first, near, mid, late = width * 2 // 7, width * 4 // 7, width * 5 // 7, width * 6 // 7
     cu_m0, cu_m1, cu_m2 = (across(u_m[:, :near]), across(u_m[:, near:mid]), across(u_m[:, mid:]))
     cg_m, u_f = up(g_x), down(u_p)
-    cg_f0, cg_f4, cg_f1 = (across(g_f[:, :first]), across(g_f[:, first:near]), across(g_f[LANES:, near:mid]))
+    cg_f0, cg_f4, cg_f1 = (
+        across(g_f[:, :first]), across(g_f[:, first:near]), across(g_f[LANES:, near:mid])
+    )
     cg_f2, cg_f3 = down(cg_p[:, mid:]), down(cg_p[:LANES, near:mid])
     cu_f2, cu_f3 = down(cu_p[:, mid:late]), down(cu_p[:, late:])
     cu_f4 = down(cu_p[:LANES, near:mid])
@@ -173,9 +185,13 @@
         ],
     )
     outs = place(outs, [(cg_f2, 0, mid, 2, 1), (cg_f3, 0, near, 2, 1), (cu_f4, 1, near, 2, 1), (cg_f0, 0, 0, 2, 1)], held=True)
-    outs = place(outs, [(cg_f4, 0, first, 2, 1), (cu_f0, 1, 0, 2, 1), (cu_f2, 1, mid, 2, 1)], held=True)
     outs = place(
-        outs, [(cg_f1, 0, near, 2, 1, LANES), (cu_f1, 1, near, 2, 1, LANES), (cu_f3, 1, late, 2, 1)], held=True
+        outs, [(cg_f4, 0, first, 2, 1), (cu_f0, 1, 0, 2, 1), (cu_f2, 1, mid, 2, 1)], held=True
+    )
+    outs = place(
+        outs,
+        [(cg_f1, 0, near, 2, 1, LANES), (cu_f1, 1, near, 2, 1, LANES), (cu_f3, 1, late, 2, 1)],
+        held=True,
     )
     return (*outs, gathered_gain(gain))
 

time: 171 us -> 171 us (level)
  no operation moved by 1% of the time
where the time goes in v6:
time: 171 us; the launch traced here: 170 us
  waiting for transfers between devices  75.9 us (44%)
  starting transfers between devices  45.3 us (26%)
  Pallas kernels  22.9 us (13%)
  local copies, waits for them, and re-layouts  12.2 us (7%)
  matrix products  8.87 us (5%)
  other arithmetic  3.82 us (2%)
    ppermute x10, waiting for transfers between devices, down(): return lax.ppermute(v, 'y', DOWN)  41.2 us
    pallas_call x8, Pallas kernels, place(): pl.pallas_call(kernel, out_shape=shapes, in_specs=[pl.BlockSpec(memory_sp...  22.9 us
    ppermute x3, waiting for transfers between devices, gathered_gain(): part = lax.ppermute(x, 'y', [(i, (i + shift) % 4) for i in range(4)])  17.9 us
    ppermute x10, starting transfers between devices, down(): return lax.ppermute(v, 'y', DOWN)  14.6 us
    ppermute x10, starting transfers between devices, across(): return lax.ppermute(v, 'xl', SWAP)  12.2 us
    dot_general x5, matrix products, merged(): lax.dot_general(low, high, (((0,), (0,)), ((), ())), preferred_element_ty...  8.87 us
    ppermute x4, starting transfers between devices, doubled(): other = lax.ppermute(x, axis, pairs)  8.13 us
    ppermute x4, waiting for transfers between devices, doubled(): other = lax.ppermute(x, axis, pairs)  7.17 us
  transfers between devices with their start and end apart: 35, of which 17 were waited for; matrix products, arithmetic and copies ran while one was open for 13% of the time, Pallas kernels for 12%

profile of v6, /device:TPU:0, one launch (start us, length us, event | category | flops | bytes accessed | tf_op | source)
XLA Modules:
  0.0 170.0 jit_solution(7336500036137803371)
XLA Ops:
  9.1 2.0 %collective-permute-start.28 = (bf16[2,32]{1,0:T(2,128)(2,1)S(1)}, bf16[2,32]{1,0:T(2,128)(2,1)S(1)}, u32[]{:S(2)}, u32[]{:S(2)}) collective-permute-start(bf16[2,32]{1,0:T(2,128)(2,1)S(1)} %broadcast_select_fusion.4), channel_id=1, source_target_pairs={{0,4},{1,5},{2,6},{3,7},{4,0},{5,1},{6,2},{7,3},{8,12},{9,13},{10,... | collective-permute-start | bytes 392 | tf_op jit(solution)/shard_map/ppermute | solution.py:110
  12.7 3.9 %collective-permute-start.29 = (bf16[4,32]{1,0:T(4,128)(2,1)S(1)}, bf16[4,32]{1,0:T(4,128)(2,1)S(1)}, u32[]{:S(2)}, u32[]{:S(2)}) collective-permute-start(bf16[4,32]{1,0:T(4,128)(2,1)S(1)} %maximum_select_fusion.4), channel_id=1, source_target_pairs={{0,8},{1,9},{2,10},{3,11},{4,12},{5,13},{6,14},{7,15},{8,0},{9,1},... | collective-permute-start | bytes 776 | tf_op jit(solution)/shard_map/ppermute | solution.py:110
  18.3 2.2 %collective-permute-start.30 = (bf16[8,32]{1,0:T(8,128)(2,1)S(1)}, bf16[8,32]{1,0:T(8,128)(2,1)}, u32[]{:S(2)}, u32[]{:S(2)}) collective-permute-start(bf16[8,32]{1,0:T(8,128)(2,1)S(1)} %maximum_select_fusion.2), channel_id=1, source_target_pairs={{0,18},{1,19},{2,16},{3,17},{4,22},{5,23},{6,20},{7,21},{8,26},{9,... | collective-permute-start | bytes 1544 | tf_op jit(solution)/shard_map/ppermute | solution.py:110
  20.4 2.8 %collective-permute-done.30 = bf16[8,32]{1,0:T(8,128)(2,1)} collective-permute-done((bf16[8,32]{1,0:T(8,128)(2,1)S(1)}, bf16[8,32]{1,0:T(8,128)(2,1)}, u32[]{:S(2)}, u32[]{:S(2)}) %collective-permute-start.30) | collective-permute-done | bytes 544 | tf_op jit(solution)/shard_map/ppermute | solution.py:110
  28.8 17.8 %collective-permute-done.32 = bf16[16,32]{1,0:T(8,128)(2,1)S(1)} collective-permute-done((bf16[16,32]{1,0:T(8,128)(2,1)S(1)}, bf16[16,32]{1,0:T(8,128)(2,1)S(1)}, u32[]{:S(2)}, u32[]{:S(2)}) %collective-permute-start.32) | collective-permute-done | bytes 1056 | tf_op jit(solution)/shard_map/ppermute | solution.py:127
  52.1 3.0 %collective-permute-done.8 = bf16[32,512]{1,0:T(8,128)(2,1)S(1)} collective-permute-done((bf16[32,512]{1,0:T(8,128)(2,1)}, bf16[32,512]{1,0:T(8,128)(2,1)S(1)}, u32[]{:S(2)}, u32[]{:S(2)}) %collective-permute-start.8) | collective-permute-done | bytes 32800 | tf_op jit(solution)/shard_map/ppermute | solution.py:144
  57.2 1.9 %collective-permute-start.26 = (bf16[512,896]{1,0:T(8,128)(2,1)S(1)}, bf16[512,896]{1,0:T(8,128)(2,1)S(1)}, u32[]{:S(2)}, u32[]{:S(2)}) collective-permute-start(bf16[512,896]{1,0:T(8,128)(2,1)S(1)} %add_convert_fusion.refs_0_), channel_id=1, source_target_pairs={{0,96},{32,0},{64,32},{96,64},{1,97},{33,1},{65,33},{97,65},{2,98}... | collective-permute-start | bytes 2752520 | tf_op jit(solution)/shard_map/ppermute | solution.py:144
  60.9 3.5 %collective-permute-done.1 = bf16[32,512]{1,0:T(8,128)(2,1)S(1)} collective-permute-done((bf16[32,512]{1,0:T(8,128)(2,1)}, bf16[32,512]{1,0:T(8,128)(2,1)S(1)}, u32[]{:S(2)}, u32[]{:S(2)}) %collective-permute-start.1) | collective-permute-done | bytes 32800 | tf_op jit(solution)/shard_map/ppermute | solution.py:141
  65.9 2.6 %add_convert_fusion.4.refs_0_ = bf16[512,896]{1,0:T(8,128)(2,1)} fusion(bf16[512,896]{1,0:T(8,128)(2,1)} %collective-permute-done, bf16[32,512]{1,0:T(8,128)(2,1)S(1)} %collective-permute-done.1, bf16[32,896]{1,0:T(8,128)(2,1)S(1)} %copy-done), kind=kOutput, calls=%fused_computation.4 | convolution fusion | flops 30736384 | bytes 1925120 | tf_op jit(solution)/shard_map/dot_general | solution.py:19
  68.5 6.4 %collective-permute-done.7 = bf16[512,896]{1,0:T(8,128)(2,1)S(1)} collective-permute-done((bf16[512,896]{1,0:T(8,128)(2,1)}, bf16[512,896]{1,0:T(8,128)(2,1)S(1)}, u32[]{:S(2)}, u32[]{:S(2)}) %collective-permute-start.7) | collective-permute-done | bytes 917536 | tf_op jit(solution)/shard_map/ppermute | solution.py:144
  76.0 2.2 %collective-permute-done.25.refs_1_ = bf16[512,896]{1,0:T(8,128)(2,1)S(1)} collective-permute-done((bf16[512,896]{1,0:T(8,128)(2,1)S(1)}, bf16[512,896]{1,0:T(8,128)(2,1)S(1)}, u32[]{:S(2)}, u32[]{:S(2)}) %collective-permute-start.25) | collective-permute-done | bytes 917536 | tf_op jit(solution)/shard_map/ppermute | solution.py:147
  80.2 14.3 %collective-permute-done.26.refs_2_ = bf16[512,896]{1,0:T(8,128)(2,1)S(1)} collective-permute-done((bf16[512,896]{1,0:T(8,128)(2,1)S(1)}, bf16[512,896]{1,0:T(8,128)(2,1)S(1)}, u32[]{:S(2)}, u32[]{:S(2)}) %collective-permute-start.26) | collective-permute-done | bytes 917536 | tf_op jit(solution)/shard_map/ppermute | solution.py:144
  97.1 3.1 %collective-permute-start.24 = (bf16[512,896]{1,0:T(8,128)(2,1)}, bf16[512,896]{1,0:T(8,128)(2,1)}, u32[]{:S(2)}, u32[]{:S(2)}) collective-permute-start(bf16[512,896]{1,0:T(8,128)(2,1)} %add_convert_fusion.2.refs_2_), channel_id=1, source_target_pairs={{0,96},{32,0},{64,32},{96,64},{1,97},{33,1},{65,33},{97,65},{2,98}... | collective-permute-start | bytes 2752520 | tf_op jit(solution)/shard_map/ppermute | solution.py:144
  100.2 2.6 %shard_map.103 = (bf16[896,4096]{1,0:T(8,128)(2,1)}, bf16[896,4096]{1,0:T(8,128)(2,1)}) custom-call(bf16[512,896]{1,0:T(8,128)(2,1)S(1)} %add_convert_fusion.refs_0_, bf16[512,896]{1,0:T(8,128)(2,1)S(1)} %add_convert_fusion.3.refs_1_), custom_call_target="tpu_custom_call" | custom-call | bytes 3670016 | tf_op jit(solution)/shard_map/pallas_call | solution.py:91
  103.6 10.7 %collective-permute-done.17.refs_1_ = bf16[512,896]{1,0:T(8,128)(2,1)} collective-permute-done((bf16[512,896]{1,0:T(8,128)(2,1)S(1)}, bf16[512,896]{1,0:T(8,128)(2,1)}, u32[]{:S(2)}, u32[]{:S(2)}) %collective-permute-start.17) | collective-permute-done | bytes 917536 | tf_op jit(solution)/shard_map/ppermute | solution.py:144
  123.6 2.4 %collective-permute-start.18 = (bf16[512,256]{1,0:T(8,128)(2,1)S(1)}, bf16[512,256]{1,0:T(8,128)(2,1)S(1)}, u32[]{:S(2)}, u32[]{:S(2)}) collective-permute-start(bf16[512,256]{1,0:T(8,128)(2,1)S(1)} %slice.55), channel_id=1, source_target_pairs={{0,96},{32,0},{64,32},{96,64},{1,97},{33,1},{65,33},{97,65},{2,98}... | collective-permute-start | bytes 786440 | tf_op jit(solution)/shard_map/ppermute | solution.py:144
  128.1 5.7 %collective-permute-done.24.refs_4_ = bf16[512,896]{1,0:T(8,128)(2,1)} collective-permute-done((bf16[512,896]{1,0:T(8,128)(2,1)}, bf16[512,896]{1,0:T(8,128)(2,1)}, u32[]{:S(2)}, u32[]{:S(2)}) %collective-permute-start.24) | collective-permute-done | bytes 917536 | tf_op jit(solution)/shard_map/ppermute | solution.py:144
  133.8 2.0 %collective-permute-start.20 = (bf16[128,128]{1,0:T(8,128)(2,1)S(1)}, bf16[128,128]{1,0:T(8,128)(2,1)S(1)}, u32[]{:S(2)}, u32[]{:S(2)}) collective-permute-start(bf16[128,128]{1,0:T(8,128)(2,1)S(1)} %slice.57), channel_id=1, source_target_pairs={{0,96},{32,0},{64,32},{96,64},{1,97},{33,1},{65,33},{97,65},{2,98}... | collective-permute-start | bytes 98312 | tf_op jit(solution)/shard_map/ppermute | solution.py:144
  142.6 3.1 %collective-permute-start.14 = (bf16[512,128]{1,0:T(8,128)(2,1)}, bf16[512,128]{1,0:T(8,128)(2,1)}, u32[]{:S(2)}, u32[]{:S(2)}) collective-permute-start(bf16[512,128]{1,0:T(8,128)(2,1)} %get-tuple-element.37), channel_id=1, source_target_pairs={{0,96},{32,0},{64,32},{96,64},{1,97},{33,1},{65,33},{97,65},{2,98}... | collective-permute-start | bytes 393224 | tf_op jit(solution)/shard_map/ppermute | solution.py:144
  149.3 3.9 %shard_map.104 = (bf16[896,4096]{1,0:T(8,128)(2,1)}, bf16[896,4096]{1,0:T(8,128)(2,1)}) custom-call(bf16[512,896]{1,0:T(8,128)(2,1)} %add_convert_fusion.4.refs_0_, bf16[512,896]{1,0:T(8,128)(2,1)S(1)} %add_convert_fusion.1.refs_1_, bf16[512,896]{1,0:T(8,128)(2,1)} %add_convert_fusion.2.refs_2_, ...), custom_call_target="tpu_custom_call", output_to_operand_aliasing={{0}: (3, {}), {1}: (4, {})} | custom-call | bytes 5505024 | tf_op jit(solution)/shard_map/pallas_call | solution.py:91
  153.3 3.6 %shard_map.105 = (bf16[896,4096]{1,0:T(8,128)(2,1)}, bf16[896,4096]{1,0:T(8,128)(2,1)}) custom-call(bf16[512,896]{1,0:T(8,128)(2,1)S(1)} %collective-permute-done.4.refs_0_, bf16[512,896]{1,0:T(8,128)(2,1)S(1)} %copy-done.2, bf16[512,896]{1,0:T(8,128)(2,1)S(1)} %copy-done.4, ...), custom_call_target="tpu_custom_call", output_to_operand_aliasing={{0}: (3, {}), {1}: (4, {})} | custom-call | bytes 5505024 | tf_op jit(solution)/shard_map/pallas_call | solution.py:91
  156.9 3.9 %shard_map.106 = (bf16[896,4096]{1,0:T(8,128)(2,1)}, bf16[896,4096]{1,0:T(8,128)(2,1)}) custom-call(bf16[512,896]{1,0:T(8,128)(2,1)} %collective-permute-done.2.refs_0_, bf16[512,896]{1,0:T(8,128)(2,1)} %collective-permute-done.17.refs_1_, bf16[512,896]{1,0:T(8,128)(2,1)} %collective-permute-done.9.refs_2_, ...), custom_call_target="tpu_custom_call", output_to_operand_aliasing={{0}: (3, {}), {1}: (4, {})} | custom-call | bytes 5505024 | tf_op jit(solution)/shard_map/pallas_call | solution.py:91
  160.8 3.8 %shard_map.107 = (bf16[896,4096]{1,0:T(8,128)(2,1)}, bf16[896,4096]{1,0:T(8,128)(2,1)}) custom-call(bf16[512,512]{1,0:T(8,128)(2,1)S(1)} %collective-permute-done.12.refs_0_, bf16[512,128]{1,0:T(8,128)(2,1)S(1)} %collective-permute-done.5.refs_1_, bf16[512,256]{1,0:T(8,128)(2,1)S(1)} %copy-done.8, ...), custom_call_target="tpu_custom_call", output_to_operand_aliasing={{0}: (5, {}), {1}: (6, {})} | custom-call | bytes 5505024 | tf_op jit(solution)/shard_map/pallas_call | solution.py:91
  165.8 2.2 %shard_map.109 = (bf16[896,4096]{1,0:T(8,128)(2,1)}, bf16[896,4096]{1,0:T(8,128)(2,1)}) custom-call(bf16[512,256]{1,0:T(8,128)(2,1)} %collective-permute-done.11.refs_0_, bf16[512,512]{1,0:T(8,128)(2,1)S(1)} %copy-done.6, bf16[512,128]{1,0:T(8,128)(2,1)} %collective-permute-done.14.refs_2_, ...), custom_call_target="tpu_custom_call", output_to_operand_aliasing={{0}: (3, {}), {1}: (4, {})} | custom-call | bytes 1835008 | tf_op jit(solution)/shard_map/pallas_call | solution.py:91
  (121 shorter events, 59.5 us)
Async XLA Ops:
  0.7 56.5 %collective-permute-start.15 = (bf16[512,896]{1,0:T(8,128)(2,1)}, bf16[512,896]{1,0:T(8,128)(2,1)S(1)}, u32[]{:S(2)}, u32[]{:S(2)}) collective-permute-start(bf16[512,896]{1,0:T(8,128)(2,1)} %param.8), channel_id=1, source_target_pairs={{0,16},{16,0},{1,17},{17,1},{2,18},{18,2},{3,19},{19,3},{4,20},{20... | collective-permute-start | bytes 2752520 | tf_op jit(solution)/shard_map/ppermute | solution.py:147
  2.3 62.1 %collective-permute-start = (bf16[512,896]{1,0:T(8,128)(2,1)}, bf16[512,896]{1,0:T(8,128)(2,1)}, u32[]{:S(2)}, u32[]{:S(2)}) collective-permute-start(bf16[512,896]{1,0:T(8,128)(2,1)} %param.8), channel_id=1, source_target_pairs={{0,32},{32,64},{64,96},{96,0},{1,33},{33,65},{65,97},{97,1},{2,34}... | collective-permute-start | bytes 2752520 | tf_op jit(solution)/shard_map/ppermute | solution.py:141
  5.6 53.5 %collective-permute-start.4 = (bf16[512,896]{1,0:T(8,128)(2,1)S(1)}, bf16[512,896]{1,0:T(8,128)(2,1)S(1)}, u32[]{:S(2)}, u32[]{:S(2)}) collective-permute-start(bf16[512,896]{1,0:T(8,128)(2,1)S(1)} %add_convert_fusion.3.refs_1_), channel_id=1, source_target_pairs={{0,32},{32,64},{64,96},{96,0},{1,33},{33,65},{65,97},{97,1},{2,34}... | collective-permute-start | bytes 2752520 | tf_op jit(solution)/shard_map/ppermute | solution.py:141
  25.6 21.0 %collective-permute-start.32 = (bf16[16,32]{1,0:T(8,128)(2,1)S(1)}, bf16[16,32]{1,0:T(8,128)(2,1)S(1)}, u32[]{:S(2)}, u32[]{:S(2)}) collective-permute-start(bf16[16,32]{1,0:T(8,128)(2,1)S(1)} %maximum_select_fusion), channel_id=1, source_target_pairs={{0,64},{32,96},{64,0},{96,32},{1,65},{33,97},{65,1},{97,33},{2,66}... | collective-permute-start | bytes 3080 | tf_op jit(solution)/shard_map/ppermute | solution.py:127
  27.5 19.1 %collective-permute-start.33 = (bf16[16,32]{1,0:T(8,128)(2,1)S(1)}, bf16[16,32]{1,0:T(8,128)(2,1)S(1)}, u32[]{:S(2)}, u32[]{:S(2)}) collective-permute-start(bf16[16,32]{1,0:T(8,128)(2,1)S(1)} %maximum_select_fusion), channel_id=1, source_target_pairs={{0,32},{32,64},{64,96},{96,0},{1,33},{33,65},{65,97},{97,1},{2,34}... | collective-permute-start | bytes 3080 | tf_op jit(solution)/shard_map/ppermute | solution.py:127
  51.5 23.4 %collective-permute-start.7 = (bf16[512,896]{1,0:T(8,128)(2,1)}, bf16[512,896]{1,0:T(8,128)(2,1)S(1)}, u32[]{:S(2)}, u32[]{:S(2)}) collective-permute-start(bf16[512,896]{1,0:T(8,128)(2,1)} %param.11), channel_id=1, source_target_pairs={{0,96},{32,0},{64,32},{96,64},{1,97},{33,1},{65,33},{97,65},{2,98}... | collective-permute-start | bytes 2752520 | tf_op jit(solution)/shard_map/ppermute | solution.py:144
  55.0 23.2 %collective-permute-start.25 = (bf16[512,896]{1,0:T(8,128)(2,1)S(1)}, bf16[512,896]{1,0:T(8,128)(2,1)S(1)}, u32[]{:S(2)}, u32[]{:S(2)}) collective-permute-start(bf16[512,896]{1,0:T(8,128)(2,1)S(1)} %add_convert_fusion.3.refs_1_), channel_id=1, source_target_pairs={{0,16},{16,0},{1,17},{17,1},{2,18},{18,2},{3,19},{19,3},{4,20},{20... | collective-permute-start | bytes 2752520 | tf_op jit(solution)/shard_map/ppermute | solution.py:147
  57.2 37.4 %collective-permute-start.26 = (bf16[512,896]{1,0:T(8,128)(2,1)S(1)}, bf16[512,896]{1,0:T(8,128)(2,1)S(1)}, u32[]{:S(2)}, u32[]{:S(2)}) collective-permute-start(bf16[512,896]{1,0:T(8,128)(2,1)S(1)} %add_convert_fusion.refs_0_), channel_id=1, source_target_pairs={{0,96},{32,0},{64,32},{96,64},{1,97},{33,1},{65,33},{97,65},{2,98}... | collective-permute-start | bytes 2752520 | tf_op jit(solution)/shard_map/ppermute | solution.py:144
  64.4 49.9 %collective-permute-start.17 = (bf16[512,896]{1,0:T(8,128)(2,1)S(1)}, bf16[512,896]{1,0:T(8,128)(2,1)}, u32[]{:S(2)}, u32[]{:S(2)}) collective-permute-start(bf16[512,896]{1,0:T(8,128)(2,1)S(1)} %add_convert_fusion.1.refs_1_), channel_id=1, source_target_pairs={{0,96},{32,0},{64,32},{96,64},{1,97},{33,1},{65,33},{97,65},{2,98}... | collective-permute-start | bytes 2752520 | tf_op jit(solution)/shard_map/ppermute | solution.py:144
  64.4 32.7 %collective-permute-start.12 = (bf16[512,512]{1,0:T(8,128)(2,1)S(1)}, bf16[512,512]{1,0:T(8,128)(2,1)S(1)}, u32[]{:S(2)}, u32[]{:S(2)}) collective-permute-start(bf16[512,512]{1,0:T(8,128)(2,1)S(1)} %slice.53), channel_id=1, source_target_pairs={{0,16},{16,0},{1,17},{17,1},{2,18},{18,2},{3,19},{19,3},{4,20},{20... | collective-permute-start | bytes 1572872 | tf_op jit(solution)/shard_map/ppermute | solution.py:147
  74.9 41.6 %collective-permute-start.2 = (bf16[512,896]{1,0:T(8,128)(2,1)}, bf16[512,896]{1,0:T(8,128)(2,1)}, u32[]{:S(2)}, u32[]{:S(2)}) collective-permute-start(bf16[512,896]{1,0:T(8,128)(2,1)} %add_convert_fusion.4.refs_0_), channel_id=1, source_target_pairs={{0,32},{32,64},{64,96},{96,0},{1,33},{33,65},{65,97},{97,1},{2,34}... | collective-permute-start | bytes 2752520 | tf_op jit(solution)/shard_map/ppermute | solution.py:141
  78.2 18.8 %collective-permute-start.5 = (bf16[512,128]{1,0:T(8,128)(2,1)S(1)}, bf16[512,128]{1,0:T(8,128)(2,1)S(1)}, u32[]{:S(2)}, u32[]{:S(2)}) collective-permute-start(bf16[512,128]{1,0:T(8,128)(2,1)S(1)} %slice.49), channel_id=1, source_target_pairs={{0,16},{16,0},{1,17},{17,1},{2,18},{18,2},{3,19},{19,3},{4,20},{20... | collective-permute-start | bytes 393224 | tf_op jit(solution)/shard_map/ppermute | solution.py:147
  95.5 28.1 %collective-permute-start.9 = (bf16[512,896]{1,0:T(8,128)(2,1)}, bf16[512,896]{1,0:T(8,128)(2,1)}, u32[]{:S(2)}, u32[]{:S(2)}) collective-permute-start(bf16[512,896]{1,0:T(8,128)(2,1)} %add_convert_fusion.2.refs_2_), channel_id=1, source_target_pairs={{0,16},{16,0},{1,17},{17,1},{2,18},{18,2},{3,19},{19,3},{4,20},{20... | collective-permute-start | bytes 2752520 | tf_op jit(solution)/shard_map/ppermute | solution.py:147
  97.0 28.9 %collective-permute-start.23 = (bf16[512,896]{1,0:T(8,128)(2,1)S(1)}, bf16[512,896]{1,0:T(8,128)(2,1)}, u32[]{:S(2)}, u32[]{:S(2)}) collective-permute-start(bf16[512,896]{1,0:T(8,128)(2,1)S(1)} %add_convert_fusion.1.refs_1_), channel_id=1, source_target_pairs={{0,32},{32,64},{64,96},{96,0},{1,33},{33,65},{65,97},{97,1},{2,34}... | collective-permute-start | bytes 2752520 | tf_op jit(solution)/shard_map/ppermute | solution.py:141
  97.1 36.7 %collective-permute-start.24 = (bf16[512,896]{1,0:T(8,128)(2,1)}, bf16[512,896]{1,0:T(8,128)(2,1)}, u32[]{:S(2)}, u32[]{:S(2)}) collective-permute-start(bf16[512,896]{1,0:T(8,128)(2,1)} %add_convert_fusion.2.refs_2_), channel_id=1, source_target_pairs={{0,96},{32,0},{64,32},{96,64},{1,97},{33,1},{65,33},{97,65},{2,98}... | collective-permute-start | bytes 2752520 | tf_op jit(solution)/shard_map/ppermute | solution.py:144
  116.5 25.2 %collective-permute-start.13 = (bf16[512,512]{1,0:T(8,128)(2,1)S(1)}, bf16[512,512]{1,0:T(8,128)(2,1)S(1)}, u32[]{:S(2)}, u32[]{:S(2)}) collective-permute-start(bf16[512,512]{1,0:T(8,128)(2,1)S(1)} %collective-permute-done.12.refs_0_), channel_id=1, source_target_pairs={{0,32},{32,64},{64,96},{96,0},{1,33},{33,65},{65,97},{97,1},{2,34}... | collective-permute-start | bytes 1572872 | tf_op jit(solution)/shard_map/ppermute | solution.py:141
  122.1 23.6 %collective-permute-start.21 = (bf16[512,256]{1,0:T(8,128)(2,1)S(1)}, bf16[512,256]{1,0:T(8,128)(2,1)S(1)}, u32[]{:S(2)}, u32[]{:S(2)}) collective-permute-start(bf16[512,256]{1,0:T(8,128)(2,1)S(1)} %get-tuple-element.35), channel_id=1, source_target_pairs={{0,16},{16,0},{1,17},{17,1},{2,18},{18,2},{3,19},{19,3},{4,20},{20... | collective-permute-start | bytes 786440 | tf_op jit(solution)/shard_map/ppermute | solution.py:147
  123.6 23.7 %collective-permute-start.18 = (bf16[512,256]{1,0:T(8,128)(2,1)S(1)}, bf16[512,256]{1,0:T(8,128)(2,1)S(1)}, u32[]{:S(2)}, u32[]{:S(2)}) collective-permute-start(bf16[512,256]{1,0:T(8,128)(2,1)S(1)} %slice.55), channel_id=1, source_target_pairs={{0,96},{32,0},{64,32},{96,64},{1,97},{33,1},{65,33},{97,65},{2,98}... | collective-permute-start | bytes 786440 | tf_op jit(solution)/shard_map/ppermute | solution.py:144
  125.9 11.0 %collective-permute-start.19 = (bf16[128,128]{1,0:T(8,128)(2,1)S(1)}, bf16[128,128]{1,0:T(8,128)(2,1)S(1)}, u32[]{:S(2)}, u32[]{:S(2)}) collective-permute-start(bf16[128,128]{1,0:T(8,128)(2,1)S(1)} %slice.56), channel_id=1, source_target_pairs={{0,96},{32,0},{64,32},{96,64},{1,97},{33,1},{65,33},{97,65},{2,98}... | collective-permute-start | bytes 98312 | tf_op jit(solution)/shard_map/ppermute | solution.py:144
  136.9 28.8 %collective-permute-start.11 = (bf16[512,256]{1,0:T(8,128)(2,1)}, bf16[512,256]{1,0:T(8,128)(2,1)}, u32[]{:S(2)}, u32[]{:S(2)}) collective-permute-start(bf16[512,256]{1,0:T(8,128)(2,1)} %get-tuple-element.36), channel_id=1, source_target_pairs={{0,16},{16,0},{1,17},{17,1},{2,18},{18,2},{3,19},{19,3},{4,20},{20... | collective-permute-start | bytes 786440 | tf_op jit(solution)/shard_map/ppermute | solution.py:147
  141.6 26.4 %collective-permute-start.6 = (bf16[384,128]{1,0:T(8,128)(2,1)}, bf16[384,128]{1,0:T(8,128)(2,1)}, u32[]{:S(2)}, u32[]{:S(2)}) collective-permute-start(bf16[384,128]{1,0:T(8,128)(2,1)} %slice.50), channel_id=1, source_target_pairs={{0,32},{32,64},{64,96},{96,0},{1,33},{33,65},{65,97},{97,1},{2,34}... | collective-permute-start | bytes 294920 | tf_op jit(solution)/shard_map/ppermute | solution.py:141
  142.6 23.1 %collective-permute-start.14 = (bf16[512,128]{1,0:T(8,128)(2,1)}, bf16[512,128]{1,0:T(8,128)(2,1)}, u32[]{:S(2)}, u32[]{:S(2)}) collective-permute-start(bf16[512,128]{1,0:T(8,128)(2,1)} %get-tuple-element.37), channel_id=1, source_target_pairs={{0,96},{32,0},{64,32},{96,64},{1,97},{33,1},{65,33},{97,65},{2,98}... | collective-permute-start | bytes 393224 | tf_op jit(solution)/shard_map/ppermute | solution.py:144
  146.4 21.6 %collective-permute-start.10 = (bf16[512,128]{1,0:T(8,128)(2,1)}, bf16[512,128]{1,0:T(8,128)(2,1)}, u32[]{:S(2)}, u32[]{:S(2)}) collective-permute-start(bf16[512,128]{1,0:T(8,128)(2,1)} %get-tuple-element.38), channel_id=1, source_target_pairs={{0,96},{32,0},{64,32},{96,64},{1,97},{33,1},{65,33},{97,65},{2,98}... | collective-permute-start | bytes 393224 | tf_op jit(solution)/shard_map/ppermute | solution.py:144
  148.0 20.0 %collective-permute-start.3 = (bf16[384,128]{1,0:T(8,128)(2,1)}, bf16[384,128]{1,0:T(8,128)(2,1)}, u32[]{:S(2)}, u32[]{:S(2)}) collective-permute-start(bf16[384,128]{1,0:T(8,128)(2,1)} %slice.48), channel_id=1, source_target_pairs={{0,16},{16,0},{1,17},{17,1},{2,18},{18,2},{3,19},{19,3},{4,20},{20... | collective-permute-start | bytes 294920 | tf_op jit(solution)/shard_map/ppermute | solution.py:147
  (30 other events, 324.1 us)
